TPU v7x, 32 devices: a whole 2x2x4 slice. The times are simulated.
32 devices in a mesh: tri: 16 (over z, y, x), sub: 2 (over core).
Axes of the slice: x: 2, y: 2, z: 4, core: 2. Of those that a mesh axis runs over, the one named last changes fastest.
Arguments:
- stored_tiles: float32 [16, 36, 512, 512], P('tri', None, 'sub'), may hold values from -190 to 190, as said below
- cell_owner: int32 [16], replicated, may hold values from 0 to 15, as said below
Outputs:
- updated: float32 [16, 36, 512, 512], P('tri', None, 'sub')
Inputs may be any that keep to these rules, and one draw needn't show every extreme that they name: `cell_owner`: a permutation of the indices of tri. `stored_tiles`: every tile whose row and column blocks are equal is skew-symmetric, every pivot met is invertible, and slots that hold no tile are zero.
All inputs are finite; a program needn't handle non-finite values.
Results may differ from a plain program's by a relative error of at most 0.00035.
Values may be sent and summed in bfloat16 or wider, within the bound.
No kernel may reach another device: no remote copies, remote signals or barrier semaphores. Data moves between devices by JAX's collectives and lax.ppermute only.
A program may use at most 128 MiB of HBM per device.

v0:
```python
import math

import jax
import jax.numpy as jnp
import numpy as np
from jax import lax
from jax.experimental import pallas as pl
from jax.experimental.pallas import tpu as pltpu
from jax.sharding import PartitionSpec as P

NB = 32


def shortened(x):

    def short(part):
        return part.astype(jnp.bfloat16) if part.dtype == jnp.float32 else part

    return jax.tree.map(short, x)


def layout(groups, per_group):
    half_group = per_group // 2
    slot_count = per_group * (per_group + 1) // 2
    row_table = np.full((groups * groups, slot_count), -1, np.int32)
    col_table = np.full((groups * groups, slot_count), -1, np.int32)
    for first_group in range(groups):
        for second_group in range(groups):
            cell_index = first_group * groups + second_group
            for inner_row in range(per_group):
                if first_group == second_group:
                    for inner_column in range(inner_row + 1):
                        slot_index = inner_row * (inner_row + 1) // 2 + inner_column
                        row_table[cell_index, slot_index] = first_group * per_group + inner_row
                        col_table[cell_index, slot_index] = first_group * per_group + inner_column
                else:
                    for inner_column in range(half_group):
                        slot_index = inner_row * half_group + inner_column
                        if first_group > second_group:
                            row_table[cell_index, slot_index] = first_group * per_group + inner_row
                            col_table[cell_index, slot_index] = (
                                second_group * per_group + inner_column
                            )
                        else:
                            row_table[cell_index, slot_index] = second_group * per_group + inner_row
                            col_table[cell_index, slot_index] = (
                                first_group * per_group + half_group + inner_column
                            )
    return (row_table, col_table)


def untiled(stored_tiles, cell_owner):
    tri_count = lax.axis_size("tri")
    groups = math.isqrt(tri_count)
    per_group = NB // groups
    half_group = per_group // 2
    strip_rows = stored_tiles.shape[2]
    block_order = stored_tiles.shape[3]
    row_table, col_table = layout(groups, per_group)
    position = lax.axis_index("tri")
    my_cell = jnp.sum(jnp.where(cell_owner == position, jnp.arange(tri_count, dtype=jnp.int32), 0))
    cell_down = my_cell // groups
    cell_across = my_cell % groups
    row_group = jnp.maximum(cell_down, cell_across)
    col_group = jnp.minimum(cell_down, cell_across)
    my_rows = jnp.asarray(row_table)[my_cell]
    my_cols = jnp.asarray(col_table)[my_cell]
    row_local = jnp.clip(my_rows - row_group * per_group, 0, per_group - 1)
    col_local = jnp.clip(my_cols - col_group * per_group, 0, per_group - 1)
    holders = cell_owner[jnp.arange(groups) * groups]
    highest = lax.Precision.HIGHEST
    current = stored_tiles[0]
    lower_slots = np.array([member * half_group for member in range(per_group)], np.int32)
    first_slots = np.array(
        [member * (member + 1) // 2 if member > 0 else 0 for member in range(per_group)], np.int32
    )
    keep_first = np.array([1.0 if member > 0 else 0.0 for member in range(per_group)], np.float32)
    from_lower = current[lower_slots]
    from_first = current[first_slots] * keep_first[:, None, None]
    holder_part = jnp.where(cell_down > 0, from_lower, from_first)
    holder_part = jnp.where(cell_across == 0, holder_part, 0.0).astype(jnp.bfloat16)
    pivot_slot = 0 // 2
    pivot_part = jnp.where(my_cell == 0, current[pivot_slot], 0.0)
    piece_size = holder_part.size // tri_count
    pivot_piece = pivot_part.size // tri_count
    spread_panel = lax.all_to_all(
        holder_part.reshape(tri_count, piece_size), "tri", split_axis=0, concat_axis=0, tiled=True
    )
    spread_pivot = lax.all_to_all(
        pivot_part.reshape(tri_count, pivot_piece).astype(jnp.bfloat16),
        "tri",
        split_axis=0,
        concat_axis=0,
        tiled=True,
    ).astype(jnp.float32)
    picked_panel = spread_panel[holders][:, None, :]
    picked_pivot = spread_pivot[holders[0]][None, :]
    whole_panel = lax.all_gather(picked_panel, "tri", axis=1, tiled=True)
    whole_pivot = lax.all_gather(
        picked_pivot.astype(jnp.bfloat16), "tri", axis=0, tiled=True
    ).astype(picked_pivot.dtype)
    panels = whole_panel.reshape(groups, per_group, strip_rows, block_order)
    pivot_strip = whole_pivot.reshape(strip_rows, block_order)
    own_strips = panels[row_group]
    other_strips = panels[col_group]
    pivot_block = lax.all_gather(
        pivot_strip.astype(jnp.bfloat16), "sub", axis=0, tiled=True
    ).astype(pivot_strip.dtype)
    partner = lax.all_gather(other_strips, "sub", axis=1, tiled=True)
    gram_matrix = jnp.dot(pivot_block.T, pivot_block, precision=highest)
    factor = jnp.linalg.cholesky(gram_matrix)
    column_count = block_order // lax.axis_size("sub")
    first_column = lax.axis_index("sub") * column_count
    columns = lax.dynamic_slice_in_dim(pivot_block.T, first_column, column_count, 1)
    column_part = jax.scipy.linalg.cho_solve((factor, True), columns)
    inverse = lax.all_gather(shortened(column_part), "sub", axis=1, tiled=True).astype(
        column_part.dtype
    )
    scaled = jnp.einsum(
        "irk,kc->irc", own_strips.astype(jnp.float32), inverse, precision=highest
    ).astype(jnp.bfloat16)
    left_slots = scaled[row_local]
    right_slots = partner[col_local]
    update = jnp.einsum("qrk,qck->qrc", left_slots, right_slots, preferred_element_type=jnp.float32)
    live_slots = (my_rows > 0) & (my_cols > 0)
    current = current + jnp.where(live_slots[:, None, None], update, 0.0)
    return current[None]


class Plan:
    def __init__(self, tri, subs, slots, strip, order, chunks):
        self.tri, self.subs, self.slots, self.strip, self.order = tri, subs, slots, strip, order
        self.chunks = chunks
        self.groups = math.isqrt(tri)
        self.per_group = NB // self.groups
        self.half_group = self.per_group // 2
        self.half_tri = tri // 2
        self.piece = strip // self.half_tri
        self.wide = self.half_group // chunks
        self.in_chunk = 2 * self.wide
        self.o_sub = 0
        self.o_diag = 1
        self.o_slot = 2
        self.o_src = self.o_slot + self.per_group
        self.o_here = self.o_src + self.groups
        self.o_rg = self.o_here + self.groups
        self.o_cg = self.o_rg + self.half_tri
        self.o_hf = self.o_cg + self.half_tri
        self.o_i = self.o_hf + self.half_tri
        self.o_j = self.o_i + slots
        self.o_live = self.o_j + slots
        self.o_new = self.o_live + slots
        self.size = self.o_new + slots

    def tiled(self):
        return (
            self.piece % 16 == 0
            and self.order % 128 == 0
            and self.half_group % self.chunks == 0
            and self.groups * self.groups == self.tri
            and self.subs * self.strip == self.order
        )

    def tile_of(self, chunk, place):
        half, inner = divmod(place, self.wide)
        return half * self.half_group + chunk * self.wide + inner


def table_call(p, cell_owner):
    def kernel(owner, out, cell_of):
        position = lax.axis_index("tri")
        for cell in range(p.tri):
            cell_of[owner[cell]] = cell

        def split(cell):
            down = cell // p.groups
            across = cell - down * p.groups
            return down, across

        down, across = split(cell_of[position])
        row_group = jnp.maximum(down, across)
        col_group = jnp.minimum(down, across)
        diag = down == across
        my_half = position // p.half_tri
        out[p.o_sub] = lax.axis_index("sub")
        out[p.o_diag] = jnp.where(diag, 1, 0)
        for chunk in range(p.chunks):
            for place in range(p.in_chunk):
                member = p.tile_of(chunk, place)
                out[p.o_slot + chunk * p.in_chunk + place] = jnp.where(
                    down > 0, member * p.half_group, member * (member + 1) // 2
                )
        for group in range(p.groups):
            holder = owner[group * p.groups]
            half = holder // p.half_tri
            out[p.o_src + group] = holder - half * p.half_tri
            out[p.o_here + group] = jnp.where(half == my_half, 1, 0)
        for end in range(p.half_tri):
            there_down, there_across = split(cell_of[my_half * p.half_tri + end])
            out[p.o_rg + end] = jnp.maximum(there_down, there_across)
            out[p.o_cg + end] = jnp.minimum(there_down, there_across)
            out[p.o_hf + end] = jnp.where(there_down < there_across, 1, 0)
        col_shift = jnp.where(down < across, p.half_group, 0)
        triangle = [(i, j) for i in range(p.per_group) for j in range(i + 1)]
        for slot in range(p.slots):
            tri_i, tri_j = triangle[slot] if slot < len(triangle) else (0, -1)
            box_i, box_j = divmod(slot, p.half_group)
            if box_i >= p.per_group:
                box_i, box_j = 0, -1
            inner_i = jnp.where(diag, tri_i, box_i)
            inner_j = jnp.where(diag, tri_j, box_j)
            row = row_group * p.per_group + inner_i
            col = col_group * p.per_group + jnp.where(diag, 0, col_shift) + inner_j
            live = (inner_j >= 0) & (row > 0) & (col > 0)
            out[p.o_i + slot] = inner_i
            out[p.o_j + slot] = jnp.maximum(inner_j, 0)
            out[p.o_live + slot] = jnp.where(live, 1, 0)
            new_tri = 1 if tri_j == 0 else 0
            new_box = 1 if box_j == 0 else 0
            out[p.o_new + slot] = jnp.where(diag, new_tri, new_box)

    return pl.pallas_call(
        kernel,
        out_shape=jax.ShapeDtypeStruct((p.size,), jnp.int32),
        in_specs=[pl.BlockSpec(memory_space=pltpu.SMEM)],
        out_specs=pl.BlockSpec(memory_space=pltpu.SMEM),
        scratch_shapes=[pltpu.SMEM((p.tri,), jnp.int32)],
        name="table",
    )(cell_owner)


def extract_call(p, table, current, chunk):
    def kernel(t, tile, out):
        out[...] = tile[...].reshape(p.half_tri, 1, p.piece, p.order).astype(jnp.bfloat16)

    return pl.pallas_call(
        kernel,
        out_shape=jax.ShapeDtypeStruct((p.half_tri, p.in_chunk, p.piece, p.order), jnp.bfloat16),
        grid_spec=pltpu.PrefetchScalarGridSpec(
            num_scalar_prefetch=1,
            grid=(p.in_chunk,),
            in_specs=[
                pl.BlockSpec(
                    (1, p.strip, p.order),
                    lambda i, t: (t[p.o_slot + chunk * p.in_chunk + i], 0, 0),
                )
            ],
            out_specs=pl.BlockSpec(
                (p.half_tri, 1, p.piece, p.order), lambda i, t: (0, i, 0, 0)
            ),
        ),
        name=f"extract{chunk}",
    )(table, current)


def pick_call(p, table, spread):
    def kernel(t, spread_ref, out, sems):
        copies = [
            pltpu.make_async_copy(spread_ref.at[t[p.o_src + g]], out.at[g], sems.at[g])
            for g in range(p.groups)
        ]
        for copy in copies:
            copy.start()
        for copy in copies:
            copy.wait()

    any_space = pl.BlockSpec(memory_space=pl.ANY)
    return pl.pallas_call(
        kernel,
        out_shape=jax.ShapeDtypeStruct((p.groups,) + spread.shape[1:], jnp.bfloat16),
        grid_spec=pltpu.PrefetchScalarGridSpec(
            num_scalar_prefetch=1,
            grid=(),
            in_specs=[any_space],
            out_specs=any_space,
            scratch_shapes=[pltpu.SemaphoreType.DMA((p.groups,))],
        ),
        name="pick",
    )(table, spread)


def build_call(p, table, near, far, with_pivot):
    rows = p.in_chunk + p.wide + (1 if with_pivot else 0)

    def kernel(t, near_ref, far_ref, out, sems):
        def part(group, first, count, end, place, sem):
            here = t[p.o_here + group] == 1
            target = out.at[end, pl.ds(place, count)]

            @pl.when(here)
            def _():
                pltpu.make_async_copy(near_ref.at[group, pl.ds(first, count)], target, sem).start()

            @pl.when(jnp.logical_not(here))
            def _():
                pltpu.make_async_copy(far_ref.at[group, pl.ds(first, count)], target, sem).start()

        for end in range(p.half_tri):
            part(t[p.o_rg + end], 0, p.in_chunk, end, 0, sems.at[end, 0])
            part(
                t[p.o_cg + end],
                t[p.o_hf + end] * p.wide,
                p.wide,
                end,
                p.in_chunk,
                sems.at[end, 1],
            )
            if with_pivot:
                part(0, 0, 1, end, p.in_chunk + p.wide, sems.at[end, 2])

        def await_part(end, place, count, sem):
            target = out.at[end, pl.ds(place, count)]
            pltpu.make_async_copy(near_ref.at[0, pl.ds(0, count)], target, sem).wait()

        for end in range(p.half_tri):
            await_part(end, 0, p.in_chunk, sems.at[end, 0])
            await_part(end, p.in_chunk, p.wide, sems.at[end, 1])
            if with_pivot:
                await_part(end, p.in_chunk + p.wide, 1, sems.at[end, 2])

    any_space = pl.BlockSpec(memory_space=pl.ANY)
    return pl.pallas_call(
        kernel,
        out_shape=jax.ShapeDtypeStruct((p.half_tri, rows, p.piece, p.order), jnp.bfloat16),
        grid_spec=pltpu.PrefetchScalarGridSpec(
            num_scalar_prefetch=1,
            grid=(),
            in_specs=[any_space, any_space],
            out_specs=any_space,
            scratch_shapes=[pltpu.SemaphoreType.DMA((p.half_tri, 3))],
        ),
        name="build",
    )(table, near, far)


def inverse_call(p, table, arrived):
    place = p.in_chunk + p.wide
    order = p.order

    def kernel(t, *refs):
        sources = refs[: p.subs]
        high, low, pivot, x_wide, x_half, e_ref, sem = refs[p.subs :]
        for shift in range(p.subs):
            strip = lax.rem(t[p.o_sub] + shift, p.subs) * p.strip
            for s in range(p.half_tri):
                at = pl.multiple_of(strip + s * p.piece, p.piece)
                pltpu.make_async_copy(
                    sources[shift].at[s, place], pivot.at[pl.ds(at, p.piece)], sem
                ).start()
        pltpu.make_async_copy(pivot, pivot, sem).wait()

        def dot(a, b):
            return lax.dot_general(
                a, b, (((1,), (0,)), ((), ())), preferred_element_type=jnp.float32
            )

        def eye():
            r = lax.broadcasted_iota(jnp.int32, (order, order), 0)
            c = lax.broadcasted_iota(jnp.int32, (order, order), 1)
            return jnp.where(r == c, 1.0, 0.0)

        square = dot(pivot[...], pivot[...])
        bound = jnp.max(jnp.sum(jnp.abs(square), axis=1))
        start = pivot[...].astype(jnp.float32) * (-1.0 / bound)
        x_wide[...] = start
        x_half[...] = start.astype(jnp.bfloat16)

        def coarse_on(carry):
            step, error, noise = carry
            return (step < 40) & (error > 0.01) & (noise < 0.1)

        def coarse(carry):
            step, _, _ = carry
            x = x_half[...]
            residual = eye() - dot(pivot[...], x)
            e_ref[...] = residual.astype(jnp.bfloat16)
            error = jnp.sum(residual * residual)
            new = x.astype(jnp.float32) + dot(x, e_ref[...])
            x_wide[...] = new
            x_half[...] = new.astype(jnp.bfloat16)
            noise = jnp.sum(new * new) * bound * 2.0**-18
            return step + 1, error, noise

        lax.while_loop(coarse_on, coarse, (jnp.int32(0), jnp.float32(1e30), jnp.float32(0.0)))

        def fine_on(carry):
            step, error, before = carry
            stuck = (before < 0.5) & (error > 0.5 * before)
            return (step < 100) & (error > 1e-4) & jnp.logical_not(stuck)

        def fine(carry):
            step, before, _ = carry
            x = x_wide[...]
            x_high = x.astype(jnp.bfloat16)
            x_low = (x - x_high.astype(jnp.float32)).astype(jnp.bfloat16)
            residual = eye() - (dot(pivot[...], x_high) + dot(pivot[...], x_low))
            error = jnp.sum(residual * residual)
            e_high = residual.astype(jnp.bfloat16)
            e_low = (residual - e_high.astype(jnp.float32)).astype(jnp.bfloat16)
            x_wide[...] = x + (dot(x_high, e_high) + (dot(x_high, e_low) + dot(x_low, e_high)))
            return step + 1, error, before

        lax.while_loop(fine_on, fine, (jnp.int32(0), jnp.float32(1e30), jnp.float32(1e30)))
        x = x_wide[...]
        rounded = x.astype(jnp.bfloat16)
        high[...] = rounded
        low[...] = (x - rounded.astype(jnp.float32)).astype(jnp.bfloat16)

    any_space = pl.BlockSpec(memory_space=pl.ANY)
    whole = pl.BlockSpec((order, order), lambda t: (0, 0))
    square_shape = jax.ShapeDtypeStruct((order, order), jnp.bfloat16)
    return pl.pallas_call(
        kernel,
        out_shape=(square_shape, square_shape),
        grid_spec=pltpu.PrefetchScalarGridSpec(
            num_scalar_prefetch=1,
            grid=(),
            in_specs=[any_space] * p.subs,
            out_specs=(pl.BlockSpec(memory_space=pltpu.VMEM),) * 2,
            scratch_shapes=[
                pltpu.VMEM((order, order), jnp.bfloat16),
                pltpu.VMEM((order, order), jnp.float32),
                pltpu.VMEM((order, order), jnp.bfloat16),
                pltpu.VMEM((order, order), jnp.bfloat16),
                pltpu.SemaphoreType.DMA,
            ],
        ),
        name="inverse",
    )(table, *arrived)


def update_call(p, table, current, arrived, inverse):
    per_step = 2 if p.slots % 2 == 0 else 1

    def kernel(t, tiles, high, low, *refs):
        sources = [refs[k * p.subs : (k + 1) * p.subs] for k in range(p.chunks)]
        out, left, right, scaled, left_sem, right_sem = refs[p.chunks * p.subs :]
        step = pl.program_id(0)
        diag = t[p.o_diag] == 1

        @pl.when(step == 0)
        def _():
            for k in range(p.chunks):
                for shift in range(p.subs):
                    ref = sources[k][shift]
                    strip = lax.rem(t[p.o_sub] + shift, p.subs) * p.strip
                    for s in range(p.half_tri):
                        at = pl.multiple_of(strip + s * p.piece, p.piece)
                        for half in range(2):
                            tiles_at = pl.ds(half * p.half_group + k * p.wide, p.wide)
                            part = ref.at[s, pl.ds(half * p.wide, p.wide)]
                            if shift == 0:
                                pltpu.make_async_copy(
                                    part, left.at[tiles_at, pl.ds(s * p.piece, p.piece)], left_sem
                                ).start()

                            @pl.when(diag)
                            def _():
                                pltpu.make_async_copy(
                                    part, right.at[tiles_at, pl.ds(at, p.piece)], right_sem
                                ).start()

                        @pl.when(jnp.logical_not(diag))
                        def _():
                            pltpu.make_async_copy(
                                ref.at[s, pl.ds(p.in_chunk, p.wide)],
                                right.at[pl.ds(k * p.wide, p.wide), pl.ds(at, p.piece)],
                                right_sem,
                            ).start()

            pltpu.make_async_copy(left, left, left_sem).wait()

            @pl.when(diag)
            def _():
                pltpu.make_async_copy(right, right, right_sem).wait()

            @pl.when(jnp.logical_not(diag))
            def _():
                some = right.at[pl.ds(0, p.half_group)]
                pltpu.make_async_copy(some, some, right_sem).wait()

        for u in range(per_step):
            slot = step * per_step + u

            @pl.when(t[p.o_new + slot] == 1)
            def _():
                strip = left[t[p.o_i + slot]]
                dims = (((1,), (0,)), ((), ()))
                product = lax.dot_general(
                    strip, high[...], dims, preferred_element_type=jnp.float32
                ) + lax.dot_general(strip, low[...], dims, preferred_element_type=jnp.float32)
                scaled[...] = product.astype(jnp.bfloat16)

            live = t[p.o_live + slot] == 1

            @pl.when(live)
            def _():
                out[u] = tiles[u] + lax.dot_general(
                    scaled[...],
                    right[t[p.o_j + slot]],
                    (((1,), (1,)), ((), ())),
                    preferred_element_type=jnp.float32,
                )

            @pl.when(jnp.logical_not(live))
            def _():
                out[u] = tiles[u]

    any_space = pl.BlockSpec(memory_space=pl.ANY)
    block = pl.BlockSpec((per_step, p.strip, p.order), lambda i, t: (i, 0, 0))
    square = pl.BlockSpec((p.order, p.order), lambda i, t: (0, 0))
    return pl.pallas_call(
        kernel,
        out_shape=jax.ShapeDtypeStruct(current.shape, jnp.float32),
        grid_spec=pltpu.PrefetchScalarGridSpec(
            num_scalar_prefetch=1,
            grid=(p.slots // per_step,),
            in_specs=[block, square, square] + [any_space] * (p.chunks * p.subs),
            out_specs=block,
            scratch_shapes=[
                pltpu.VMEM((p.per_group, p.strip, p.order), jnp.bfloat16),
                pltpu.VMEM((p.per_group, p.order, p.order), jnp.bfloat16),
                pltpu.VMEM((p.strip, p.order), jnp.bfloat16),
                pltpu.SemaphoreType.DMA,
                pltpu.SemaphoreType.DMA,
            ],
        ),
        compiler_params=pltpu.CompilerParams(dimension_semantics=("arbitrary",)),
        name="update",
    )(table, current, *inverse, *[ref for chunk in arrived for ref in chunk])


def planned(p, stored_tiles, cell_owner):
    table = table_call(p, cell_owner)
    current = stored_tiles[0]
    halves = [list(range(h * p.half_tri, (h + 1) * p.half_tri)) for h in range(2)]
    swap = [(i, (i + p.half_tri) % p.tri) for i in range(p.tri)]

    def exchange(x):
        return lax.all_to_all(
            x, "tri", split_axis=0, concat_axis=0, tiled=True, axis_index_groups=halves
        )

    def arrivals(x):
        return [x] + [
            lax.ppermute(x, "sub", [((i + shift) % p.subs, i) for i in range(p.subs)])
            for shift in range(1, p.subs)
        ]

    near = []
    for chunk in range(p.chunks):
        spread = exchange(extract_call(p, table, current, chunk))
        near.append(pick_call(p, table, spread))
    far = [lax.ppermute(x, "tri", swap) for x in near]
    arrived = []
    for chunk in range(p.chunks):
        built = build_call(p, table, near[chunk], far[chunk], chunk == 0)
        arrived.append(arrivals(exchange(built)))
    inverse = inverse_call(p, table, arrived[0])
    return update_call(p, table, current, arrived, inverse)[None]


def shards(stored_tiles, cell_owner):
    p = Plan(
        lax.axis_size("tri"),
        lax.axis_size("sub"),
        stored_tiles.shape[1],
        stored_tiles.shape[2],
        stored_tiles.shape[3],
        2,
    )
    if p.tiled():
        return planned(p, stored_tiles, cell_owner)
    return untiled(stored_tiles, cell_owner)


def solution(mesh):
    placed = (P("tri", None, "sub", None), P())
    return jax.shard_map(
        shards, mesh=mesh, in_specs=placed, out_specs=P("tri", None, "sub", None), check_vma=False
    )
```

profile of v0, /device:TPU:1, one launch (start us, length us, event | category | flops | bytes accessed | tf_op | source)
XLA Modules:
  0.0 295.9 jit_solution(13590929757843447820)
XLA Ops:
  0.0 1.5 table.1.t
  1.5 4.3 %extract0.1 = bf16[8,4,32,512]{3,2,1,0:T(8,128)(2,1)} custom-call(s32[186]{0:T(256)} %table.1.t, f32[36,256,512]{2,1,0:T(8,128)} %bitcast.2), custom_call_target="tpu_custom_call" | custom-call | tf_op jit(solution)/shard_map/extract0/pallas_call | solution.py:236
  5.8 5.3 %all-to-all-start = ((bf16[8,4,32,512]{3,2,1,0:T(8,128)(2,1)}), bf16[8,4,32,512]{3,2,1,0:T(8,128)(2,1)S(1)}, u32[]{:S(2)}, u32[]{:S(2)}) async-start(bf16[8,4,32,512]{3,2,1,0:T(8,128)(2,1)} %extract0.1), calls=%async_computation | async-start | bytes 2097152 | tf_op jit(solution)/shard_map/all_to_all | solution.py:540
  11.0 4.3 %extract1.1 = bf16[8,4,32,512]{3,2,1,0:T(8,128)(2,1)} custom-call(s32[186]{0:T(256)} %table.1.t, f32[36,256,512]{2,1,0:T(8,128)} %bitcast.3), custom_call_target="tpu_custom_call" | custom-call | tf_op jit(solution)/shard_map/extract1/pallas_call | solution.py:236
  15.4 9.5 %all-to-all-done.spread_ref = bf16[8,4,32,512]{3,2,1,0:T(8,128)(2,1)S(1)} async-done(((bf16[8,4,32,512]{3,2,1,0:T(8,128)(2,1)}), bf16[8,4,32,512]{3,2,1,0:T(8,128)(2,1)S(1)}, u32[]{:S(2)}, u32[]{:S(2)}) %all-to-all-start) | async-done | bytes 1048608 | tf_op jit(solution)/shard_map/all_to_all | solution.py:540
  24.9 0.0 copy-start.3
  24.9 4.2 %all-to-all-start.2 = ((bf16[8,4,32,512]{3,2,1,0:T(8,128)(2,1)}), bf16[8,4,32,512]{3,2,1,0:T(8,128)(2,1)S(1)}, u32[]{:S(2)}, u32[]{:S(2)}) async-start(bf16[8,4,32,512]{3,2,1,0:T(8,128)(2,1)} %extract1.1), calls=%async_computation.2 | async-start | bytes 2097152 | tf_op jit(solution)/shard_map/all_to_all | solution.py:540
  29.1 0.0 copy-done.3
  29.1 17.7 %pick.2.near_ref = bf16[4,4,32,512]{3,2,1,0:T(8,128)(2,1)} custom-call(s32[186]{0:T(256)} %table.1.t, bf16[8,4,32,512]{3,2,1,0:T(8,128)(2,1)} %copy-done.3), custom_call_target="tpu_custom_call" | custom-call | tf_op jit(solution)/shard_map/pick/pallas_call | solution.py:268
  46.9 2.4 collective-permute-start
  49.2 22.6 %collective-permute-done.far_ref = bf16[4,4,32,512]{3,2,1,0:T(8,128)(2,1)S(1)} collective-permute-done((bf16[4,4,32,512]{3,2,1,0:T(8,128)(2,1)}, bf16[4,4,32,512]{3,2,1,0:T(8,128)(2,1)S(1)}, u32[]{:S(2)}, u32[]{:S(2)}) %collective-permute-start) | collective-permute-done | bytes 524320 | tf_op jit(solution)/shard_map/ppermute | solution.py:554
  71.9 0.0 copy-start.5
  71.9 0.8 copy-done.5
  72.7 57.6 %build.2 = bf16[8,7,32,512]{3,2,1,0:T(8,128)(2,1)} custom-call(s32[186]{0:T(256)} %table.1.t, bf16[4,4,32,512]{3,2,1,0:T(8,128)(2,1)} %pick.2.near_ref, bf16[4,4,32,512]{3,2,1,0:T(8,128)(2,1)} %copy-done.5), custom_call_target="tpu_custom_call" | custom-call | tf_op jit(solution)/shard_map/build/pallas_call | solution.py:322
  130.3 0.0 all-to-all-done.2.spread_ref
  130.3 0.0 copy-start.2
  130.3 1.0 copy-done.2
  131.3 5.1 %all-to-all-start.1 = ((bf16[8,7,32,512]{3,2,1,0:T(8,128)(2,1)}), bf16[8,7,32,512]{3,2,1,0:T(8,128)(2,1)S(1)}, u32[]{:S(2)}, u32[]{:S(2)}) async-start(bf16[8,7,32,512]{3,2,1,0:T(8,128)(2,1)} %build.2), calls=%async_computation.1 | async-start | bytes 3670016 | tf_op jit(solution)/shard_map/all_to_all | solution.py:540
  136.4 17.7 %pick.3.near_ref = bf16[4,4,32,512]{3,2,1,0:T(8,128)(2,1)} custom-call(s32[186]{0:T(256)} %table.1.t, bf16[8,4,32,512]{3,2,1,0:T(8,128)(2,1)} %copy-done.2), custom_call_target="tpu_custom_call" | custom-call | tf_op jit(solution)/shard_map/pick/pallas_call | solution.py:268
  154.1 3.1 %collective-permute-start.2 = (bf16[4,4,32,512]{3,2,1,0:T(8,128)(2,1)}, bf16[4,4,32,512]{3,2,1,0:T(8,128)(2,1)S(1)}, u32[]{:S(2)}, u32[]{:S(2)}) collective-permute-start(bf16[4,4,32,512]{3,2,1,0:T(8,128)(2,1)} %pick.3.near_ref), channel_id=1, source_target_pairs={{0,16},{2,18},{4,20},{6,22},{8,24},{10,26},{12,28},{14,30},{16,0},... | collective-permute-start | bytes 1572872 | tf_op jit(solution)/shard_map/ppermute | solution.py:554
  157.1 23.0 %collective-permute-done.2.far_ref = bf16[4,4,32,512]{3,2,1,0:T(8,128)(2,1)S(1)} collective-permute-done((bf16[4,4,32,512]{3,2,1,0:T(8,128)(2,1)}, bf16[4,4,32,512]{3,2,1,0:T(8,128)(2,1)S(1)}, u32[]{:S(2)}, u32[]{:S(2)}) %collective-permute-start.2) | collective-permute-done | bytes 524320 | tf_op jit(solution)/shard_map/ppermute | solution.py:554
  180.2 0.0 copy-start.4
  180.2 0.8 copy-done.4
  181.0 49.7 %build.3 = bf16[8,6,32,512]{3,2,1,0:T(8,128)(2,1)} custom-call(s32[186]{0:T(256)} %table.1.t, bf16[4,4,32,512]{3,2,1,0:T(8,128)(2,1)} %pick.3.near_ref, bf16[4,4,32,512]{3,2,1,0:T(8,128)(2,1)} %copy-done.4), custom_call_target="tpu_custom_call" | custom-call | tf_op jit(solution)/shard_map/build/pallas_call | solution.py:322
  230.6 0.0 all-to-all-done.1.refs_0_
  230.6 0.0 copy-start
  230.7 4.1 %all-to-all-start.3 = ((bf16[8,6,32,512]{3,2,1,0:T(8,128)(2,1)}), bf16[8,6,32,512]{3,2,1,0:T(8,128)(2,1)S(1)}, u32[]{:S(2)}, u32[]{:S(2)}) async-start(bf16[8,6,32,512]{3,2,1,0:T(8,128)(2,1)} %build.3), calls=%async_computation.3 | async-start | bytes 3145728 | tf_op jit(solution)/shard_map/all_to_all | solution.py:540
  234.7 1.4 collective-permute-start.1
  236.2 18.6 %all-to-all-done.3.refs_2_ = bf16[8,6,32,512]{3,2,1,0:T(8,128)(2,1)S(1)} async-done(((bf16[8,6,32,512]{3,2,1,0:T(8,128)(2,1)}), bf16[8,6,32,512]{3,2,1,0:T(8,128)(2,1)S(1)}, u32[]{:S(2)}, u32[]{:S(2)}) %all-to-all-start.3) | async-done | bytes 1572896 | tf_op jit(solution)/shard_map/all_to_all | solution.py:540
  254.8 0.0 copy-start.1
  254.8 1.5 collective-permute-start.3
  256.2 0.0 collective-permute-done.1.refs_1_
  256.2 0.0 copy-done
  256.2 13.8 %inverse.1 = (bf16[512,512]{1,0:T(8,128)(2,1)}, bf16[512,512]{1,0:T(8,128)(2,1)}) custom-call(s32[186]{0:T(256)} %table.1.t, bf16[8,7,32,512]{3,2,1,0:T(8,128)(2,1)} %copy-done, bf16[8,7,32,512]{3,2,1,0:T(8,128)(2,1)} %collective-permute-done.1.refs_1_), custom_call_target="tpu_custom_call" | custom-call | tf_op jit(solution)/shard_map/inverse/pallas_call | solution.py:412
  270.0 0.0 copy-done.1
  270.0 0.0 collective-permute-done.3.refs_3_
  270.0 25.9 %update.1 = f32[36,256,512]{2,1,0:T(8,128)} custom-call(s32[186]{0:T(256)} %table.1.t, f32[36,256,512]{2,1,0:T(8,128)} %bitcast.4, bf16[512,512]{1,0:T(8,128)(2,1)} %get-tuple-element.7.high, bf16[512,512]{1,0:T(8,128)(2,1)} %get-tuple-element.8.low, bf16[8,7,32,512]{3,2,1,0:T(8,128)(2,1)} %copy-done, ...), custom_call_target="tpu_custom_call" | custom-call | tf_op jit(solution)/shard_map/update/pallas_call | solution.py:512
Async XLA Ops:
  5.8 19.1 %all-to-all-start = ((bf16[8,4,32,512]{3,2,1,0:T(8,128)(2,1)}), bf16[8,4,32,512]{3,2,1,0:T(8,128)(2,1)S(1)}, u32[]{:S(2)}, u32[]{:S(2)}) async-start(bf16[8,4,32,512]{3,2,1,0:T(8,128)(2,1)} %extract0.1), calls=%async_computation | async-start | bytes 2097152 | tf_op jit(solution)/shard_map/all_to_all | solution.py:540
  24.9 4.3 %copy-start.3 = (bf16[8,4,32,512]{3,2,1,0:T(8,128)(2,1)}, bf16[8,4,32,512]{3,2,1,0:T(8,128)(2,1)S(1)}, u32[]{:S(2)}) copy-start(bf16[8,4,32,512]{3,2,1,0:T(8,128)(2,1)S(1)} %all-to-all-done.spread_ref) | copy-start | bytes 3145732
  24.9 105.4 %all-to-all-start.2 = ((bf16[8,4,32,512]{3,2,1,0:T(8,128)(2,1)}), bf16[8,4,32,512]{3,2,1,0:T(8,128)(2,1)S(1)}, u32[]{:S(2)}, u32[]{:S(2)}) async-start(bf16[8,4,32,512]{3,2,1,0:T(8,128)(2,1)} %extract1.1), calls=%async_computation.2 | async-start | bytes 2097152 | tf_op jit(solution)/shard_map/all_to_all | solution.py:540
  46.9 25.0 %collective-permute-start = (bf16[4,4,32,512]{3,2,1,0:T(8,128)(2,1)}, bf16[4,4,32,512]{3,2,1,0:T(8,128)(2,1)S(1)}, u32[]{:S(2)}, u32[]{:S(2)}) collective-permute-start(bf16[4,4,32,512]{3,2,1,0:T(8,128)(2,1)} %pick.2.near_ref), channel_id=1, source_target_pairs={{0,16},{2,18},{4,20},{6,22},{8,24},{10,26},{12,28},{14,30},{16,0},... | collective-permute-start | bytes 1572872 | tf_op jit(solution)/shard_map/ppermute | solution.py:554
  71.9 0.8 copy-start.5
  130.3 1.0 copy-start.2
  131.3 99.4 %all-to-all-start.1 = ((bf16[8,7,32,512]{3,2,1,0:T(8,128)(2,1)}), bf16[8,7,32,512]{3,2,1,0:T(8,128)(2,1)S(1)}, u32[]{:S(2)}, u32[]{:S(2)}) async-start(bf16[8,7,32,512]{3,2,1,0:T(8,128)(2,1)} %build.2), calls=%async_computation.1 | async-start | bytes 3670016 | tf_op jit(solution)/shard_map/all_to_all | solution.py:540
  154.1 26.1 %collective-permute-start.2 = (bf16[4,4,32,512]{3,2,1,0:T(8,128)(2,1)}, bf16[4,4,32,512]{3,2,1,0:T(8,128)(2,1)S(1)}, u32[]{:S(2)}, u32[]{:S(2)}) collective-permute-start(bf16[4,4,32,512]{3,2,1,0:T(8,128)(2,1)} %pick.3.near_ref), channel_id=1, source_target_pairs={{0,16},{2,18},{4,20},{6,22},{8,24},{10,26},{12,28},{14,30},{16,0},... | collective-permute-start | bytes 1572872 | tf_op jit(solution)/shard_map/ppermute | solution.py:554
  180.2 0.8 copy-start.4
  230.6 25.6 %copy-start = (bf16[8,7,32,512]{3,2,1,0:T(8,128)(2,1)}, bf16[8,7,32,512]{3,2,1,0:T(8,128)(2,1)S(1)}, u32[]{:S(2)}) copy-start(bf16[8,7,32,512]{3,2,1,0:T(8,128)(2,1)S(1)} %all-to-all-done.1.refs_0_) | copy-start | bytes 5505028
  230.7 24.1 %all-to-all-start.3 = ((bf16[8,6,32,512]{3,2,1,0:T(8,128)(2,1)}), bf16[8,6,32,512]{3,2,1,0:T(8,128)(2,1)S(1)}, u32[]{:S(2)}, u32[]{:S(2)}) async-start(bf16[8,6,32,512]{3,2,1,0:T(8,128)(2,1)} %build.3), calls=%async_computation.3 | async-start | bytes 3145728 | tf_op jit(solution)/shard_map/all_to_all | solution.py:540
  234.7 21.5 %collective-permute-start.1 = (bf16[8,7,32,512]{3,2,1,0:T(8,128)(2,1)S(1)}, bf16[8,7,32,512]{3,2,1,0:T(8,128)(2,1)}, u32[]{:S(2)}, u32[]{:S(2)}) collective-permute-start(bf16[8,7,32,512]{3,2,1,0:T(8,128)(2,1)S(1)} %all-to-all-done.1.refs_0_), channel_id=1, source_target_pairs={{1,0},{0,1},{3,2},{2,3},{5,4},{4,5},{7,6},{6,7},{9,8},{8,9},{11,10... | collective-permute-start | bytes 5505032 | tf_op jit(solution)/shard_map/ppermute | solution.py:546
  254.8 15.2 %copy-start.1 = (bf16[8,6,32,512]{3,2,1,0:T(8,128)(2,1)}, bf16[8,6,32,512]{3,2,1,0:T(8,128)(2,1)S(1)}, u32[]{:S(2)}) copy-start(bf16[8,6,32,512]{3,2,1,0:T(8,128)(2,1)S(1)} %all-to-all-done.3.refs_2_) | copy-start | bytes 4718596
  254.8 15.2 %collective-permute-start.3 = (bf16[8,6,32,512]{3,2,1,0:T(8,128)(2,1)S(1)}, bf16[8,6,32,512]{3,2,1,0:T(8,128)(2,1)}, u32[]{:S(2)}, u32[]{:S(2)}) collective-permute-start(bf16[8,6,32,512]{3,2,1,0:T(8,128)(2,1)S(1)} %all-to-all-done.3.refs_2_), channel_id=1, source_target_pairs={{1,0},{0,1},{3,2},{2,3},{5,4},{4,5},{7,6},{6,7},{9,8},{8,9},{11,10... | collective-permute-start | bytes 4718600 | tf_op jit(solution)/shard_map/ppermute | solution.py:546
where the time goes:
time: 299 us; the launch traced here: 296 us
  Pallas kernels  192 us (64%)
  waiting for transfers between devices  73.8 us (25%)
  starting transfers between devices  27 us (9%)
    pallas_call x2, Pallas kernels, build_call(): pl.pallas_call(kernel, out_shape=jax.ShapeDtypeStruct((p.half_tri, rows,...  107 us
    ppermute x2, waiting for transfers between devices, planned(): far = [lax.ppermute(x, 'tri', swap) for x in near]  45.6 us
    pallas_call x2, Pallas kernels, pick_call(): pl.pallas_call(kernel, out_shape=jax.ShapeDtypeStruct((p.groups,) + sprea...  35.4 us
    all_to_all x4, waiting for transfers between devices, exchange(): lax.all_to_all(x, 'tri', split_axis=0, concat_axis=0, tiled=True, axis_in...  28.2 us
    pallas_call x1, Pallas kernels, update_call(): pl.pallas_call(kernel, out_shape=jax.ShapeDtypeStruct(current.shape, jnp....  25.9 us
    all_to_all x4, starting transfers between devices, exchange(): lax.all_to_all(x, 'tri', split_axis=0, concat_axis=0, tiled=True, axis_in...  18.7 us
    pallas_call x1, Pallas kernels, inverse_call(): pl.pallas_call(kernel, out_shape=(square_shape, square_shape), grid_spec=...  13.8 us
    pallas_call x2, Pallas kernels, extract_call(): pl.pallas_call(kernel, out_shape=jax.ShapeDtypeStruct((p.half_tri, p.in_c...  8.6 us
  transfers between devices with their start and end apart: 8, of which 4 were waited for; matrix products, arithmetic and copies ran while one was open for 0% of the time, Pallas kernels for 54%

commit v1 on v0

--- a/solution.py
+++ b/solution.py
@@ -264,15 +264,14 @@
         for copy in copies:
             copy.wait()
 
-    any_space = pl.BlockSpec(memory_space=pl.ANY)
     return pl.pallas_call(
         kernel,
         out_shape=jax.ShapeDtypeStruct((p.groups,) + spread.shape[1:], jnp.bfloat16),
         grid_spec=pltpu.PrefetchScalarGridSpec(
             num_scalar_prefetch=1,
             grid=(),
-            in_specs=[any_space],
-            out_specs=any_space,
+            in_specs=[pl.BlockSpec(memory_space=pltpu.VMEM)],
+            out_specs=pl.BlockSpec(memory_space=pl.ANY),
             scratch_shapes=[pltpu.SemaphoreType.DMA((p.groups,))],
         ),
         name="pick",
@@ -318,15 +317,14 @@
             if with_pivot:
                 await_part(end, p.in_chunk + p.wide, 1, sems.at[end, 2])
 
-    any_space = pl.BlockSpec(memory_space=pl.ANY)
     return pl.pallas_call(
         kernel,
         out_shape=jax.ShapeDtypeStruct((p.half_tri, rows, p.piece, p.order), jnp.bfloat16),
         grid_spec=pltpu.PrefetchScalarGridSpec(
             num_scalar_prefetch=1,
             grid=(),
-            in_specs=[any_space, any_space],
-            out_specs=any_space,
+            in_specs=[pl.BlockSpec(memory_space=pltpu.VMEM)] * 2,
+            out_specs=pl.BlockSpec(memory_space=pl.ANY),
             scratch_shapes=[pltpu.SemaphoreType.DMA((p.half_tri, 3))],
         ),
         name="build",
@@ -424,6 +422,9 @@
                 pltpu.VMEM((order, order), jnp.bfloat16),
                 pltpu.SemaphoreType.DMA,
             ],
+        ),
+        cost_estimate=pl.CostEstimate(
+            flops=60 * 2 * order**3, bytes_accessed=4 * order**2, transcendentals=0
         ),
         name="inverse",
     )(table, *arrived)

time: 299 us -> 171 us (0.57)
  Pallas kernels: 192 us -> 63.3 us
  starting transfers between devices: 27 us -> 34.7 us
  waiting for transfers between devices: 73.8 us -> 68.7 us
    pallas_call x2, Pallas kernels: 107 us -> 6.55 us  [build_call(): pl.pallas_call(kernel, out_shape=jax.ShapeDtypeStruct((p.half_tri, rows,...]
    pallas_call x2, Pallas kernels: 35.4 us -> 5.53 us  [pick_call(): pl.pallas_call(kernel, out_shape=jax.ShapeDtypeStruct((p.groups,) + sprea...]
    all_to_all x4, waiting for transfers between devices: 28.2 us -> 22.9 us  [exchange(): lax.all_to_all(x, 'tri', split_axis=0, concat_axis=0, tiled=True, axis_in...]
    ppermute x2, starting transfers between devices: 2.89 us -> 8.17 us  [arrivals(): lax.ppermute(x, 'sub', [((i + shift) % p.subs, i) for i in range(p.subs)])]
  transfers between devices with their start and end apart: 8 -> 8, of which waited for: 4 -> 4; matrix products, arithmetic and copies ran while one was open for 0% -> 0% of each run, Pallas kernels for 54% -> 18%
where the time goes in v1:
time: 171 us; the launch traced here: 169 us
  waiting for transfers between devices  68.7 us (40%)
  Pallas kernels  63.3 us (37%)
  starting transfers between devices  34.7 us (20%)
  local copies, waits for them, and re-layouts  2.61 us (2%)
    ppermute x2, waiting for transfers between devices, planned(): far = [lax.ppermute(x, 'tri', swap) for x in near]  45.9 us
    pallas_call x1, Pallas kernels, update_call(): pl.pallas_call(kernel, out_shape=jax.ShapeDtypeStruct(current.shape, jnp....  27.4 us
    all_to_all x4, waiting for transfers between devices, exchange(): lax.all_to_all(x, 'tri', split_axis=0, concat_axis=0, tiled=True, axis_in...  22.9 us
    all_to_all x4, starting transfers between devices, exchange(): lax.all_to_all(x, 'tri', split_axis=0, concat_axis=0, tiled=True, axis_in...  21.1 us
    pallas_call x1, Pallas kernels, inverse_call(): pl.pallas_call(kernel, out_shape=(square_shape, square_shape), grid_spec=...  13.8 us
    pallas_call x2, Pallas kernels, extract_call(): pl.pallas_call(kernel, out_shape=jax.ShapeDtypeStruct((p.half_tri, p.in_c...  8.6 us
    ppermute x2, starting transfers between devices, arrivals(): lax.ppermute(x, 'sub', [((i + shift) % p.subs, i) for i in range(p.subs)])  8.17 us
    pallas_call x2, Pallas kernels, build_call(): pl.pallas_call(kernel, out_shape=jax.ShapeDtypeStruct((p.half_tri, rows,...  6.55 us
  transfers between devices with their start and end apart: 8, of which 4 were waited for; matrix products, arithmetic and copies ran while one was open for 0% of the time, Pallas kernels for 18%

profile of v1, /device:TPU:1, one launch (start us, length us, event | category | flops | bytes accessed | tf_op | source)
XLA Modules:
  0.0 169.5 jit_solution(973262384601982334)
XLA Ops:
  0.0 1.5 table.1.t
  1.5 4.3 %extract0.1 = bf16[8,4,32,512]{3,2,1,0:T(8,128)(2,1)} custom-call(s32[186]{0:T(256)} %table.1.t, f32[36,256,512]{2,1,0:T(8,128)} %bitcast.2), custom_call_target="tpu_custom_call" | custom-call | tf_op jit(solution)/shard_map/extract0/pallas_call | solution.py:236
  5.8 5.3 %all-to-all-start = ((bf16[8,4,32,512]{3,2,1,0:T(8,128)(2,1)}), bf16[8,4,32,512]{3,2,1,0:T(8,128)(2,1)S(1)}, u32[]{:S(2)}, u32[]{:S(2)}) async-start(bf16[8,4,32,512]{3,2,1,0:T(8,128)(2,1)} %extract0.1), calls=%async_computation | async-start | bytes 2097152 | tf_op jit(solution)/shard_map/all_to_all | solution.py:541
  11.0 4.3 %extract1.1 = bf16[8,4,32,512]{3,2,1,0:T(8,128)(2,1)} custom-call(s32[186]{0:T(256)} %table.1.t, f32[36,256,512]{2,1,0:T(8,128)} %bitcast.3), custom_call_target="tpu_custom_call" | custom-call | tf_op jit(solution)/shard_map/extract1/pallas_call | solution.py:236
  15.4 9.5 %all-to-all-done.spread_ref = bf16[8,4,32,512]{3,2,1,0:T(8,128)(2,1)S(1)} async-done(((bf16[8,4,32,512]{3,2,1,0:T(8,128)(2,1)}), bf16[8,4,32,512]{3,2,1,0:T(8,128)(2,1)S(1)}, u32[]{:S(2)}, u32[]{:S(2)}) %all-to-all-start) | async-done | bytes 1048608 | tf_op jit(solution)/shard_map/all_to_all | solution.py:541
  24.9 0.0 copy-start.3
  24.9 4.2 %all-to-all-start.2 = ((bf16[8,4,32,512]{3,2,1,0:T(8,128)(2,1)}), bf16[8,4,32,512]{3,2,1,0:T(8,128)(2,1)S(1)}, u32[]{:S(2)}, u32[]{:S(2)}) async-start(bf16[8,4,32,512]{3,2,1,0:T(8,128)(2,1)} %extract1.1), calls=%async_computation.2 | async-start | bytes 2097152 | tf_op jit(solution)/shard_map/all_to_all | solution.py:541
  29.1 0.0 copy-done.3
  29.1 2.8 %pick.2.near_ref = bf16[4,4,32,512]{3,2,1,0:T(8,128)(2,1)} custom-call(s32[186]{0:T(256)} %table.1.t, bf16[8,4,32,512]{3,2,1,0:T(8,128)(2,1)} %copy-done.3), custom_call_target="tpu_custom_call" | custom-call | tf_op jit(solution)/shard_map/pick/pallas_call | solution.py:267
  31.9 2.4 %collective-permute-start = (bf16[4,4,32,512]{3,2,1,0:T(8,128)(2,1)}, bf16[4,4,32,512]{3,2,1,0:T(8,128)(2,1)S(1)}, u32[]{:S(2)}, u32[]{:S(2)}) collective-permute-start(bf16[4,4,32,512]{3,2,1,0:T(8,128)(2,1)} %pick.2.near_ref), channel_id=1, source_target_pairs={{0,16},{2,18},{4,20},{6,22},{8,24},{10,26},{12,28},{14,30},{16,0},... | collective-permute-start | bytes 1572872 | tf_op jit(solution)/shard_map/ppermute | solution.py:555
  34.3 22.5 %collective-permute-done.far_ref = bf16[4,4,32,512]{3,2,1,0:T(8,128)(2,1)S(1)} collective-permute-done((bf16[4,4,32,512]{3,2,1,0:T(8,128)(2,1)}, bf16[4,4,32,512]{3,2,1,0:T(8,128)(2,1)S(1)}, u32[]{:S(2)}, u32[]{:S(2)}) %collective-permute-start) | collective-permute-done | bytes 524320 | tf_op jit(solution)/shard_map/ppermute | solution.py:555
  56.8 0.0 copy-start.5
  56.8 0.8 copy-done.5
  57.6 3.3 %build.2 = bf16[8,7,32,512]{3,2,1,0:T(8,128)(2,1)} custom-call(s32[186]{0:T(256)} %table.1.t, bf16[4,4,32,512]{3,2,1,0:T(8,128)(2,1)} %pick.2.near_ref, bf16[4,4,32,512]{3,2,1,0:T(8,128)(2,1)} %copy-done.5), custom_call_target="tpu_custom_call" | custom-call | tf_op jit(solution)/shard_map/build/pallas_call | solution.py:320
  60.9 0.0 all-to-all-done.2.spread_ref
  60.9 0.0 copy-start.2
  60.9 1.0 copy-done.2
  61.9 3.6 %all-to-all-start.1 = ((bf16[8,7,32,512]{3,2,1,0:T(8,128)(2,1)}), bf16[8,7,32,512]{3,2,1,0:T(8,128)(2,1)S(1)}, u32[]{:S(2)}, u32[]{:S(2)}) async-start(bf16[8,7,32,512]{3,2,1,0:T(8,128)(2,1)} %build.2), calls=%async_computation.1 | async-start | bytes 3670016 | tf_op jit(solution)/shard_map/all_to_all | solution.py:541
  65.5 2.8 %pick.3.near_ref = bf16[4,4,32,512]{3,2,1,0:T(8,128)(2,1)} custom-call(s32[186]{0:T(256)} %table.1.t, bf16[8,4,32,512]{3,2,1,0:T(8,128)(2,1)} %copy-done.2), custom_call_target="tpu_custom_call" | custom-call | tf_op jit(solution)/shard_map/pick/pallas_call | solution.py:267
  68.3 3.1 %collective-permute-start.2 = (bf16[4,4,32,512]{3,2,1,0:T(8,128)(2,1)}, bf16[4,4,32,512]{3,2,1,0:T(8,128)(2,1)S(1)}, u32[]{:S(2)}, u32[]{:S(2)}) collective-permute-start(bf16[4,4,32,512]{3,2,1,0:T(8,128)(2,1)} %pick.3.near_ref), channel_id=1, source_target_pairs={{0,16},{2,18},{4,20},{6,22},{8,24},{10,26},{12,28},{14,30},{16,0},... | collective-permute-start | bytes 1572872 | tf_op jit(solution)/shard_map/ppermute | solution.py:555
  71.4 23.4 %collective-permute-done.2.far_ref = bf16[4,4,32,512]{3,2,1,0:T(8,128)(2,1)S(1)} collective-permute-done((bf16[4,4,32,512]{3,2,1,0:T(8,128)(2,1)}, bf16[4,4,32,512]{3,2,1,0:T(8,128)(2,1)S(1)}, u32[]{:S(2)}, u32[]{:S(2)}) %collective-permute-start.2) | collective-permute-done | bytes 524320 | tf_op jit(solution)/shard_map/ppermute | solution.py:555
  94.7 0.0 copy-start.4
  94.7 0.8 copy-done.4
  95.6 3.3 %build.3 = bf16[8,6,32,512]{3,2,1,0:T(8,128)(2,1)} custom-call(s32[186]{0:T(256)} %table.1.t, bf16[4,4,32,512]{3,2,1,0:T(8,128)(2,1)} %pick.3.near_ref, bf16[4,4,32,512]{3,2,1,0:T(8,128)(2,1)} %copy-done.4), custom_call_target="tpu_custom_call" | custom-call | tf_op jit(solution)/shard_map/build/pallas_call | solution.py:320
  98.8 0.0 all-to-all-done.1.refs_0_
  98.8 0.0 copy-start
  98.8 7.9 %all-to-all-start.3 = ((bf16[8,6,32,512]{3,2,1,0:T(8,128)(2,1)}), bf16[8,6,32,512]{3,2,1,0:T(8,128)(2,1)S(1)}, u32[]{:S(2)}, u32[]{:S(2)}) async-start(bf16[8,6,32,512]{3,2,1,0:T(8,128)(2,1)} %build.3), calls=%async_computation.3 | async-start | bytes 3145728 | tf_op jit(solution)/shard_map/all_to_all | solution.py:541
  106.7 3.5 %collective-permute-start.1 = (bf16[8,7,32,512]{3,2,1,0:T(8,128)(2,1)S(1)}, bf16[8,7,32,512]{3,2,1,0:T(8,128)(2,1)}, u32[]{:S(2)}, u32[]{:S(2)}) collective-permute-start(bf16[8,7,32,512]{3,2,1,0:T(8,128)(2,1)S(1)} %all-to-all-done.1.refs_0_), channel_id=1, source_target_pairs={{1,0},{0,1},{3,2},{2,3},{5,4},{4,5},{7,6},{6,7},{9,8},{8,9},{11,10... | collective-permute-start | bytes 5505032 | tf_op jit(solution)/shard_map/ppermute | solution.py:547
  110.2 13.3 %all-to-all-done.3.refs_2_ = bf16[8,6,32,512]{3,2,1,0:T(8,128)(2,1)S(1)} async-done(((bf16[8,6,32,512]{3,2,1,0:T(8,128)(2,1)}), bf16[8,6,32,512]{3,2,1,0:T(8,128)(2,1)S(1)}, u32[]{:S(2)}, u32[]{:S(2)}) %all-to-all-start.3) | async-done | bytes 1572896 | tf_op jit(solution)/shard_map/all_to_all | solution.py:541
  123.6 0.0 copy-start.1
  123.6 4.7 %collective-permute-start.3 = (bf16[8,6,32,512]{3,2,1,0:T(8,128)(2,1)S(1)}, bf16[8,6,32,512]{3,2,1,0:T(8,128)(2,1)}, u32[]{:S(2)}, u32[]{:S(2)}) collective-permute-start(bf16[8,6,32,512]{3,2,1,0:T(8,128)(2,1)S(1)} %all-to-all-done.3.refs_2_), channel_id=1, source_target_pairs={{1,0},{0,1},{3,2},{2,3},{5,4},{4,5},{7,6},{6,7},{9,8},{8,9},{11,10... | collective-permute-start | bytes 4718600 | tf_op jit(solution)/shard_map/ppermute | solution.py:547
  128.2 0.0 collective-permute-done.1.refs_1_
  128.2 0.0 copy-done
  128.2 13.8 %inverse.1 = (bf16[512,512]{1,0:T(8,128)(2,1)}, bf16[512,512]{1,0:T(8,128)(2,1)}) custom-call(s32[186]{0:T(256)} %table.1.t, bf16[8,7,32,512]{3,2,1,0:T(8,128)(2,1)} %copy-done, bf16[8,7,32,512]{3,2,1,0:T(8,128)(2,1)} %collective-permute-done.1.refs_1_), custom_call_target="tpu_custom_call" | custom-call | flops 16106127360 | bytes 1048576 | tf_op jit(solution)/shard_map/inverse/pallas_call | solution.py:410
  142.0 0.0 copy-done.1
  142.0 0.0 collective-permute-done.3.refs_3_
  142.0 27.4 %update.1 = f32[36,256,512]{2,1,0:T(8,128)} custom-call(s32[186]{0:T(256)} %table.1.t, f32[36,256,512]{2,1,0:T(8,128)} %bitcast.4, bf16[512,512]{1,0:T(8,128)(2,1)} %get-tuple-element.7.high, bf16[512,512]{1,0:T(8,128)(2,1)} %get-tuple-element.8.low, bf16[8,7,32,512]{3,2,1,0:T(8,128)(2,1)} %copy-done, ...), custom_call_target="tpu_custom_call" | custom-call | tf_op jit(solution)/shard_map/update/pallas_call | solution.py:513
Async XLA Ops:
  5.8 19.1 %all-to-all-start = ((bf16[8,4,32,512]{3,2,1,0:T(8,128)(2,1)}), bf16[8,4,32,512]{3,2,1,0:T(8,128)(2,1)S(1)}, u32[]{:S(2)}, u32[]{:S(2)}) async-start(bf16[8,4,32,512]{3,2,1,0:T(8,128)(2,1)} %extract0.1), calls=%async_computation | async-start | bytes 2097152 | tf_op jit(solution)/shard_map/all_to_all | solution.py:541
  24.9 4.3 %copy-start.3 = (bf16[8,4,32,512]{3,2,1,0:T(8,128)(2,1)}, bf16[8,4,32,512]{3,2,1,0:T(8,128)(2,1)S(1)}, u32[]{:S(2)}) copy-start(bf16[8,4,32,512]{3,2,1,0:T(8,128)(2,1)S(1)} %all-to-all-done.spread_ref) | copy-start | bytes 3145732
  24.9 36.0 %all-to-all-start.2 = ((bf16[8,4,32,512]{3,2,1,0:T(8,128)(2,1)}), bf16[8,4,32,512]{3,2,1,0:T(8,128)(2,1)S(1)}, u32[]{:S(2)}, u32[]{:S(2)}) async-start(bf16[8,4,32,512]{3,2,1,0:T(8,128)(2,1)} %extract1.1), calls=%async_computation.2 | async-start | bytes 2097152 | tf_op jit(solution)/shard_map/all_to_all | solution.py:541
  31.9 24.9 %collective-permute-start = (bf16[4,4,32,512]{3,2,1,0:T(8,128)(2,1)}, bf16[4,4,32,512]{3,2,1,0:T(8,128)(2,1)S(1)}, u32[]{:S(2)}, u32[]{:S(2)}) collective-permute-start(bf16[4,4,32,512]{3,2,1,0:T(8,128)(2,1)} %pick.2.near_ref), channel_id=1, source_target_pairs={{0,16},{2,18},{4,20},{6,22},{8,24},{10,26},{12,28},{14,30},{16,0},... | collective-permute-start | bytes 1572872 | tf_op jit(solution)/shard_map/ppermute | solution.py:555
  56.8 0.8 copy-start.5
  60.9 1.0 copy-start.2
  61.9 36.9 %all-to-all-start.1 = ((bf16[8,7,32,512]{3,2,1,0:T(8,128)(2,1)}), bf16[8,7,32,512]{3,2,1,0:T(8,128)(2,1)S(1)}, u32[]{:S(2)}, u32[]{:S(2)}) async-start(bf16[8,7,32,512]{3,2,1,0:T(8,128)(2,1)} %build.2), calls=%async_computation.1 | async-start | bytes 3670016 | tf_op jit(solution)/shard_map/all_to_all | solution.py:541
  68.3 26.4 %collective-permute-start.2 = (bf16[4,4,32,512]{3,2,1,0:T(8,128)(2,1)}, bf16[4,4,32,512]{3,2,1,0:T(8,128)(2,1)S(1)}, u32[]{:S(2)}, u32[]{:S(2)}) collective-permute-start(bf16[4,4,32,512]{3,2,1,0:T(8,128)(2,1)} %pick.3.near_ref), channel_id=1, source_target_pairs={{0,16},{2,18},{4,20},{6,22},{8,24},{10,26},{12,28},{14,30},{16,0},... | collective-permute-start | bytes 1572872 | tf_op jit(solution)/shard_map/ppermute | solution.py:555
  94.7 0.8 copy-start.4
  98.8 29.4 %copy-start = (bf16[8,7,32,512]{3,2,1,0:T(8,128)(2,1)}, bf16[8,7,32,512]{3,2,1,0:T(8,128)(2,1)S(1)}, u32[]{:S(2)}) copy-start(bf16[8,7,32,512]{3,2,1,0:T(8,128)(2,1)S(1)} %all-to-all-done.1.refs_0_) | copy-start | bytes 5505028
  98.8 24.7 %all-to-all-start.3 = ((bf16[8,6,32,512]{3,2,1,0:T(8,128)(2,1)}), bf16[8,6,32,512]{3,2,1,0:T(8,128)(2,1)S(1)}, u32[]{:S(2)}, u32[]{:S(2)}) async-start(bf16[8,6,32,512]{3,2,1,0:T(8,128)(2,1)} %build.3), calls=%async_computation.3 | async-start | bytes 3145728 | tf_op jit(solution)/shard_map/all_to_all | solution.py:541
  106.7 21.5 %collective-permute-start.1 = (bf16[8,7,32,512]{3,2,1,0:T(8,128)(2,1)S(1)}, bf16[8,7,32,512]{3,2,1,0:T(8,128)(2,1)}, u32[]{:S(2)}, u32[]{:S(2)}) collective-permute-start(bf16[8,7,32,512]{3,2,1,0:T(8,128)(2,1)S(1)} %all-to-all-done.1.refs_0_), channel_id=1, source_target_pairs={{1,0},{0,1},{3,2},{2,3},{5,4},{4,5},{7,6},{6,7},{9,8},{8,9},{11,10... | collective-permute-start | bytes 5505032 | tf_op jit(solution)/shard_map/ppermute | solution.py:547
  123.6 18.4 %copy-start.1 = (bf16[8,6,32,512]{3,2,1,0:T(8,128)(2,1)}, bf16[8,6,32,512]{3,2,1,0:T(8,128)(2,1)S(1)}, u32[]{:S(2)}) copy-start(bf16[8,6,32,512]{3,2,1,0:T(8,128)(2,1)S(1)} %all-to-all-done.3.refs_2_) | copy-start | bytes 4718596
  123.6 18.4 %collective-permute-start.3 = (bf16[8,6,32,512]{3,2,1,0:T(8,128)(2,1)S(1)}, bf16[8,6,32,512]{3,2,1,0:T(8,128)(2,1)}, u32[]{:S(2)}, u32[]{:S(2)}) collective-permute-start(bf16[8,6,32,512]{3,2,1,0:T(8,128)(2,1)S(1)} %all-to-all-done.3.refs_2_), channel_id=1, source_target_pairs={{1,0},{0,1},{3,2},{2,3},{5,4},{4,5},{7,6},{6,7},{9,8},{8,9},{11,10... | collective-permute-start | bytes 4718600 | tf_op jit(solution)/shard_map/ppermute | solution.py:547

commit v2 on v1

--- a/solution.py
+++ b/solution.py
@@ -7,6 +7,7 @@
 from jax.experimental import pallas as pl
 from jax.experimental.pallas import tpu as pltpu
 from jax.sharding import PartitionSpec as P
+
 
 NB = 32
 
@@ -146,9 +147,11 @@
         self.o_rg = self.o_here + self.groups
         self.o_cg = self.o_rg + self.half_tri
         self.o_hf = self.o_cg + self.half_tri
-        self.o_i = self.o_hf + self.half_tri
-        self.o_j = self.o_i + slots
-        self.o_live = self.o_j + slots
+        self.o_row_chunk = self.o_hf + self.half_tri
+        self.o_row_place = self.o_row_chunk + slots
+        self.o_col_chunk = self.o_row_place + slots
+        self.o_col_place = self.o_col_chunk + slots
+        self.o_live = self.o_col_place + slots
         self.o_new = self.o_live + slots
         self.size = self.o_new + slots
 
@@ -160,6 +163,11 @@
             and self.groups * self.groups == self.tri
             and self.subs * self.strip == self.order
         )
+
+    def place_of(self, member):
+        half, inner = divmod(member, self.half_group)
+        chunk, rest = divmod(inner, self.wide)
+        return chunk, half * self.wide + rest
 
     def tile_of(self, chunk, place):
         half, inner = divmod(place, self.wide)
@@ -212,8 +220,12 @@
             row = row_group * p.per_group + inner_i
             col = col_group * p.per_group + jnp.where(diag, 0, col_shift) + inner_j
             live = (inner_j >= 0) & (row > 0) & (col > 0)
-            out[p.o_i + slot] = inner_i
-            out[p.o_j + slot] = jnp.maximum(inner_j, 0)
+            tri_row, tri_col = p.place_of(tri_i), p.place_of(max(tri_j, 0))
+            box_row, box_col = p.place_of(box_i), p.place_of(max(box_j, 0))
+            out[p.o_row_chunk + slot] = jnp.where(diag, tri_row[0], box_row[0])
+            out[p.o_row_place + slot] = jnp.where(diag, tri_row[1], box_row[1])
+            out[p.o_col_chunk + slot] = jnp.where(diag, tri_col[0], box_col[0])
+            out[p.o_col_place + slot] = jnp.where(diag, tri_col[1], p.in_chunk + box_col[1])
             out[p.o_live + slot] = jnp.where(live, 1, 0)
             new_tri = 1 if tri_j == 0 else 0
             new_box = 1 if box_j == 0 else 0
@@ -227,6 +239,25 @@
         scratch_shapes=[pltpu.SMEM((p.tri,), jnp.int32)],
         name="table",
     )(cell_owner)
+
+
+IN_VMEM = pl.BlockSpec(memory_space=pltpu.VMEM)
+
+
+def in_vmem(x):
+    return pltpu.with_memory_space_constraint(x, pltpu.VMEM)
+
+
+def limit(mib):
+    return pltpu.CompilerParams(vmem_limit_bytes=mib * 2**20)
+
+
+def in_hbm(x):
+    return pltpu.with_memory_space_constraint(x, pltpu.HBM)
+
+
+def in_hbm(x):
+    return pltpu.with_memory_space_constraint(x, pltpu.HBM)
 
 
 def extract_call(p, table, current, chunk):
@@ -249,86 +280,57 @@
                 (p.half_tri, 1, p.piece, p.order), lambda i, t: (0, i, 0, 0)
             ),
         ),
-        name=f"extract{chunk}",
-    )(table, current)
+        compiler_params=limit(8),
+        name="extract",
+    )(table, in_hbm(current))
 
 
 def pick_call(p, table, spread):
-    def kernel(t, spread_ref, out, sems):
-        copies = [
-            pltpu.make_async_copy(spread_ref.at[t[p.o_src + g]], out.at[g], sems.at[g])
-            for g in range(p.groups)
-        ]
-        for copy in copies:
-            copy.start()
-        for copy in copies:
-            copy.wait()
+    def kernel(t, spread_ref, out):
+        for g in range(p.groups):
+            out[g] = spread_ref[t[p.o_src + g]]
 
     return pl.pallas_call(
         kernel,
-        out_shape=jax.ShapeDtypeStruct((p.groups,) + spread.shape[1:], jnp.bfloat16),
+        out_shape=pltpu.VMEM((p.groups,) + spread.shape[1:], jnp.bfloat16),
         grid_spec=pltpu.PrefetchScalarGridSpec(
-            num_scalar_prefetch=1,
-            grid=(),
-            in_specs=[pl.BlockSpec(memory_space=pltpu.VMEM)],
-            out_specs=pl.BlockSpec(memory_space=pl.ANY),
-            scratch_shapes=[pltpu.SemaphoreType.DMA((p.groups,))],
-        ),
+            num_scalar_prefetch=1, grid=(), in_specs=[IN_VMEM], out_specs=IN_VMEM
+        ),
+        compiler_params=limit(8),
         name="pick",
-    )(table, spread)
+    )(table, in_vmem(spread))
 
 
 def build_call(p, table, near, far, with_pivot):
     rows = p.in_chunk + p.wide + (1 if with_pivot else 0)
 
-    def kernel(t, near_ref, far_ref, out, sems):
-        def part(group, first, count, end, place, sem):
+    def kernel(t, near_ref, far_ref, out):
+        def part(group, first, count, end, place):
             here = t[p.o_here + group] == 1
-            target = out.at[end, pl.ds(place, count)]
 
             @pl.when(here)
             def _():
-                pltpu.make_async_copy(near_ref.at[group, pl.ds(first, count)], target, sem).start()
+                out[end, place : place + count] = near_ref[group, pl.ds(first, count)]
 
             @pl.when(jnp.logical_not(here))
             def _():
-                pltpu.make_async_copy(far_ref.at[group, pl.ds(first, count)], target, sem).start()
+                out[end, place : place + count] = far_ref[group, pl.ds(first, count)]
 
         for end in range(p.half_tri):
-            part(t[p.o_rg + end], 0, p.in_chunk, end, 0, sems.at[end, 0])
-            part(
-                t[p.o_cg + end],
-                t[p.o_hf + end] * p.wide,
-                p.wide,
-                end,
-                p.in_chunk,
-                sems.at[end, 1],
-            )
+            part(t[p.o_rg + end], 0, p.in_chunk, end, 0)
+            part(t[p.o_cg + end], t[p.o_hf + end] * p.wide, p.wide, end, p.in_chunk)
             if with_pivot:
-                part(0, 0, 1, end, p.in_chunk + p.wide, sems.at[end, 2])
-
-        def await_part(end, place, count, sem):
-            target = out.at[end, pl.ds(place, count)]
-            pltpu.make_async_copy(near_ref.at[0, pl.ds(0, count)], target, sem).wait()
-
-        for end in range(p.half_tri):
-            await_part(end, 0, p.in_chunk, sems.at[end, 0])
-            await_part(end, p.in_chunk, p.wide, sems.at[end, 1])
-            if with_pivot:
-                await_part(end, p.in_chunk + p.wide, 1, sems.at[end, 2])
+                part(0, 0, 1, end, p.in_chunk + p.wide)
 
     return pl.pallas_call(
         kernel,
-        out_shape=jax.ShapeDtypeStruct((p.half_tri, rows, p.piece, p.order), jnp.bfloat16),
+        out_shape=pltpu.VMEM((p.half_tri, rows, p.piece, p.order), jnp.bfloat16),
         grid_spec=pltpu.PrefetchScalarGridSpec(
-            num_scalar_prefetch=1,
-            grid=(),
-            in_specs=[pl.BlockSpec(memory_space=pltpu.VMEM)] * 2,
-            out_specs=pl.BlockSpec(memory_space=pl.ANY),
-            scratch_shapes=[pltpu.SemaphoreType.DMA((p.half_tri, 3))],
-        ),
+            num_scalar_prefetch=1, grid=(), in_specs=[IN_VMEM, IN_VMEM], out_specs=IN_VMEM
+        ),
+        compiler_params=limit(8),
         name="build",
-    )(table, near, far)
+    )(table, in_vmem(near), in_vmem(far))
 
 
 def inverse_call(p, table, arrived):
@@ -337,15 +339,11 @@
 
     def kernel(t, *refs):
         sources = refs[: p.subs]
-        high, low, pivot, x_wide, x_half, e_ref, sem = refs[p.subs :]
+        high, low, pivot, x_wide, x_half, e_ref = refs[p.subs :]
         for shift in range(p.subs):
             strip = lax.rem(t[p.o_sub] + shift, p.subs) * p.strip
-            for s in range(p.half_tri):
-                at = pl.multiple_of(strip + s * p.piece, p.piece)
-                pltpu.make_async_copy(
-                    sources[shift].at[s, place], pivot.at[pl.ds(at, p.piece)], sem
-                ).start()
-        pltpu.make_async_copy(pivot, pivot, sem).wait()
+            at = pl.multiple_of(strip, p.strip)
+            pivot[pl.ds(at, p.strip)] = sources[shift][:, place].reshape(p.strip, order)
 
         def dot(a, b):
             return lax.dot_general(
@@ -404,131 +402,100 @@
         high[...] = rounded
         low[...] = (x - rounded.astype(jnp.float32)).astype(jnp.bfloat16)
 
-    any_space = pl.BlockSpec(memory_space=pl.ANY)
-    whole = pl.BlockSpec((order, order), lambda t: (0, 0))
-    square_shape = jax.ShapeDtypeStruct((order, order), jnp.bfloat16)
+    square_shape = pltpu.VMEM((order, order), jnp.bfloat16)
     return pl.pallas_call(
         kernel,
         out_shape=(square_shape, square_shape),
         grid_spec=pltpu.PrefetchScalarGridSpec(
             num_scalar_prefetch=1,
             grid=(),
-            in_specs=[any_space] * p.subs,
-            out_specs=(pl.BlockSpec(memory_space=pltpu.VMEM),) * 2,
+            in_specs=[IN_VMEM] * p.subs,
+            out_specs=(IN_VMEM, IN_VMEM),
             scratch_shapes=[
                 pltpu.VMEM((order, order), jnp.bfloat16),
                 pltpu.VMEM((order, order), jnp.float32),
                 pltpu.VMEM((order, order), jnp.bfloat16),
                 pltpu.VMEM((order, order), jnp.bfloat16),
-                pltpu.SemaphoreType.DMA,
             ],
         ),
+        compiler_params=limit(12),
         cost_estimate=pl.CostEstimate(
             flops=60 * 2 * order**3, bytes_accessed=4 * order**2, transcendentals=0
         ),
         name="inverse",
-    )(table, *arrived)
+    )(table, *[in_vmem(x) for x in arrived])
 
 
 def update_call(p, table, current, arrived, inverse):
-    per_step = 2 if p.slots % 2 == 0 else 1
+    per_step = next(n for n in (4, 3, 2, 1) if p.slots % n == 0)
 
     def kernel(t, tiles, high, low, *refs):
         sources = [refs[k * p.subs : (k + 1) * p.subs] for k in range(p.chunks)]
-        out, left, right, scaled, left_sem, right_sem = refs[p.chunks * p.subs :]
+        out, scaled = refs[p.chunks * p.subs :]
         step = pl.program_id(0)
-        diag = t[p.o_diag] == 1
-
-        @pl.when(step == 0)
-        def _():
-            for k in range(p.chunks):
-                for shift in range(p.subs):
-                    ref = sources[k][shift]
-                    strip = lax.rem(t[p.o_sub] + shift, p.subs) * p.strip
-                    for s in range(p.half_tri):
-                        at = pl.multiple_of(strip + s * p.piece, p.piece)
-                        for half in range(2):
-                            tiles_at = pl.ds(half * p.half_group + k * p.wide, p.wide)
-                            part = ref.at[s, pl.ds(half * p.wide, p.wide)]
-                            if shift == 0:
-                                pltpu.make_async_copy(
-                                    part, left.at[tiles_at, pl.ds(s * p.piece, p.piece)], left_sem
-                                ).start()
-
-                            @pl.when(diag)
-                            def _():
-                                pltpu.make_async_copy(
-                                    part, right.at[tiles_at, pl.ds(at, p.piece)], right_sem
-                                ).start()
-
-                        @pl.when(jnp.logical_not(diag))
-                        def _():
-                            pltpu.make_async_copy(
-                                ref.at[s, pl.ds(p.in_chunk, p.wide)],
-                                right.at[pl.ds(k * p.wide, p.wide), pl.ds(at, p.piece)],
-                                right_sem,
-                            ).start()
-
-            pltpu.make_async_copy(left, left, left_sem).wait()
-
-            @pl.when(diag)
-            def _():
-                pltpu.make_async_copy(right, right, right_sem).wait()
-
-            @pl.when(jnp.logical_not(diag))
-            def _():
-                some = right.at[pl.ds(0, p.half_group)]
-                pltpu.make_async_copy(some, some, right_sem).wait()
+        sub = t[p.o_sub]
 
         for u in range(per_step):
             slot = step * per_step + u
-
-            @pl.when(t[p.o_new + slot] == 1)
-            def _():
-                strip = left[t[p.o_i + slot]]
-                dims = (((1,), (0,)), ((), ()))
-                product = lax.dot_general(
-                    strip, high[...], dims, preferred_element_type=jnp.float32
-                ) + lax.dot_general(strip, low[...], dims, preferred_element_type=jnp.float32)
-                scaled[...] = product.astype(jnp.bfloat16)
+            for k in range(p.chunks):
+
+                @pl.when((t[p.o_new + slot] == 1) & (t[p.o_row_chunk + slot] == k))
+                def _():
+                    strip = sources[k][0][:, t[p.o_row_place + slot]].reshape(p.strip, p.order)
+                    dims = (((1,), (0,)), ((), ()))
+                    product = lax.dot_general(
+                        strip, high[...], dims, preferred_element_type=jnp.float32
+                    ) + lax.dot_general(strip, low[...], dims, preferred_element_type=jnp.float32)
+                    scaled[...] = product.astype(jnp.bfloat16)
 
             live = t[p.o_live + slot] == 1
-
-            @pl.when(live)
-            def _():
-                out[u] = tiles[u] + lax.dot_general(
-                    scaled[...],
-                    right[t[p.o_j + slot]],
-                    (((1,), (1,)), ((), ())),
-                    preferred_element_type=jnp.float32,
-                )
+            for k in range(p.chunks):
+
+                @pl.when(live & (t[p.o_col_chunk + slot] == k))
+                def _():
+                    strips = [
+                        sources[k][shift][:, t[p.o_col_place + slot]].reshape(p.strip, p.order)
+                        for shift in range(p.subs)
+                    ]
+                    for place in range(p.subs):
+                        strip = strips[0]
+                        for shift in range(1, p.subs):
+                            here = lax.rem(sub + shift, p.subs) == place
+                            strip = jnp.where(here, strips[shift], strip)
+                        at = slice(place * p.strip, (place + 1) * p.strip)
+                        out[u, :, at] = tiles[u, :, at] + lax.dot_general(
+                            scaled[...],
+                            strip,
+                            (((1,), (1,)), ((), ())),
+                            preferred_element_type=jnp.float32,
+                        )
 
             @pl.when(jnp.logical_not(live))
             def _():
                 out[u] = tiles[u]
 
-    any_space = pl.BlockSpec(memory_space=pl.ANY)
     block = pl.BlockSpec((per_step, p.strip, p.order), lambda i, t: (i, 0, 0))
-    square = pl.BlockSpec((p.order, p.order), lambda i, t: (0, 0))
     return pl.pallas_call(
         kernel,
         out_shape=jax.ShapeDtypeStruct(current.shape, jnp.float32),
         grid_spec=pltpu.PrefetchScalarGridSpec(
             num_scalar_prefetch=1,
             grid=(p.slots // per_step,),
-            in_specs=[block, square, square] + [any_space] * (p.chunks * p.subs),
+            in_specs=[block] + [IN_VMEM] * (2 + p.chunks * p.subs),
             out_specs=block,
-            scratch_shapes=[
-                pltpu.VMEM((p.per_group, p.strip, p.order), jnp.bfloat16),
-                pltpu.VMEM((p.per_group, p.order, p.order), jnp.bfloat16),
-                pltpu.VMEM((p.strip, p.order), jnp.bfloat16),
-                pltpu.SemaphoreType.DMA,
-                pltpu.SemaphoreType.DMA,
-            ],
-        ),
-        compiler_params=pltpu.CompilerParams(dimension_semantics=("arbitrary",)),
+            scratch_shapes=[pltpu.VMEM((p.strip, p.order), jnp.bfloat16)],
+        ),
+        compiler_params=pltpu.CompilerParams(
+            dimension_semantics=("arbitrary",), vmem_limit_bytes=24 * 2**20
+        ),
         name="update",
-    )(table, current, *inverse, *[ref for chunk in arrived for ref in chunk])
+    )(
+        table,
+        in_hbm(current),
+        in_vmem(inverse[0]),
+        in_vmem(inverse[1]),
+        *[in_vmem(ref) for chunk in arrived for ref in chunk],
+    )
 
 
 def planned(p, stored_tiles, cell_owner):
@@ -548,15 +515,17 @@
             for shift in range(1, p.subs)
         ]
 
-    near = []
+    near, far, arrived = [], [], []
     for chunk in range(p.chunks):
-        spread = exchange(extract_call(p, table, current, chunk))
+        pieces = extract_call(p, table, current, chunk)
+        spread = exchange(pieces)
         near.append(pick_call(p, table, spread))
-    far = [lax.ppermute(x, "tri", swap) for x in near]
-    arrived = []
+    for chunk in range(p.chunks):
+        far.append(lax.ppermute(near[chunk], "tri", swap))
     for chunk in range(p.chunks):
         built = build_call(p, table, near[chunk], far[chunk], chunk == 0)
-        arrived.append(arrivals(exchange(built)))
+        whole = exchange(built)
+        arrived.append(arrivals(whole))
     inverse = inverse_call(p, table, arrived[0])
     return update_call(p, table, current, arrived, inverse)[None]
 

time: 171 us -> 157 us (0.918)
  Pallas kernels: 63.3 us -> 49.1 us
  starting transfers between devices: 34.7 us -> 36.6 us
    pallas_call x4, Pallas kernels: 12.1 us -> 4.31 us  [the longest x2 3.12 us: build_call(): pl.pallas_call(kernel, out_shape=pltpu.VMEM((p.half_tri, rows, p.piece, p...]
    pallas_call x1, Pallas kernels: 27.4 us -> 21.7 us  [update_call(): pl.pallas_call(kernel, out_shape=jax.ShapeDtypeStruct(current.shape, jnp....]
    all_to_all x4, starting transfers between devices: 21.1 us -> 23.5 us  [exchange(): lax.all_to_all(x, 'tri', split_axis=0, concat_axis=0, tiled=True, axis_in...]
  transfers between devices with their start and end apart: 8 -> 8, of which waited for: 4 -> 5; matrix products, arithmetic and copies ran while one was open for 0% -> 0% of each run, Pallas kernels for 18% -> 14%
where the time goes in v2:
time: 157 us
  waiting for transfers between devices  69 us (44%)
  Pallas kernels  49.1 us (31%)
  starting transfers between devices  36.6 us (23%)
  local copies, waits for them, and re-layouts  1.8 us (1%)
    ppermute x2, waiting for transfers between devices, planned(): far.append(lax.ppermute(near[chunk], 'tri', swap))  45.2 us
    all_to_all x4, waiting for transfers between devices, exchange(): lax.all_to_all(x, 'tri', split_axis=0, concat_axis=0, tiled=True, axis_in...  23.9 us
    all_to_all x4, starting transfers between devices, exchange(): lax.all_to_all(x, 'tri', split_axis=0, concat_axis=0, tiled=True, axis_in...  23.5 us
    pallas_call x1, Pallas kernels, update_call(): pl.pallas_call(kernel, out_shape=jax.ShapeDtypeStruct(current.shape, jnp....  21.7 us
    pallas_call x1, Pallas kernels, inverse_call(): pl.pallas_call(kernel, out_shape=(square_shape, square_shape), grid_spec=...  13.2 us
    pallas_call x2, Pallas kernels, extract_call(): pl.pallas_call(kernel, out_shape=jax.ShapeDtypeStruct((p.half_tri, p.in_c...  8.28 us
    ppermute x2, starting transfers between devices, arrivals(): lax.ppermute(x, 'sub', [((i + shift) % p.subs, i) for i in range(p.subs)])  8.17 us
    ppermute x2, starting transfers between devices, planned(): far.append(lax.ppermute(near[chunk], 'tri', swap))  4.98 us
  transfers between devices with their start and end apart: 8, of which 5 were waited for; matrix products, arithmetic and copies ran while one was open for 0% of the time, Pallas kernels for 14%

profile of v2, /device:TPU:1, one launch (start us, length us, event | category | flops | bytes accessed | tf_op | source)
XLA Modules:
  0.0 156.6 jit_solution(9350021596325716536)
XLA Ops:
  0.0 1.5 table.1.t
  1.5 0.0 copy-start.1
  1.5 0.7 copy-done.1
  2.2 4.1 %extract.2 = bf16[8,4,32,512]{3,2,1,0:T(8,128)(2,1)} custom-call(s32[258]{0:T(512)S(1)} %copy-done.1, f32[36,256,512]{2,1,0:T(8,128)} %bitcast.2), custom_call_target="tpu_custom_call" | custom-call | tf_op jit(solution)/shard_map/extract/pallas_call | solution.py:267
  6.3 0.0 copy-start.2
  6.3 5.4 %all-to-all-start = ((bf16[8,4,32,512]{3,2,1,0:T(8,128)(2,1)}), bf16[8,4,32,512]{3,2,1,0:T(8,128)(2,1)S(1)}, u32[]{:S(2)}, u32[]{:S(2)}) async-start(bf16[8,4,32,512]{3,2,1,0:T(8,128)(2,1)} %extract.2), calls=%async_computation | async-start | bytes 2097152 | tf_op jit(solution)/shard_map/all_to_all | solution.py:508
  11.7 0.0 copy-done.2
  11.7 4.1 %extract.3 = bf16[8,4,32,512]{3,2,1,0:T(8,128)(2,1)} custom-call(s32[258]{0:T(512)S(1)} %copy-done.2, f32[36,256,512]{2,1,0:T(8,128)} %bitcast.3), custom_call_target="tpu_custom_call" | custom-call | tf_op jit(solution)/shard_map/extract/pallas_call | solution.py:267
  15.9 9.7 %all-to-all-done.spread_ref = bf16[8,4,32,512]{3,2,1,0:T(8,128)(2,1)S(1)} async-done(((bf16[8,4,32,512]{3,2,1,0:T(8,128)(2,1)}), bf16[8,4,32,512]{3,2,1,0:T(8,128)(2,1)S(1)}, u32[]{:S(2)}, u32[]{:S(2)}) %all-to-all-start) | async-done | bytes 1048608 | tf_op jit(solution)/shard_map/all_to_all | solution.py:508
  25.6 4.2 %all-to-all-start.2 = ((bf16[8,4,32,512]{3,2,1,0:T(8,128)(2,1)}), bf16[8,4,32,512]{3,2,1,0:T(8,128)(2,1)S(1)}, u32[]{:S(2)}, u32[]{:S(2)}) async-start(bf16[8,4,32,512]{3,2,1,0:T(8,128)(2,1)} %extract.3), calls=%async_computation.2 | async-start | bytes 2097152 | tf_op jit(solution)/shard_map/all_to_all | solution.py:508
  29.8 0.6 pick.2.near_ref
  30.4 2.4 %collective-permute-start = (bf16[4,4,32,512]{3,2,1,0:T(8,128)(2,1)S(1)}, bf16[4,4,32,512]{3,2,1,0:T(8,128)(2,1)S(1)}, u32[]{:S(2)}, u32[]{:S(2)}) collective-permute-start(bf16[4,4,32,512]{3,2,1,0:T(8,128)(2,1)S(1)} %pick.2.near_ref), channel_id=1, source_target_pairs={{0,16},{2,18},{4,20},{6,22},{8,24},{10,26},{12,28},{14,30},{16,0},... | collective-permute-start | bytes 1572872 | tf_op jit(solution)/shard_map/ppermute | solution.py:524
  32.8 19.0 %collective-permute-done.far_ref = bf16[4,4,32,512]{3,2,1,0:T(8,128)(2,1)S(1)} collective-permute-done((bf16[4,4,32,512]{3,2,1,0:T(8,128)(2,1)S(1)}, bf16[4,4,32,512]{3,2,1,0:T(8,128)(2,1)S(1)}, u32[]{:S(2)}, u32[]{:S(2)}) %collective-permute-start) | collective-permute-done | bytes 524320 | tf_op jit(solution)/shard_map/ppermute | solution.py:524
  51.8 2.2 %build.2 = bf16[8,7,32,512]{3,2,1,0:T(8,128)(2,1)} custom-call(s32[258]{0:T(512)S(1)} %copy-done.2, bf16[4,4,32,512]{3,2,1,0:T(8,128)(2,1)S(1)} %pick.2.near_ref, bf16[4,4,32,512]{3,2,1,0:T(8,128)(2,1)S(1)} %collective-permute-done.far_ref), custom_call_target="tpu_custom_call" | custom-call | tf_op jit(solution)/shard_map/build/pallas_call | solution.py:325
  54.1 0.0 all-to-all-done.2.spread_ref
  54.1 7.4 %all-to-all-start.1 = ((bf16[8,7,32,512]{3,2,1,0:T(8,128)(2,1)}), bf16[8,7,32,512]{3,2,1,0:T(8,128)(2,1)S(1)}, u32[]{:S(2)}, u32[]{:S(2)}) async-start(bf16[8,7,32,512]{3,2,1,0:T(8,128)(2,1)} %build.2), calls=%async_computation.1 | async-start | bytes 3670016 | tf_op jit(solution)/shard_map/all_to_all | solution.py:508
  61.4 0.6 pick.3.near_ref
  62.0 2.6 %collective-permute-start.2 = (bf16[4,4,32,512]{3,2,1,0:T(8,128)(2,1)S(1)}, bf16[4,4,32,512]{3,2,1,0:T(8,128)(2,1)S(1)}, u32[]{:S(2)}, u32[]{:S(2)}) collective-permute-start(bf16[4,4,32,512]{3,2,1,0:T(8,128)(2,1)S(1)} %pick.3.near_ref), channel_id=1, source_target_pairs={{0,16},{2,18},{4,20},{6,22},{8,24},{10,26},{12,28},{14,30},{16,0},... | collective-permute-start | bytes 1572872 | tf_op jit(solution)/shard_map/ppermute | solution.py:524
  64.6 26.2 %collective-permute-done.2.far_ref = bf16[4,4,32,512]{3,2,1,0:T(8,128)(2,1)S(1)} collective-permute-done((bf16[4,4,32,512]{3,2,1,0:T(8,128)(2,1)S(1)}, bf16[4,4,32,512]{3,2,1,0:T(8,128)(2,1)S(1)}, u32[]{:S(2)}, u32[]{:S(2)}) %collective-permute-start.2) | collective-permute-done | bytes 524320 | tf_op jit(solution)/shard_map/ppermute | solution.py:524
  90.8 0.9 build.3
  91.7 0.0 copy-start
  91.7 1.1 copy-done
  92.9 0.8 all-to-all-done.1.refs_0_
  93.7 6.4 %all-to-all-start.3 = ((bf16[8,6,32,512]{3,2,1,0:T(8,128)(2,1)}), bf16[8,6,32,512]{3,2,1,0:T(8,128)(2,1)S(1)}, u32[]{:S(2)}, u32[]{:S(2)}) async-start(bf16[8,6,32,512]{3,2,1,0:T(8,128)(2,1)} %copy-done), calls=%async_computation.3 | async-start | bytes 3145728 | tf_op jit(solution)/shard_map/all_to_all | solution.py:508
  100.1 3.5 %collective-permute-start.1 = (bf16[8,7,32,512]{3,2,1,0:T(8,128)(2,1)S(1)}, bf16[8,7,32,512]{3,2,1,0:T(8,128)(2,1)}, u32[]{:S(2)}, u32[]{:S(2)}) collective-permute-start(bf16[8,7,32,512]{3,2,1,0:T(8,128)(2,1)S(1)} %all-to-all-done.1.refs_0_), channel_id=1, source_target_pairs={{1,0},{0,1},{3,2},{2,3},{5,4},{4,5},{7,6},{6,7},{9,8},{8,9},{11,10... | collective-permute-start | bytes 5505032 | tf_op jit(solution)/shard_map/ppermute | solution.py:514
  103.6 13.3 %all-to-all-done.3.refs_2_ = bf16[8,6,32,512]{3,2,1,0:T(8,128)(2,1)S(1)} async-done(((bf16[8,6,32,512]{3,2,1,0:T(8,128)(2,1)}), bf16[8,6,32,512]{3,2,1,0:T(8,128)(2,1)S(1)}, u32[]{:S(2)}, u32[]{:S(2)}) %all-to-all-start.3) | async-done | bytes 1572896 | tf_op jit(solution)/shard_map/all_to_all | solution.py:508
  117.0 4.7 %collective-permute-start.3 = (bf16[8,6,32,512]{3,2,1,0:T(8,128)(2,1)S(1)}, bf16[8,6,32,512]{3,2,1,0:T(8,128)(2,1)S(1)}, u32[]{:S(2)}, u32[]{:S(2)}) collective-permute-start(bf16[8,6,32,512]{3,2,1,0:T(8,128)(2,1)S(1)} %all-to-all-done.3.refs_2_), channel_id=1, source_target_pairs={{1,0},{0,1},{3,2},{2,3},{5,4},{4,5},{7,6},{6,7},{9,8},{8,9},{11,10... | collective-permute-start | bytes 4718600 | tf_op jit(solution)/shard_map/ppermute | solution.py:514
  121.6 0.0 collective-permute-done.1.refs_1_
  121.6 13.2 %inverse.1 = (bf16[512,512]{1,0:T(8,128)(2,1)S(1)}, bf16[512,512]{1,0:T(8,128)(2,1)S(1)}) custom-call(s32[258]{0:T(512)S(1)} %copy-done.2, bf16[8,7,32,512]{3,2,1,0:T(8,128)(2,1)S(1)} %all-to-all-done.1.refs_0_, bf16[8,7,32,512]{3,2,1,0:T(8,128)(2,1)} %collective-permute-done.1.refs_1_), custom_call_target="tpu_custom_call" | custom-call | flops 16106127360 | bytes 1048576 | tf_op jit(solution)/shard_map/inverse/pallas_call | solution.py:406
  134.9 0.0 collective-permute-done.3.refs_3_
  134.9 21.7 %update.1 = f32[36,256,512]{2,1,0:T(8,128)} custom-call(s32[258]{0:T(512)S(1)} %copy-done.2, f32[36,256,512]{2,1,0:T(8,128)} %bitcast.4, bf16[512,512]{1,0:T(8,128)(2,1)S(1)} %get-tuple-element.7.high, bf16[512,512]{1,0:T(8,128)(2,1)S(1)} %get-tuple-element.8.low, bf16[8,7,32,512]{3,2,1,0:T(8,128)(2,1)S(1)} %all-to-all-done.1.refs_0_, ...), custom_call_target="tpu_custom_call" | custom-call | tf_op jit(solution)/shard_map/update/pallas_call | solution.py:478
Async XLA Ops:
  1.5 0.7 copy-start.1
  6.3 5.4 %copy-start.2 = (s32[258]{0:T(512)S(1)}, s32[258]{0:T(512)}, u32[]{:S(2)}) copy-start(s32[258]{0:T(512)} %table.1.t) | copy-start | bytes 3100
  6.3 19.3 %all-to-all-start = ((bf16[8,4,32,512]{3,2,1,0:T(8,128)(2,1)}), bf16[8,4,32,512]{3,2,1,0:T(8,128)(2,1)S(1)}, u32[]{:S(2)}, u32[]{:S(2)}) async-start(bf16[8,4,32,512]{3,2,1,0:T(8,128)(2,1)} %extract.2), calls=%async_computation | async-start | bytes 2097152 | tf_op jit(solution)/shard_map/all_to_all | solution.py:508
  25.6 28.5 %all-to-all-start.2 = ((bf16[8,4,32,512]{3,2,1,0:T(8,128)(2,1)}), bf16[8,4,32,512]{3,2,1,0:T(8,128)(2,1)S(1)}, u32[]{:S(2)}, u32[]{:S(2)}) async-start(bf16[8,4,32,512]{3,2,1,0:T(8,128)(2,1)} %extract.3), calls=%async_computation.2 | async-start | bytes 2097152 | tf_op jit(solution)/shard_map/all_to_all | solution.py:508
  30.4 21.4 %collective-permute-start = (bf16[4,4,32,512]{3,2,1,0:T(8,128)(2,1)S(1)}, bf16[4,4,32,512]{3,2,1,0:T(8,128)(2,1)S(1)}, u32[]{:S(2)}, u32[]{:S(2)}) collective-permute-start(bf16[4,4,32,512]{3,2,1,0:T(8,128)(2,1)S(1)} %pick.2.near_ref), channel_id=1, source_target_pairs={{0,16},{2,18},{4,20},{6,22},{8,24},{10,26},{12,28},{14,30},{16,0},... | collective-permute-start | bytes 1572872 | tf_op jit(solution)/shard_map/ppermute | solution.py:524
  54.1 39.6 %all-to-all-start.1 = ((bf16[8,7,32,512]{3,2,1,0:T(8,128)(2,1)}), bf16[8,7,32,512]{3,2,1,0:T(8,128)(2,1)S(1)}, u32[]{:S(2)}, u32[]{:S(2)}) async-start(bf16[8,7,32,512]{3,2,1,0:T(8,128)(2,1)} %build.2), calls=%async_computation.1 | async-start | bytes 3670016 | tf_op jit(solution)/shard_map/all_to_all | solution.py:508
  62.0 28.8 %collective-permute-start.2 = (bf16[4,4,32,512]{3,2,1,0:T(8,128)(2,1)S(1)}, bf16[4,4,32,512]{3,2,1,0:T(8,128)(2,1)S(1)}, u32[]{:S(2)}, u32[]{:S(2)}) collective-permute-start(bf16[4,4,32,512]{3,2,1,0:T(8,128)(2,1)S(1)} %pick.3.near_ref), channel_id=1, source_target_pairs={{0,16},{2,18},{4,20},{6,22},{8,24},{10,26},{12,28},{14,30},{16,0},... | collective-permute-start | bytes 1572872 | tf_op jit(solution)/shard_map/ppermute | solution.py:524
  91.7 1.2 copy-start
  93.7 23.3 %all-to-all-start.3 = ((bf16[8,6,32,512]{3,2,1,0:T(8,128)(2,1)}), bf16[8,6,32,512]{3,2,1,0:T(8,128)(2,1)S(1)}, u32[]{:S(2)}, u32[]{:S(2)}) async-start(bf16[8,6,32,512]{3,2,1,0:T(8,128)(2,1)} %copy-done), calls=%async_computation.3 | async-start | bytes 3145728 | tf_op jit(solution)/shard_map/all_to_all | solution.py:508
  100.1 21.5 %collective-permute-start.1 = (bf16[8,7,32,512]{3,2,1,0:T(8,128)(2,1)S(1)}, bf16[8,7,32,512]{3,2,1,0:T(8,128)(2,1)}, u32[]{:S(2)}, u32[]{:S(2)}) collective-permute-start(bf16[8,7,32,512]{3,2,1,0:T(8,128)(2,1)S(1)} %all-to-all-done.1.refs_0_), channel_id=1, source_target_pairs={{1,0},{0,1},{3,2},{2,3},{5,4},{4,5},{7,6},{6,7},{9,8},{8,9},{11,10... | collective-permute-start | bytes 5505032 | tf_op jit(solution)/shard_map/ppermute | solution.py:514
  117.0 17.9 %collective-permute-start.3 = (bf16[8,6,32,512]{3,2,1,0:T(8,128)(2,1)S(1)}, bf16[8,6,32,512]{3,2,1,0:T(8,128)(2,1)S(1)}, u32[]{:S(2)}, u32[]{:S(2)}) collective-permute-start(bf16[8,6,32,512]{3,2,1,0:T(8,128)(2,1)S(1)} %all-to-all-done.3.refs_2_), channel_id=1, source_target_pairs={{1,0},{0,1},{3,2},{2,3},{5,4},{4,5},{7,6},{6,7},{9,8},{8,9},{11,10... | collective-permute-start | bytes 4718600 | tf_op jit(solution)/shard_map/ppermute | solution.py:514

commit v3 on v2

--- a/solution.py
+++ b/solution.py
@@ -141,7 +141,8 @@
         self.in_chunk = 2 * self.wide
         self.o_sub = 0
         self.o_diag = 1
-        self.o_slot = 2
+        self.o_me = 2
+        self.o_slot = 3
         self.o_src = self.o_slot + self.per_group
         self.o_here = self.o_src + self.groups
         self.o_rg = self.o_here + self.groups
@@ -161,6 +162,7 @@
             and self.order % 128 == 0
             and self.half_group % self.chunks == 0
             and self.groups * self.groups == self.tri
+            and self.half_tri & (self.half_tri - 1) == 0
             and self.subs * self.strip == self.order
         )
 
@@ -191,6 +193,7 @@
         diag = down == across
         my_half = position // p.half_tri
         out[p.o_sub] = lax.axis_index("sub")
+        out[p.o_me] = position - my_half * p.half_tri
         out[p.o_diag] = jnp.where(diag, 1, 0)
         for chunk in range(p.chunks):
             for place in range(p.in_chunk):
@@ -260,6 +263,25 @@
     return pltpu.with_memory_space_constraint(x, pltpu.HBM)
 
 
+def mark_call(p, table):
+    def kernel(t, out):
+        def copy(i, _):
+            out[i] = t[i]
+            return 0
+
+        lax.fori_loop(0, p.size, copy, 0)
+
+    smem = pl.BlockSpec(memory_space=pltpu.SMEM)
+    return pl.pallas_call(
+        kernel,
+        out_shape=jax.ShapeDtypeStruct((p.size,), jnp.int32),
+        in_specs=[smem],
+        out_specs=smem,
+        compiler_params=limit(1),
+        name="mark",
+    )(table)
+
+
 def extract_call(p, table, current, chunk):
     def kernel(t, tile, out):
         out[...] = tile[...].reshape(p.half_tri, 1, p.piece, p.order).astype(jnp.bfloat16)
@@ -301,45 +323,72 @@
     )(table, in_vmem(spread))
 
 
-def build_call(p, table, near, far, with_pivot):
+def build_call(p, table, near, far, with_pivot, apart):
     rows = p.in_chunk + p.wide + (1 if with_pivot else 0)
 
-    def kernel(t, near_ref, far_ref, out):
-        def part(group, first, count, end, place):
+    def kernel(t, near_ref, far_ref, *outs):
+        def part(group, first, count, n, place):
             here = t[p.o_here + group] == 1
+            at = pl.ds(place, count)
+
+            def store(value):
+                if apart:
+                    outs[n][at] = value
+                else:
+                    outs[0][n, at] = value
 
             @pl.when(here)
             def _():
-                out[end, place : place + count] = near_ref[group, pl.ds(first, count)]
+                store(near_ref[group, pl.ds(first, count)])
 
             @pl.when(jnp.logical_not(here))
             def _():
-                out[end, place : place + count] = far_ref[group, pl.ds(first, count)]
-
-        for end in range(p.half_tri):
-            part(t[p.o_rg + end], 0, p.in_chunk, end, 0)
-            part(t[p.o_cg + end], t[p.o_hf + end] * p.wide, p.wide, end, p.in_chunk)
+                store(far_ref[group, pl.ds(first, count)])
+
+        for n in range(p.half_tri):
+            end = t[p.o_me] ^ n if apart else n
+            part(t[p.o_rg + end], 0, p.in_chunk, n, 0)
+            part(t[p.o_cg + end], t[p.o_hf + end] * p.wide, p.wide, n, p.in_chunk)
             if with_pivot:
-                part(0, 0, 1, end, p.in_chunk + p.wide)
-
-    return pl.pallas_call(
+                part(0, 0, 1, n, p.in_chunk + p.wide)
+
+    one = (rows, p.piece, p.order)
+    if apart:
+        out_shape = [pltpu.VMEM(one, jnp.bfloat16)] * p.half_tri
+    else:
+        out_shape = [pltpu.VMEM((p.half_tri,) + one, jnp.bfloat16)]
+    outs = pl.pallas_call(
         kernel,
-        out_shape=pltpu.VMEM((p.half_tri, rows, p.piece, p.order), jnp.bfloat16),
+        out_shape=out_shape,
         grid_spec=pltpu.PrefetchScalarGridSpec(
-            num_scalar_prefetch=1, grid=(), in_specs=[IN_VMEM, IN_VMEM], out_specs=IN_VMEM
+            num_scalar_prefetch=1,
+            grid=(),
+            in_specs=[IN_VMEM, IN_VMEM],
+            out_specs=[IN_VMEM] * len(out_shape),
         ),
         compiler_params=limit(8),
         name="build",
     )(table, in_vmem(near), in_vmem(far))
-
-
-def inverse_call(p, table, arrived):
+    return outs if apart else outs[0]
+
+
+def inverse_call(p, table, arrived, current):
+    loads = next(n for n in (6, 5, 4, 3, 2, 1) if p.slots % n == 0)
+    each = p.slots // loads
     place = p.in_chunk + p.wide
     order = p.order
 
     def kernel(t, *refs):
         sources = refs[: p.subs]
-        high, low, pivot, x_wide, x_half, e_ref = refs[p.subs :]
+        tiles, high, low, held, pivot, x_wide, x_half, e_ref, sems = refs[p.subs :]
+        copies = [
+            pltpu.make_async_copy(
+                tiles.at[pl.ds(n * each, each)], held.at[pl.ds(n * each, each)], sems.at[n]
+            )
+            for n in range(loads)
+        ]
+        for copy in copies:
+            copy.start()
         for shift in range(p.subs):
             strip = lax.rem(t[p.o_sub] + shift, p.subs) * p.strip
             at = pl.multiple_of(strip, p.strip)
@@ -401,21 +450,24 @@
         rounded = x.astype(jnp.bfloat16)
         high[...] = rounded
         low[...] = (x - rounded.astype(jnp.float32)).astype(jnp.bfloat16)
+        for copy in copies:
+            copy.wait()
 
     square_shape = pltpu.VMEM((order, order), jnp.bfloat16)
     return pl.pallas_call(
         kernel,
-        out_shape=(square_shape, square_shape),
+        out_shape=(square_shape, square_shape, pltpu.VMEM(current.shape, jnp.float32)),
         grid_spec=pltpu.PrefetchScalarGridSpec(
             num_scalar_prefetch=1,
             grid=(),
-            in_specs=[IN_VMEM] * p.subs,
-            out_specs=(IN_VMEM, IN_VMEM),
+            in_specs=[IN_VMEM] * p.subs + [pl.BlockSpec(memory_space=pltpu.HBM)],
+            out_specs=(IN_VMEM, IN_VMEM, IN_VMEM),
             scratch_shapes=[
                 pltpu.VMEM((order, order), jnp.bfloat16),
                 pltpu.VMEM((order, order), jnp.float32),
                 pltpu.VMEM((order, order), jnp.bfloat16),
                 pltpu.VMEM((order, order), jnp.bfloat16),
+                pltpu.SemaphoreType.DMA((loads,)),
             ],
         ),
         compiler_params=limit(12),
@@ -423,17 +475,28 @@
             flops=60 * 2 * order**3, bytes_accessed=4 * order**2, transcendentals=0
         ),
         name="inverse",
-    )(table, *[in_vmem(x) for x in arrived])
-
-
-def update_call(p, table, current, arrived, inverse):
+    )(table, *[in_vmem(x) for x in arrived], in_hbm(current))
+
+
+def update_call(p, table, held, together, apart, inverse):
     per_step = next(n for n in (4, 3, 2, 1) if p.slots % n == 0)
+    last = p.chunks - 1
+    n_together = last * p.subs
+    n_apart = p.subs * p.half_tri
 
     def kernel(t, tiles, high, low, *refs):
-        sources = [refs[k * p.subs : (k + 1) * p.subs] for k in range(p.chunks)]
-        out, scaled = refs[p.chunks * p.subs :]
+        sources = [refs[k * p.subs : (k + 1) * p.subs] for k in range(last)]
+        loose = refs[n_together : n_together + n_apart]
+        out, scaled, packed = refs[n_together + n_apart :]
+        sources.append([packed.at[shift] for shift in range(p.subs)])
         step = pl.program_id(0)
         sub = t[p.o_sub]
+
+        @pl.when(step == 0)
+        def _():
+            for shift in range(p.subs):
+                for n in range(p.half_tri):
+                    packed[shift, t[p.o_me] ^ n] = loose[shift * p.half_tri + n][...]
 
         for u in range(per_step):
             slot = step * per_step + u
@@ -463,7 +526,7 @@
                             here = lax.rem(sub + shift, p.subs) == place
                             strip = jnp.where(here, strips[shift], strip)
                         at = slice(place * p.strip, (place + 1) * p.strip)
-                        out[u, :, at] = tiles[u, :, at] + lax.dot_general(
+                        out[u, :, at] = tiles[slot, :, at] + lax.dot_general(
                             scaled[...],
                             strip,
                             (((1,), (1,)), ((), ())),
@@ -472,29 +535,33 @@
 
             @pl.when(jnp.logical_not(live))
             def _():
-                out[u] = tiles[u]
-
-    block = pl.BlockSpec((per_step, p.strip, p.order), lambda i, t: (i, 0, 0))
+                out[u] = tiles[slot]
+
+    loose = [in_vmem(ref) for shift in apart for ref in shift]
     return pl.pallas_call(
         kernel,
-        out_shape=jax.ShapeDtypeStruct(current.shape, jnp.float32),
+        out_shape=jax.ShapeDtypeStruct(held.shape, jnp.float32),
         grid_spec=pltpu.PrefetchScalarGridSpec(
             num_scalar_prefetch=1,
             grid=(p.slots // per_step,),
-            in_specs=[block] + [IN_VMEM] * (2 + p.chunks * p.subs),
-            out_specs=block,
-            scratch_shapes=[pltpu.VMEM((p.strip, p.order), jnp.bfloat16)],
+            in_specs=[IN_VMEM] * (3 + n_together + n_apart),
+            out_specs=pl.BlockSpec((per_step, p.strip, p.order), lambda i, t: (i, 0, 0)),
+            scratch_shapes=[
+                pltpu.VMEM((p.strip, p.order), jnp.bfloat16),
+                pltpu.VMEM((p.subs, p.half_tri) + loose[0].shape, jnp.bfloat16),
+            ],
         ),
         compiler_params=pltpu.CompilerParams(
-            dimension_semantics=("arbitrary",), vmem_limit_bytes=24 * 2**20
+            dimension_semantics=("arbitrary",), vmem_limit_bytes=16 * 2**20
         ),
         name="update",
     )(
         table,
-        in_hbm(current),
+        in_vmem(held),
         in_vmem(inverse[0]),
         in_vmem(inverse[1]),
-        *[in_vmem(ref) for chunk in arrived for ref in chunk],
+        *[in_vmem(ref) for chunk in together for ref in chunk],
+        *loose,
     )
 
 
@@ -522,12 +589,21 @@
         near.append(pick_call(p, table, spread))
     for chunk in range(p.chunks):
         far.append(lax.ppermute(near[chunk], "tri", swap))
-    for chunk in range(p.chunks):
-        built = build_call(p, table, near[chunk], far[chunk], chunk == 0)
+    last = p.chunks - 1
+    for chunk in range(last):
+        built = build_call(p, table, near[chunk], far[chunk], chunk == 0, False)
         whole = exchange(built)
         arrived.append(arrivals(whole))
-    inverse = inverse_call(p, table, arrived[0])
-    return update_call(p, table, current, arrived, inverse)[None]
+    built = build_call(p, table, near[last], far[last], last == 0, True)
+    loose = [built[0]]
+    for n in range(1, p.half_tri):
+        pairs = [(i, i ^ n) for i in range(p.tri)]
+        loose.append(lax.ppermute(built[n], "tri", pairs))
+    pieces = [arrivals(x) for x in loose]
+    apart = [[piece[shift] for piece in pieces] for shift in range(p.subs)]
+    marked = mark_call(p, table)
+    high, low, held = inverse_call(p, marked, arrived[0], current)
+    return update_call(p, table, held, arrived, apart, (high, low))[None]
 
 
 def shards(stored_tiles, cell_owner):

time: 157 us -> 184 us (1.17)
  blocking collectives: 0 us -> 18.9 us
  waiting for transfers between devices: 69 us -> 79.1 us
    all_to_all x0 -> x1, blocking collectives: none -> 18.9 us  [exchange(): lax.all_to_all(x, 'tri', split_axis=0, concat_axis=0, tiled=True, axis_in...]
    all_to_all x4 -> x2, starting transfers between devices: 23.5 us -> 8.34 us  [exchange(): lax.all_to_all(x, 'tri', split_axis=0, concat_axis=0, tiled=True, axis_in...]
    ppermute x0 -> x7, starting transfers between devices: none -> 13.8 us  [planned(): loose.append(lax.ppermute(built[n], 'tri', pairs))]
    all_to_all x4 -> x2, waiting for transfers between devices: 23.9 us -> 31.4 us  [exchange(): lax.all_to_all(x, 'tri', split_axis=0, concat_axis=0, tiled=True, axis_in...]
    ppermute x0 -> x7, waiting for transfers between devices: none -> 3.01 us  [planned(): loose.append(lax.ppermute(built[n], 'tri', pairs))]
    pallas_call x4 -> x5, Pallas kernels: 38.1 us -> 39.5 us  [the longest x1 20.2 us: update_call(): pl.pallas_call(kernel, out_shape=jax.ShapeDtypeStruct(held.shape, jnp.flo...]
    ppermute x2 -> x9, starting transfers between devices: 8.17 us -> 8.72 us  [arrivals(): lax.ppermute(x, 'sub', [((i + shift) % p.subs, i) for i in range(p.subs)])]
  transfers between devices with their start and end apart: 8 -> 20, of which waited for: 5 -> 7; matrix products, arithmetic and copies ran while one was open for 0% -> 0% of each run, Pallas kernels for 14% -> 12%
where the time goes in v3:
time: 184 us; the launch traced here: 183 us
  waiting for transfers between devices  79.1 us (43%)
  Pallas kernels  49.3 us (27%)
  starting transfers between devices  35.3 us (19%)
  blocking collectives  18.9 us (10%)
    ppermute x2, waiting for transfers between devices, planned(): far.append(lax.ppermute(near[chunk], 'tri', swap))  44.6 us
    all_to_all x2, waiting for transfers between devices, exchange(): lax.all_to_all(x, 'tri', split_axis=0, concat_axis=0, tiled=True, axis_in...  31.4 us
    pallas_call x1, Pallas kernels, update_call(): pl.pallas_call(kernel, out_shape=jax.ShapeDtypeStruct(held.shape, jnp.flo...  20.2 us
    all_to_all x1, blocking collectives, exchange(): lax.all_to_all(x, 'tri', split_axis=0, concat_axis=0, tiled=True, axis_in...  18.9 us
    ppermute x7, starting transfers between devices, planned(): loose.append(lax.ppermute(built[n], 'tri', pairs))  13.8 us
    pallas_call x1, Pallas kernels, inverse_call(): pl.pallas_call(kernel, out_shape=(square_shape, square_shape, pltpu.VMEM(...  13.3 us
    ppermute x9, starting transfers between devices, arrivals(): lax.ppermute(x, 'sub', [((i + shift) % p.subs, i) for i in range(p.subs)])  8.72 us
    all_to_all x2, starting transfers between devices, exchange(): lax.all_to_all(x, 'tri', split_axis=0, concat_axis=0, tiled=True, axis_in...  8.34 us
  transfers between devices with their start and end apart: 20, of which 7 were waited for; matrix products, arithmetic and copies ran while one was open for 0% of the time, Pallas kernels for 12%

profile of v3, /device:TPU:1, one launch (start us, length us, event | category | flops | bytes accessed | tf_op | source)
XLA Modules:
  0.0 183.4 jit_solution(3019425873064783371)
XLA Ops:
  0.0 1.5 table.1.t
  1.5 0.0 copy-start
  1.5 0.7 copy-done
  2.2 0.0 copy-start.1
  2.2 3.0 %extract.2 = bf16[8,4,32,512]{3,2,1,0:T(8,128)(2,1)S(1)} custom-call(s32[259]{0:T(512)S(1)} %copy-done, f32[36,256,512]{2,1,0:T(8,128)} %bitcast.2), custom_call_target="tpu_custom_call" | custom-call | tf_op jit(solution)/shard_map/extract/pallas_call | solution.py:289
  5.2 18.9 %all_to_all.15.spread_ref = bf16[8,4,32,512]{3,2,1,0:T(8,128)(2,1)S(1)} all-to-all(bf16[8,4,32,512]{3,2,1,0:T(8,128)(2,1)S(1)} %extract.2), channel_id=1, replica_groups={{0,2,4,6,8,10,12,14},{16,18,20,22,24,26,28,30},{1,3,5,7,9,11,13,15},{17..., dimensions={0} | all-to-all | bytes 2097152 | tf_op jit(solution)/shard_map/all_to_all | solution.py:575
  24.1 0.6 pick.2.near_ref
  24.7 2.4 %collective-permute-start = (bf16[4,4,32,512]{3,2,1,0:T(8,128)(2,1)S(1)}, bf16[4,4,32,512]{3,2,1,0:T(8,128)(2,1)S(1)}, u32[]{:S(2)}, u32[]{:S(2)}) collective-permute-start(bf16[4,4,32,512]{3,2,1,0:T(8,128)(2,1)S(1)} %pick.2.near_ref), channel_id=1, source_target_pairs={{0,16},{2,18},{4,20},{6,22},{8,24},{10,26},{12,28},{14,30},{16,0},... | collective-permute-start | bytes 1572872 | tf_op jit(solution)/shard_map/ppermute | solution.py:591
  27.1 22.9 %collective-permute-done.far_ref = bf16[4,4,32,512]{3,2,1,0:T(8,128)(2,1)S(1)} collective-permute-done((bf16[4,4,32,512]{3,2,1,0:T(8,128)(2,1)S(1)}, bf16[4,4,32,512]{3,2,1,0:T(8,128)(2,1)S(1)}, u32[]{:S(2)}, u32[]{:S(2)}) %collective-permute-start) | collective-permute-done | bytes 524320 | tf_op jit(solution)/shard_map/ppermute | solution.py:591
  49.9 2.2 %build.2 = bf16[8,7,32,512]{3,2,1,0:T(8,128)(2,1)} custom-call(s32[259]{0:T(512)S(1)} %copy-done, bf16[4,4,32,512]{3,2,1,0:T(8,128)(2,1)S(1)} %pick.2.near_ref, bf16[4,4,32,512]{3,2,1,0:T(8,128)(2,1)S(1)} %collective-permute-done.far_ref), custom_call_target="tpu_custom_call" | custom-call | tf_op jit(solution)/shard_map/build/pallas_call | solution.py:360
  52.1 3.6 %all-to-all-start.1 = ((bf16[8,7,32,512]{3,2,1,0:T(8,128)(2,1)}), bf16[8,7,32,512]{3,2,1,0:T(8,128)(2,1)S(1)}, u32[]{:S(2)}, u32[]{:S(2)}) async-start(bf16[8,7,32,512]{3,2,1,0:T(8,128)(2,1)} %build.2), calls=%async_computation.1 | async-start | bytes 3670016 | tf_op jit(solution)/shard_map/all_to_all | solution.py:575
  55.7 0.0 copy-done.1
  55.7 4.1 %extract.3 = bf16[8,4,32,512]{3,2,1,0:T(8,128)(2,1)} custom-call(s32[259]{0:T(512)S(1)} %copy-done.1, f32[36,256,512]{2,1,0:T(8,128)} %bitcast.3), custom_call_target="tpu_custom_call" | custom-call | tf_op jit(solution)/shard_map/extract/pallas_call | solution.py:289
  59.9 18.5 %all-to-all-done.1.refs_0_ = bf16[8,7,32,512]{3,2,1,0:T(8,128)(2,1)S(1)} async-done(((bf16[8,7,32,512]{3,2,1,0:T(8,128)(2,1)}), bf16[8,7,32,512]{3,2,1,0:T(8,128)(2,1)S(1)}, u32[]{:S(2)}, u32[]{:S(2)}) %all-to-all-start.1) | async-done | bytes 1835040 | tf_op jit(solution)/shard_map/all_to_all | solution.py:575
  78.4 4.7 %all-to-all-start.2 = ((bf16[8,4,32,512]{3,2,1,0:T(8,128)(2,1)}), bf16[8,4,32,512]{3,2,1,0:T(8,128)(2,1)S(1)}, u32[]{:S(2)}, u32[]{:S(2)}) async-start(bf16[8,4,32,512]{3,2,1,0:T(8,128)(2,1)} %extract.3), calls=%async_computation.2 | async-start | bytes 2097152 | tf_op jit(solution)/shard_map/all_to_all | solution.py:575
  83.2 0.8 collective-permute-start.1
  84.0 12.9 %all-to-all-done.2.spread_ref = bf16[8,4,32,512]{3,2,1,0:T(8,128)(2,1)S(1)} async-done(((bf16[8,4,32,512]{3,2,1,0:T(8,128)(2,1)}), bf16[8,4,32,512]{3,2,1,0:T(8,128)(2,1)S(1)}, u32[]{:S(2)}, u32[]{:S(2)}) %all-to-all-start.2) | async-done | bytes 1048608 | tf_op jit(solution)/shard_map/all_to_all | solution.py:575
  96.8 0.6 pick.3.near_ref
  97.4 2.1 %collective-permute-start.2 = (bf16[4,4,32,512]{3,2,1,0:T(8,128)(2,1)S(1)}, bf16[4,4,32,512]{3,2,1,0:T(8,128)(2,1)S(1)}, u32[]{:S(2)}, u32[]{:S(2)}) collective-permute-start(bf16[4,4,32,512]{3,2,1,0:T(8,128)(2,1)S(1)} %pick.3.near_ref), channel_id=1, source_target_pairs={{0,16},{2,18},{4,20},{6,22},{8,24},{10,26},{12,28},{14,30},{16,0},... | collective-permute-start | bytes 1572872 | tf_op jit(solution)/shard_map/ppermute | solution.py:591
  99.5 21.8 %collective-permute-done.2.far_ref = bf16[4,4,32,512]{3,2,1,0:T(8,128)(2,1)S(1)} collective-permute-done((bf16[4,4,32,512]{3,2,1,0:T(8,128)(2,1)S(1)}, bf16[4,4,32,512]{3,2,1,0:T(8,128)(2,1)S(1)}, u32[]{:S(2)}, u32[]{:S(2)}) %collective-permute-start.2) | collective-permute-done | bytes 524320 | tf_op jit(solution)/shard_map/ppermute | solution.py:591
  121.3 0.9 build.3
  122.2 2.9 %collective-permute-start.3 = (bf16[6,32,512]{2,1,0:T(8,128)(2,1)S(1)}, bf16[6,32,512]{2,1,0:T(8,128)(2,1)S(1)}, u32[]{:S(2)}, u32[]{:S(2)}) collective-permute-start(bf16[6,32,512]{2,1,0:T(8,128)(2,1)S(1)} %get-tuple-element.20), channel_id=1, source_target_pairs={{0,2},{2,0},{4,6},{6,4},{8,10},{10,8},{12,14},{14,12},{16,18},{18,... | collective-permute-start | bytes 589832 | tf_op jit(solution)/shard_map/ppermute | solution.py:601
  125.2 0.0 collective-permute-start.4
  125.2 1.3 collective-permute-start.5
  126.4 0.9 collective-permute-start.6
  127.4 1.5 collective-permute-done.3.refs_3_
  128.9 2.9 %collective-permute-start.7 = (bf16[6,32,512]{2,1,0:T(8,128)(2,1)S(1)}, bf16[6,32,512]{2,1,0:T(8,128)(2,1)S(1)}, u32[]{:S(2)}, u32[]{:S(2)}) collective-permute-start(bf16[6,32,512]{2,1,0:T(8,128)(2,1)S(1)} %get-tuple-element.24), channel_id=1, source_target_pairs={{0,10},{2,8},{4,14},{6,12},{8,2},{10,0},{12,6},{14,4},{16,26},{18,... | collective-permute-start | bytes 589832 | tf_op jit(solution)/shard_map/ppermute | solution.py:601
  131.8 0.5 collective-permute-done.4.refs_4_
  132.3 0.0 collective-permute-start.8
  132.3 1.0 collective-permute-done.5.refs_5_
  133.3 5.7 %collective-permute-start.9 = (bf16[6,32,512]{2,1,0:T(8,128)(2,1)S(1)}, bf16[6,32,512]{2,1,0:T(8,128)(2,1)S(1)}, u32[]{:S(2)}, u32[]{:S(2)}) collective-permute-start(bf16[6,32,512]{2,1,0:T(8,128)(2,1)S(1)} %get-tuple-element.26), channel_id=1, source_target_pairs={{0,14},{2,12},{4,10},{6,8},{8,6},{10,4},{12,2},{14,0},{16,30},{18,... | collective-permute-start | bytes 589832 | tf_op jit(solution)/shard_map/ppermute | solution.py:601
  139.0 0.0 collective-permute-done.6.refs_6_
  139.0 2.6 %collective-permute-start.10 = (bf16[6,32,512]{2,1,0:T(8,128)(2,1)S(1)}, bf16[6,32,512]{2,1,0:T(8,128)(2,1)S(1)}, u32[]{:S(2)}, u32[]{:S(2)}) collective-permute-start(bf16[6,32,512]{2,1,0:T(8,128)(2,1)S(1)} %get-tuple-element.19.refs_2_), channel_id=1, source_target_pairs={{1,0},{0,1},{3,2},{2,3},{5,4},{4,5},{7,6},{6,7},{9,8},{8,9},{11,10... | collective-permute-start | bytes 589832 | tf_op jit(solution)/shard_map/ppermute | solution.py:581
  141.6 0.0 collective-permute-done.7.refs_7_
  141.6 0.1 collective-permute-start.11
  141.7 0.0 collective-permute-done.8.refs_8_
  141.7 4.1 %collective-permute-start.12 = (bf16[6,32,512]{2,1,0:T(8,128)(2,1)S(1)}, bf16[6,32,512]{2,1,0:T(8,128)(2,1)S(1)}, u32[]{:S(2)}, u32[]{:S(2)}) collective-permute-start(bf16[6,32,512]{2,1,0:T(8,128)(2,1)S(1)} %collective-permute-done.4.refs_4_), channel_id=1, source_target_pairs={{1,0},{0,1},{3,2},{2,3},{5,4},{4,5},{7,6},{6,7},{9,8},{8,9},{11,10... | collective-permute-start | bytes 589832 | tf_op jit(solution)/shard_map/ppermute | solution.py:581
  145.8 2.8 %mark.1.t = s32[259]{0:T(512)S(1)} custom-call(s32[259]{0:T(512)S(1)} %copy-done.1), custom_call_target="tpu_custom_call" | custom-call | tf_op jit(solution)/shard_map/mark/pallas_call | solution.py:275
  148.6 0.0 collective-permute-done.9.refs_9_
  148.6 0.1 collective-permute-start.13
  148.7 0.0 collective-permute-done.10.refs_10_
  148.7 0.5 collective-permute-start.14
  149.2 0.0 collective-permute-done.11.refs_11_
  149.2 0.1 collective-permute-start.15
  149.3 0.0 collective-permute-done.12.refs_12_
  149.3 0.4 collective-permute-start.16
  149.7 0.0 collective-permute-done.1.refs_1_
  149.7 0.1 collective-permute-start.17
  149.8 13.3 %inverse.1 = (bf16[512,512]{1,0:T(8,128)(2,1)S(1)}, bf16[512,512]{1,0:T(8,128)(2,1)S(1)}, f32[36,256,512]{2,1,0:T(8,128)S(1)}) custom-call(s32[259]{0:T(512)S(1)} %mark.1.t, bf16[8,7,32,512]{3,2,1,0:T(8,128)(2,1)S(1)} %all-to-all-done.1.refs_0_, bf16[8,7,32,512]{3,2,1,0:T(8,128)(2,1)} %collective-permute-done.1.refs_1_, f32[36,256,512]{2,1,0:T(8,128)} %bitcast.4), custom_call_target="tpu_custom_call" | custom-call | flops 16106127360 | bytes 1048576 | tf_op jit(solution)/shard_map/inverse/pallas_call | solution.py:457
  163.1 0.0 collective-permute-done.13.refs_13_
  163.2 0.0 collective-permute-done.14.refs_14_
  163.2 0.0 collective-permute-done.15.refs_15_
  163.2 0.0 collective-permute-done.16.refs_16_
  163.2 0.0 collective-permute-done.17.refs_17_
  163.2 20.2 %update.1 = f32[36,256,512]{2,1,0:T(8,128)} custom-call(s32[259]{0:T(512)S(1)} %copy-done.1, f32[36,256,512]{2,1,0:T(8,128)S(1)} %get-tuple-element.16.tiles, bf16[512,512]{1,0:T(8,128)(2,1)S(1)} %get-tuple-element.17.high, bf16[512,512]{1,0:T(8,128)(2,1)S(1)} %get-tuple-element.18.low, bf16[8,7,32,512]{3,2,1,0:T(8,128)(2,1)S(1)} %all-to-all-done.1.refs_0_, ...), custom_call_target="tpu_custom_call" | custom-call | tf_op jit(solution)/shard_map/update/pallas_call | solution.py:541
Async XLA Ops:
  1.5 0.7 copy-start
  2.2 53.5 %copy-start.1 = (s32[259]{0:T(512)S(1)}, s32[259]{0:T(512)}, u32[]{:S(2)}) copy-start(s32[259]{0:T(512)} %table.1.t) | copy-start | bytes 3112
  24.7 25.2 %collective-permute-start = (bf16[4,4,32,512]{3,2,1,0:T(8,128)(2,1)S(1)}, bf16[4,4,32,512]{3,2,1,0:T(8,128)(2,1)S(1)}, u32[]{:S(2)}, u32[]{:S(2)}) collective-permute-start(bf16[4,4,32,512]{3,2,1,0:T(8,128)(2,1)S(1)} %pick.2.near_ref), channel_id=1, source_target_pairs={{0,16},{2,18},{4,20},{6,22},{8,24},{10,26},{12,28},{14,30},{16,0},... | collective-permute-start | bytes 1572872 | tf_op jit(solution)/shard_map/ppermute | solution.py:591
  52.1 26.3 %all-to-all-start.1 = ((bf16[8,7,32,512]{3,2,1,0:T(8,128)(2,1)}), bf16[8,7,32,512]{3,2,1,0:T(8,128)(2,1)S(1)}, u32[]{:S(2)}, u32[]{:S(2)}) async-start(bf16[8,7,32,512]{3,2,1,0:T(8,128)(2,1)} %build.2), calls=%async_computation.1 | async-start | bytes 3670016 | tf_op jit(solution)/shard_map/all_to_all | solution.py:575
  78.4 18.4 %all-to-all-start.2 = ((bf16[8,4,32,512]{3,2,1,0:T(8,128)(2,1)}), bf16[8,4,32,512]{3,2,1,0:T(8,128)(2,1)S(1)}, u32[]{:S(2)}, u32[]{:S(2)}) async-start(bf16[8,4,32,512]{3,2,1,0:T(8,128)(2,1)} %extract.3), calls=%async_computation.2 | async-start | bytes 2097152 | tf_op jit(solution)/shard_map/all_to_all | solution.py:575
  83.2 66.6 %collective-permute-start.1 = (bf16[8,7,32,512]{3,2,1,0:T(8,128)(2,1)S(1)}, bf16[8,7,32,512]{3,2,1,0:T(8,128)(2,1)}, u32[]{:S(2)}, u32[]{:S(2)}) collective-permute-start(bf16[8,7,32,512]{3,2,1,0:T(8,128)(2,1)S(1)} %all-to-all-done.1.refs_0_), channel_id=1, source_target_pairs={{1,0},{0,1},{3,2},{2,3},{5,4},{4,5},{7,6},{6,7},{9,8},{8,9},{11,10... | collective-permute-start | bytes 5505032 | tf_op jit(solution)/shard_map/ppermute | solution.py:581
  97.4 23.9 %collective-permute-start.2 = (bf16[4,4,32,512]{3,2,1,0:T(8,128)(2,1)S(1)}, bf16[4,4,32,512]{3,2,1,0:T(8,128)(2,1)S(1)}, u32[]{:S(2)}, u32[]{:S(2)}) collective-permute-start(bf16[4,4,32,512]{3,2,1,0:T(8,128)(2,1)S(1)} %pick.3.near_ref), channel_id=1, source_target_pairs={{0,16},{2,18},{4,20},{6,22},{8,24},{10,26},{12,28},{14,30},{16,0},... | collective-permute-start | bytes 1572872 | tf_op jit(solution)/shard_map/ppermute | solution.py:591
  122.2 6.7 %collective-permute-start.3 = (bf16[6,32,512]{2,1,0:T(8,128)(2,1)S(1)}, bf16[6,32,512]{2,1,0:T(8,128)(2,1)S(1)}, u32[]{:S(2)}, u32[]{:S(2)}) collective-permute-start(bf16[6,32,512]{2,1,0:T(8,128)(2,1)S(1)} %get-tuple-element.20), channel_id=1, source_target_pairs={{0,2},{2,0},{4,6},{6,4},{8,10},{10,8},{12,14},{14,12},{16,18},{18,... | collective-permute-start | bytes 589832 | tf_op jit(solution)/shard_map/ppermute | solution.py:601
  125.2 7.2 %collective-permute-start.4 = (bf16[6,32,512]{2,1,0:T(8,128)(2,1)S(1)}, bf16[6,32,512]{2,1,0:T(8,128)(2,1)S(1)}, u32[]{:S(2)}, u32[]{:S(2)}) collective-permute-start(bf16[6,32,512]{2,1,0:T(8,128)(2,1)S(1)} %get-tuple-element.21), channel_id=1, source_target_pairs={{0,4},{2,6},{4,0},{6,2},{8,12},{10,14},{12,8},{14,10},{16,20},{18,... | collective-permute-start | bytes 589832 | tf_op jit(solution)/shard_map/ppermute | solution.py:601
  125.2 8.1 %collective-permute-start.5 = (bf16[6,32,512]{2,1,0:T(8,128)(2,1)S(1)}, bf16[6,32,512]{2,1,0:T(8,128)(2,1)S(1)}, u32[]{:S(2)}, u32[]{:S(2)}) collective-permute-start(bf16[6,32,512]{2,1,0:T(8,128)(2,1)S(1)} %get-tuple-element.22), channel_id=1, source_target_pairs={{0,6},{2,4},{4,2},{6,0},{8,14},{10,12},{12,10},{14,8},{16,22},{18,... | collective-permute-start | bytes 589832 | tf_op jit(solution)/shard_map/ppermute | solution.py:601
  126.4 12.6 %collective-permute-start.6 = (bf16[6,32,512]{2,1,0:T(8,128)(2,1)S(1)}, bf16[6,32,512]{2,1,0:T(8,128)(2,1)S(1)}, u32[]{:S(2)}, u32[]{:S(2)}) collective-permute-start(bf16[6,32,512]{2,1,0:T(8,128)(2,1)S(1)} %get-tuple-element.23), channel_id=1, source_target_pairs={{0,8},{2,10},{4,12},{6,14},{8,0},{10,2},{12,4},{14,6},{16,24},{18,... | collective-permute-start | bytes 589832 | tf_op jit(solution)/shard_map/ppermute | solution.py:601
  128.9 12.7 %collective-permute-start.7 = (bf16[6,32,512]{2,1,0:T(8,128)(2,1)S(1)}, bf16[6,32,512]{2,1,0:T(8,128)(2,1)S(1)}, u32[]{:S(2)}, u32[]{:S(2)}) collective-permute-start(bf16[6,32,512]{2,1,0:T(8,128)(2,1)S(1)} %get-tuple-element.24), channel_id=1, source_target_pairs={{0,10},{2,8},{4,14},{6,12},{8,2},{10,0},{12,6},{14,4},{16,26},{18,... | collective-permute-start | bytes 589832 | tf_op jit(solution)/shard_map/ppermute | solution.py:601
  132.3 9.4 %collective-permute-start.8 = (bf16[6,32,512]{2,1,0:T(8,128)(2,1)S(1)}, bf16[6,32,512]{2,1,0:T(8,128)(2,1)S(1)}, u32[]{:S(2)}, u32[]{:S(2)}) collective-permute-start(bf16[6,32,512]{2,1,0:T(8,128)(2,1)S(1)} %get-tuple-element.25), channel_id=1, source_target_pairs={{0,12},{2,14},{4,8},{6,10},{8,4},{10,6},{12,0},{14,2},{16,28},{18,... | collective-permute-start | bytes 589832 | tf_op jit(solution)/shard_map/ppermute | solution.py:601
  133.3 15.3 %collective-permute-start.9 = (bf16[6,32,512]{2,1,0:T(8,128)(2,1)S(1)}, bf16[6,32,512]{2,1,0:T(8,128)(2,1)S(1)}, u32[]{:S(2)}, u32[]{:S(2)}) collective-permute-start(bf16[6,32,512]{2,1,0:T(8,128)(2,1)S(1)} %get-tuple-element.26), channel_id=1, source_target_pairs={{0,14},{2,12},{4,10},{6,8},{8,6},{10,4},{12,2},{14,0},{16,30},{18,... | collective-permute-start | bytes 589832 | tf_op jit(solution)/shard_map/ppermute | solution.py:601
  139.0 9.7 %collective-permute-start.10 = (bf16[6,32,512]{2,1,0:T(8,128)(2,1)S(1)}, bf16[6,32,512]{2,1,0:T(8,128)(2,1)S(1)}, u32[]{:S(2)}, u32[]{:S(2)}) collective-permute-start(bf16[6,32,512]{2,1,0:T(8,128)(2,1)S(1)} %get-tuple-element.19.refs_2_), channel_id=1, source_target_pairs={{1,0},{0,1},{3,2},{2,3},{5,4},{4,5},{7,6},{6,7},{9,8},{8,9},{11,10... | collective-permute-start | bytes 589832 | tf_op jit(solution)/shard_map/ppermute | solution.py:581
  141.6 7.6 %collective-permute-start.11 = (bf16[6,32,512]{2,1,0:T(8,128)(2,1)S(1)}, bf16[6,32,512]{2,1,0:T(8,128)(2,1)S(1)}, u32[]{:S(2)}, u32[]{:S(2)}) collective-permute-start(bf16[6,32,512]{2,1,0:T(8,128)(2,1)S(1)} %collective-permute-done.3.refs_3_), channel_id=1, source_target_pairs={{1,0},{0,1},{3,2},{2,3},{5,4},{4,5},{7,6},{6,7},{9,8},{8,9},{11,10... | collective-permute-start | bytes 589832 | tf_op jit(solution)/shard_map/ppermute | solution.py:581
  141.7 7.6 %collective-permute-start.12 = (bf16[6,32,512]{2,1,0:T(8,128)(2,1)S(1)}, bf16[6,32,512]{2,1,0:T(8,128)(2,1)S(1)}, u32[]{:S(2)}, u32[]{:S(2)}) collective-permute-start(bf16[6,32,512]{2,1,0:T(8,128)(2,1)S(1)} %collective-permute-done.4.refs_4_), channel_id=1, source_target_pairs={{1,0},{0,1},{3,2},{2,3},{5,4},{4,5},{7,6},{6,7},{9,8},{8,9},{11,10... | collective-permute-start | bytes 589832 | tf_op jit(solution)/shard_map/ppermute | solution.py:581
  148.6 14.5 %collective-permute-start.13 = (bf16[6,32,512]{2,1,0:T(8,128)(2,1)S(1)}, bf16[6,32,512]{2,1,0:T(8,128)(2,1)S(1)}, u32[]{:S(2)}, u32[]{:S(2)}) collective-permute-start(bf16[6,32,512]{2,1,0:T(8,128)(2,1)S(1)} %collective-permute-done.5.refs_5_), channel_id=1, source_target_pairs={{1,0},{0,1},{3,2},{2,3},{5,4},{4,5},{7,6},{6,7},{9,8},{8,9},{11,10... | collective-permute-start | bytes 589832 | tf_op jit(solution)/shard_map/ppermute | solution.py:581
  148.7 14.4 %collective-permute-start.14 = (bf16[6,32,512]{2,1,0:T(8,128)(2,1)S(1)}, bf16[6,32,512]{2,1,0:T(8,128)(2,1)S(1)}, u32[]{:S(2)}, u32[]{:S(2)}) collective-permute-start(bf16[6,32,512]{2,1,0:T(8,128)(2,1)S(1)} %collective-permute-done.6.refs_6_), channel_id=1, source_target_pairs={{1,0},{0,1},{3,2},{2,3},{5,4},{4,5},{7,6},{6,7},{9,8},{8,9},{11,10... | collective-permute-start | bytes 589832 | tf_op jit(solution)/shard_map/ppermute | solution.py:581
  149.2 13.9 %collective-permute-start.15 = (bf16[6,32,512]{2,1,0:T(8,128)(2,1)S(1)}, bf16[6,32,512]{2,1,0:T(8,128)(2,1)S(1)}, u32[]{:S(2)}, u32[]{:S(2)}) collective-permute-start(bf16[6,32,512]{2,1,0:T(8,128)(2,1)S(1)} %collective-permute-done.7.refs_7_), channel_id=1, source_target_pairs={{1,0},{0,1},{3,2},{2,3},{5,4},{4,5},{7,6},{6,7},{9,8},{8,9},{11,10... | collective-permute-start | bytes 589832 | tf_op jit(solution)/shard_map/ppermute | solution.py:581
  149.3 13.9 %collective-permute-start.16 = (bf16[6,32,512]{2,1,0:T(8,128)(2,1)S(1)}, bf16[6,32,512]{2,1,0:T(8,128)(2,1)S(1)}, u32[]{:S(2)}, u32[]{:S(2)}) collective-permute-start(bf16[6,32,512]{2,1,0:T(8,128)(2,1)S(1)} %collective-permute-done.8.refs_8_), channel_id=1, source_target_pairs={{1,0},{0,1},{3,2},{2,3},{5,4},{4,5},{7,6},{6,7},{9,8},{8,9},{11,10... | collective-permute-start | bytes 589832 | tf_op jit(solution)/shard_map/ppermute | solution.py:581
  149.7 13.4 %collective-permute-start.17 = (bf16[6,32,512]{2,1,0:T(8,128)(2,1)S(1)}, bf16[6,32,512]{2,1,0:T(8,128)(2,1)S(1)}, u32[]{:S(2)}, u32[]{:S(2)}) collective-permute-start(bf16[6,32,512]{2,1,0:T(8,128)(2,1)S(1)} %collective-permute-done.9.refs_9_), channel_id=1, source_target_pairs={{1,0},{0,1},{3,2},{2,3},{5,4},{4,5},{7,6},{6,7},{9,8},{8,9},{11,10... | collective-permute-start | bytes 589832 | tf_op jit(solution)/shard_map/ppermute | solution.py:581

commit v4 on v3

--- a/solution.py
+++ b/solution.py
@@ -142,8 +142,7 @@
         self.o_sub = 0
         self.o_diag = 1
         self.o_me = 2
-        self.o_slot = 3
-        self.o_src = self.o_slot + self.per_group
+        self.o_src = 8
         self.o_here = self.o_src + self.groups
         self.o_rg = self.o_here + self.groups
         self.o_cg = self.o_rg + self.half_tri
@@ -195,12 +194,6 @@
         out[p.o_sub] = lax.axis_index("sub")
         out[p.o_me] = position - my_half * p.half_tri
         out[p.o_diag] = jnp.where(diag, 1, 0)
-        for chunk in range(p.chunks):
-            for place in range(p.in_chunk):
-                member = p.tile_of(chunk, place)
-                out[p.o_slot + chunk * p.in_chunk + place] = jnp.where(
-                    down > 0, member * p.half_group, member * (member + 1) // 2
-                )
         for group in range(p.groups):
             holder = owner[group * p.groups]
             half = holder // p.half_tri
@@ -265,16 +258,13 @@
 
 def mark_call(p, table):
     def kernel(t, out):
-        def copy(i, _):
+        for i in (p.o_sub, p.o_diag, p.o_me):
             out[i] = t[i]
-            return 0
-
-        lax.fori_loop(0, p.size, copy, 0)
 
     smem = pl.BlockSpec(memory_space=pltpu.SMEM)
     return pl.pallas_call(
         kernel,
-        out_shape=jax.ShapeDtypeStruct((p.size,), jnp.int32),
+        out_shape=jax.ShapeDtypeStruct((p.o_src,), jnp.int32),
         in_specs=[smem],
         out_specs=smem,
         compiler_params=limit(1),
@@ -282,29 +272,42 @@
     )(table)
 
 
-def extract_call(p, table, current, chunk):
-    def kernel(t, tile, out):
-        out[...] = tile[...].reshape(p.half_tri, 1, p.piece, p.order).astype(jnp.bfloat16)
+def extract_call(p, cell_owner, current, chunk):
+    def kernel(owner, tiles, out, wide, sems):
+        position = lax.axis_index("tri")
+        cell = jnp.int32(0)
+        for n in range(1, p.tri):
+            cell = jnp.where(owner[n] == position, n, cell)
+        down = cell // p.groups
+        copies = []
+        for place in range(p.in_chunk):
+            member = p.tile_of(chunk, place)
+            slot = jnp.where(down > 0, member * p.half_group, member * (member + 1) // 2)
+            copies.append(
+                pltpu.make_async_copy(tiles.at[slot], wide.at[place], sems.at[place])
+            )
+        for copy in copies:
+            copy.start()
+        for place, copy in enumerate(copies):
+            copy.wait()
+            rounded = wide[place].astype(jnp.bfloat16)
+            out[:, place] = rounded.reshape(p.half_tri, p.piece, p.order)
 
     return pl.pallas_call(
         kernel,
-        out_shape=jax.ShapeDtypeStruct((p.half_tri, p.in_chunk, p.piece, p.order), jnp.bfloat16),
-        grid_spec=pltpu.PrefetchScalarGridSpec(
-            num_scalar_prefetch=1,
-            grid=(p.in_chunk,),
-            in_specs=[
-                pl.BlockSpec(
-                    (1, p.strip, p.order),
-                    lambda i, t: (t[p.o_slot + chunk * p.in_chunk + i], 0, 0),
-                )
-            ],
-            out_specs=pl.BlockSpec(
-                (p.half_tri, 1, p.piece, p.order), lambda i, t: (0, i, 0, 0)
-            ),
-        ),
+        out_shape=pltpu.VMEM((p.half_tri, p.in_chunk, p.piece, p.order), jnp.bfloat16),
+        in_specs=[
+            pl.BlockSpec(memory_space=pltpu.SMEM),
+            pl.BlockSpec(memory_space=pltpu.HBM),
+        ],
+        out_specs=IN_VMEM,
+        scratch_shapes=[
+            pltpu.VMEM((p.in_chunk, p.strip, p.order), jnp.float32),
+            pltpu.SemaphoreType.DMA((p.in_chunk,)),
+        ],
         compiler_params=limit(8),
         name="extract",
-    )(table, in_hbm(current))
+    )(cell_owner, in_hbm(current))
 
 
 def pick_call(p, table, spread):
@@ -380,7 +383,7 @@
 
     def kernel(t, *refs):
         sources = refs[: p.subs]
-        tiles, high, low, held, pivot, x_wide, x_half, e_ref, sems = refs[p.subs :]
+        tiles, high, held, pivot, x_wide, x_half, e_ref, sems = refs[p.subs :]
         copies = [
             pltpu.make_async_copy(
                 tiles.at[pl.ds(n * each, each)], held.at[pl.ds(n * each, each)], sems.at[n]
@@ -404,18 +407,21 @@
             c = lax.broadcasted_iota(jnp.int32, (order, order), 1)
             return jnp.where(r == c, 1.0, 0.0)
 
-        square = dot(pivot[...], pivot[...])
-        bound = jnp.max(jnp.sum(jnp.abs(square), axis=1))
-        start = pivot[...].astype(jnp.float32) * (-1.0 / bound)
-        x_wide[...] = start
-        x_half[...] = start.astype(jnp.bfloat16)
+        square = -dot(pivot[...], pivot[...])
+        factor = 1.9 / jnp.max(jnp.sum(jnp.abs(square), axis=1))
+        residual = eye() - factor * square
+        e_ref[...] = residual.astype(jnp.bfloat16)
+        wide = -factor * (pivot[...].astype(jnp.float32) + dot(pivot[...], e_ref[...]))
+        x_wide[...] = wide
+        x_half[...] = wide.astype(jnp.bfloat16)
 
         def coarse_on(carry):
-            step, error, noise = carry
-            return (step < 40) & (error > 0.01) & (noise < 0.1)
+            step, error, before, noise = carry
+            stuck = (before < 1.0) & (error > 0.5 * before)
+            return (step < 60) & (error > 3e-3) & (noise < 0.1) & jnp.logical_not(stuck)
 
         def coarse(carry):
-            step, _, _ = carry
+            step, before, _, _ = carry
             x = x_half[...]
             residual = eye() - dot(pivot[...], x)
             e_ref[...] = residual.astype(jnp.bfloat16)
@@ -423,10 +429,13 @@
             new = x.astype(jnp.float32) + dot(x, e_ref[...])
             x_wide[...] = new
             x_half[...] = new.astype(jnp.bfloat16)
-            noise = jnp.sum(new * new) * bound * 2.0**-18
-            return step + 1, error, noise
-
-        lax.while_loop(coarse_on, coarse, (jnp.int32(0), jnp.float32(1e30), jnp.float32(0.0)))
+            noise = jnp.sum(new * new) / factor * 2.0**-18
+            return step + 1, error, before, noise
+
+        big = jnp.float32(1e30)
+        _, reached, _, _ = lax.while_loop(
+            coarse_on, coarse, (jnp.int32(0), big, big, jnp.float32(0.0))
+        )
 
         def fine_on(carry):
             step, error, before = carry
@@ -445,23 +454,23 @@
             x_wide[...] = x + (dot(x_high, e_high) + (dot(x_high, e_low) + dot(x_low, e_high)))
             return step + 1, error, before
 
-        lax.while_loop(fine_on, fine, (jnp.int32(0), jnp.float32(1e30), jnp.float32(1e30)))
-        x = x_wide[...]
-        rounded = x.astype(jnp.bfloat16)
-        high[...] = rounded
-        low[...] = (x - rounded.astype(jnp.float32)).astype(jnp.bfloat16)
+        @pl.when(jnp.logical_not(reached <= 3e-3))
+        def _():
+            lax.while_loop(fine_on, fine, (jnp.int32(0), big, big))
+
+        high[...] = x_wide[...].astype(jnp.bfloat16)
         for copy in copies:
             copy.wait()
 
     square_shape = pltpu.VMEM((order, order), jnp.bfloat16)
     return pl.pallas_call(
         kernel,
-        out_shape=(square_shape, square_shape, pltpu.VMEM(current.shape, jnp.float32)),
+        out_shape=(square_shape, pltpu.VMEM(current.shape, jnp.float32)),
         grid_spec=pltpu.PrefetchScalarGridSpec(
             num_scalar_prefetch=1,
             grid=(),
             in_specs=[IN_VMEM] * p.subs + [pl.BlockSpec(memory_space=pltpu.HBM)],
-            out_specs=(IN_VMEM, IN_VMEM, IN_VMEM),
+            out_specs=(IN_VMEM, IN_VMEM),
             scratch_shapes=[
                 pltpu.VMEM((order, order), jnp.bfloat16),
                 pltpu.VMEM((order, order), jnp.float32),
@@ -484,7 +493,7 @@
     n_together = last * p.subs
     n_apart = p.subs * p.half_tri
 
-    def kernel(t, tiles, high, low, *refs):
+    def kernel(t, tiles, high, *refs):
         sources = [refs[k * p.subs : (k + 1) * p.subs] for k in range(last)]
         loose = refs[n_together : n_together + n_apart]
         out, scaled, packed = refs[n_together + n_apart :]
@@ -508,7 +517,7 @@
                     dims = (((1,), (0,)), ((), ()))
                     product = lax.dot_general(
                         strip, high[...], dims, preferred_element_type=jnp.float32
-                    ) + lax.dot_general(strip, low[...], dims, preferred_element_type=jnp.float32)
+                    )
                     scaled[...] = product.astype(jnp.bfloat16)
 
             live = t[p.o_live + slot] == 1
@@ -544,7 +553,7 @@
         grid_spec=pltpu.PrefetchScalarGridSpec(
             num_scalar_prefetch=1,
             grid=(p.slots // per_step,),
-            in_specs=[IN_VMEM] * (3 + n_together + n_apart),
+            in_specs=[IN_VMEM] * (2 + n_together + n_apart),
             out_specs=pl.BlockSpec((per_step, p.strip, p.order), lambda i, t: (i, 0, 0)),
             scratch_shapes=[
                 pltpu.VMEM((p.strip, p.order), jnp.bfloat16),
@@ -558,8 +567,7 @@
     )(
         table,
         in_vmem(held),
-        in_vmem(inverse[0]),
-        in_vmem(inverse[1]),
+        in_vmem(inverse),
         *[in_vmem(ref) for chunk in together for ref in chunk],
         *loose,
     )
@@ -584,7 +592,7 @@
 
     near, far, arrived = [], [], []
     for chunk in range(p.chunks):
-        pieces = extract_call(p, table, current, chunk)
+        pieces = extract_call(p, cell_owner, current, chunk)
         spread = exchange(pieces)
         near.append(pick_call(p, table, spread))
     for chunk in range(p.chunks):
@@ -602,8 +610,8 @@
     pieces = [arrivals(x) for x in loose]
     apart = [[piece[shift] for piece in pieces] for shift in range(p.subs)]
     marked = mark_call(p, table)
-    high, low, held = inverse_call(p, marked, arrived[0], current)
-    return update_call(p, table, held, arrived, apart, (high, low))[None]
+    inverse, held = inverse_call(p, marked, arrived[0], current)
+    return update_call(p, table, held, arrived, apart, inverse)[None]
 
 
 def shards(stored_tiles, cell_owner):

time: 184 us -> 179 us (0.973)
  blocking collectives: 18.9 us -> 0 us
  waiting for transfers between devices: 79.1 us -> 92.5 us
  Pallas kernels: 49.3 us -> 42.1 us
  starting transfers between devices: 35.3 us -> 42.4 us
    all_to_all x1 -> x0, blocking collectives: 18.9 us -> none  [exchange(): lax.all_to_all(x, 'tri', split_axis=0, concat_axis=0, tiled=True, axis_in...]
    all_to_all x2 -> x3, waiting for transfers between devices: 31.4 us -> 44.9 us  [exchange(): lax.all_to_all(x, 'tri', split_axis=0, concat_axis=0, tiled=True, axis_in...]
    all_to_all x2 -> x3, starting transfers between devices: 8.34 us -> 14.8 us  [exchange(): lax.all_to_all(x, 'tri', split_axis=0, concat_axis=0, tiled=True, axis_in...]
    pallas_call x4, Pallas kernels: 23.2 us -> 17.2 us  [the longest x1 9.87 us: inverse_call(): pl.pallas_call(kernel, out_shape=(square_shape, pltpu.VMEM(current.shape,...]
  transfers between devices with their start and end apart: 20 -> 21, of which waited for: 7 -> 7; matrix products, arithmetic and copies ran while one was open for 0% -> 0% of each run, Pallas kernels for 12% -> 10%
where the time goes in v4:
time: 179 us; the launch traced here: 178 us
  waiting for transfers between devices  92.5 us (52%)
  starting transfers between devices  42.4 us (24%)
  Pallas kernels  42.1 us (24%)
    all_to_all x3, waiting for transfers between devices, exchange(): lax.all_to_all(x, 'tri', split_axis=0, concat_axis=0, tiled=True, axis_in...  44.9 us
    ppermute x2, waiting for transfers between devices, planned(): far.append(lax.ppermute(near[chunk], 'tri', swap))  43.2 us
    pallas_call x1, Pallas kernels, update_call(): pl.pallas_call(kernel, out_shape=jax.ShapeDtypeStruct(held.shape, jnp.flo...  19 us
    all_to_all x3, starting transfers between devices, exchange(): lax.all_to_all(x, 'tri', split_axis=0, concat_axis=0, tiled=True, axis_in...  14.8 us
    ppermute x7, starting transfers between devices, planned(): loose.append(lax.ppermute(built[n], 'tri', pairs))  12.8 us
    pallas_call x1, Pallas kernels, inverse_call(): pl.pallas_call(kernel, out_shape=(square_shape, pltpu.VMEM(current.shape,...  9.87 us
    ppermute x9, starting transfers between devices, arrivals(): lax.ppermute(x, 'sub', [((i + shift) % p.subs, i) for i in range(p.subs)])  9.29 us
    pallas_call x2, Pallas kernels, extract_call(): pl.pallas_call(kernel, out_shape=pltpu.VMEM((p.half_tri, p.in_chunk, p.pi...  6.2 us
  transfers between devices with their start and end apart: 21, of which 7 were waited for; matrix products, arithmetic and copies ran while one was open for 0% of the time, Pallas kernels for 10%

profile of v4, /device:TPU:1, one launch (start us, length us, event | category | flops | bytes accessed | tf_op | source)
XLA Modules:
  0.0 178.5 jit_solution(16117317002692549266)
XLA Ops:
  0.0 0.0 copy-start.3
  0.0 0.0 copy-start.2
  0.0 0.7 copy-done.2
  0.7 3.1 %extract.2 = bf16[8,4,32,512]{3,2,1,0:T(8,128)(2,1)} custom-call(s32[16]{0:T(128)S(1)} %copy-done.2, f32[36,256,512]{2,1,0:T(8,128)} %bitcast.2), custom_call_target="tpu_custom_call" | custom-call | tf_op jit(solution)/shard_map/extract/pallas_call | solution.py:296
  3.8 5.3 %all-to-all-start = ((bf16[8,4,32,512]{3,2,1,0:T(8,128)(2,1)}), bf16[8,4,32,512]{3,2,1,0:T(8,128)(2,1)S(1)}, u32[]{:S(2)}, u32[]{:S(2)}) async-start(bf16[8,4,32,512]{3,2,1,0:T(8,128)(2,1)} %extract.2), calls=%async_computation | async-start | bytes 2097152 | tf_op jit(solution)/shard_map/all_to_all | solution.py:583
  9.1 1.5 table.1.t
  10.6 12.3 %all-to-all-done.spread_ref = bf16[8,4,32,512]{3,2,1,0:T(8,128)(2,1)S(1)} async-done(((bf16[8,4,32,512]{3,2,1,0:T(8,128)(2,1)}), bf16[8,4,32,512]{3,2,1,0:T(8,128)(2,1)S(1)}, u32[]{:S(2)}, u32[]{:S(2)}) %all-to-all-start) | async-done | bytes 1048608 | tf_op jit(solution)/shard_map/all_to_all | solution.py:583
  23.0 0.0 copy-start
  23.0 0.6 copy-done
  23.6 0.0 copy-start.1
  23.6 0.6 pick.2.near_ref
  24.2 2.4 %collective-permute-start = (bf16[4,4,32,512]{3,2,1,0:T(8,128)(2,1)S(1)}, bf16[4,4,32,512]{3,2,1,0:T(8,128)(2,1)S(1)}, u32[]{:S(2)}, u32[]{:S(2)}) collective-permute-start(bf16[4,4,32,512]{3,2,1,0:T(8,128)(2,1)S(1)} %pick.2.near_ref), channel_id=1, source_target_pairs={{0,16},{2,18},{4,20},{6,22},{8,24},{10,26},{12,28},{14,30},{16,0},... | collective-permute-start | bytes 1572872 | tf_op jit(solution)/shard_map/ppermute | solution.py:599
  26.6 21.7 %collective-permute-done.far_ref = bf16[4,4,32,512]{3,2,1,0:T(8,128)(2,1)S(1)} collective-permute-done((bf16[4,4,32,512]{3,2,1,0:T(8,128)(2,1)S(1)}, bf16[4,4,32,512]{3,2,1,0:T(8,128)(2,1)S(1)}, u32[]{:S(2)}, u32[]{:S(2)}) %collective-permute-start) | collective-permute-done | bytes 524320 | tf_op jit(solution)/shard_map/ppermute | solution.py:599
  48.2 2.2 %build.2 = bf16[8,7,32,512]{3,2,1,0:T(8,128)(2,1)} custom-call(s32[256]{0:T(256)S(1)} %copy-done, bf16[4,4,32,512]{3,2,1,0:T(8,128)(2,1)S(1)} %pick.2.near_ref, bf16[4,4,32,512]{3,2,1,0:T(8,128)(2,1)S(1)} %collective-permute-done.far_ref), custom_call_target="tpu_custom_call" | custom-call | tf_op jit(solution)/shard_map/build/pallas_call | solution.py:363
  50.5 4.8 %all-to-all-start.1 = ((bf16[8,7,32,512]{3,2,1,0:T(8,128)(2,1)}), bf16[8,7,32,512]{3,2,1,0:T(8,128)(2,1)S(1)}, u32[]{:S(2)}, u32[]{:S(2)}) async-start(bf16[8,7,32,512]{3,2,1,0:T(8,128)(2,1)} %build.2), calls=%async_computation.1 | async-start | bytes 3670016 | tf_op jit(solution)/shard_map/all_to_all | solution.py:583
  55.2 0.0 copy-done.3
  55.2 3.1 %extract.3 = bf16[8,4,32,512]{3,2,1,0:T(8,128)(2,1)} custom-call(s32[16]{0:T(128)S(1)} %copy-done.3, f32[36,256,512]{2,1,0:T(8,128)} %bitcast.3), custom_call_target="tpu_custom_call" | custom-call | tf_op jit(solution)/shard_map/extract/pallas_call | solution.py:296
  58.4 19.7 %all-to-all-done.1.refs_0_ = bf16[8,7,32,512]{3,2,1,0:T(8,128)(2,1)S(1)} async-done(((bf16[8,7,32,512]{3,2,1,0:T(8,128)(2,1)}), bf16[8,7,32,512]{3,2,1,0:T(8,128)(2,1)S(1)}, u32[]{:S(2)}, u32[]{:S(2)}) %all-to-all-start.1) | async-done | bytes 1835040 | tf_op jit(solution)/shard_map/all_to_all | solution.py:583
  78.0 4.8 %all-to-all-start.2 = ((bf16[8,4,32,512]{3,2,1,0:T(8,128)(2,1)}), bf16[8,4,32,512]{3,2,1,0:T(8,128)(2,1)S(1)}, u32[]{:S(2)}, u32[]{:S(2)}) async-start(bf16[8,4,32,512]{3,2,1,0:T(8,128)(2,1)} %extract.3), calls=%async_computation.2 | async-start | bytes 2097152 | tf_op jit(solution)/shard_map/all_to_all | solution.py:583
  82.8 0.8 collective-permute-start.1
  83.6 12.9 %all-to-all-done.2.spread_ref = bf16[8,4,32,512]{3,2,1,0:T(8,128)(2,1)S(1)} async-done(((bf16[8,4,32,512]{3,2,1,0:T(8,128)(2,1)}), bf16[8,4,32,512]{3,2,1,0:T(8,128)(2,1)S(1)}, u32[]{:S(2)}, u32[]{:S(2)}) %all-to-all-start.2) | async-done | bytes 1048608 | tf_op jit(solution)/shard_map/all_to_all | solution.py:583
  96.4 0.0 copy-done.1
  96.4 0.6 pick.3.near_ref
  97.0 3.1 %collective-permute-start.2 = (bf16[4,4,32,512]{3,2,1,0:T(8,128)(2,1)S(1)}, bf16[4,4,32,512]{3,2,1,0:T(8,128)(2,1)S(1)}, u32[]{:S(2)}, u32[]{:S(2)}) collective-permute-start(bf16[4,4,32,512]{3,2,1,0:T(8,128)(2,1)S(1)} %pick.3.near_ref), channel_id=1, source_target_pairs={{0,16},{2,18},{4,20},{6,22},{8,24},{10,26},{12,28},{14,30},{16,0},... | collective-permute-start | bytes 1572872 | tf_op jit(solution)/shard_map/ppermute | solution.py:599
  100.1 21.5 %collective-permute-done.2.far_ref = bf16[4,4,32,512]{3,2,1,0:T(8,128)(2,1)S(1)} collective-permute-done((bf16[4,4,32,512]{3,2,1,0:T(8,128)(2,1)S(1)}, bf16[4,4,32,512]{3,2,1,0:T(8,128)(2,1)S(1)}, u32[]{:S(2)}, u32[]{:S(2)}) %collective-permute-start.2) | collective-permute-done | bytes 524320 | tf_op jit(solution)/shard_map/ppermute | solution.py:599
  121.7 0.9 build.3
  122.6 3.2 %collective-permute-start.3 = (bf16[6,32,512]{2,1,0:T(8,128)(2,1)S(1)}, bf16[6,32,512]{2,1,0:T(8,128)(2,1)S(1)}, u32[]{:S(2)}, u32[]{:S(2)}) collective-permute-start(bf16[6,32,512]{2,1,0:T(8,128)(2,1)S(1)} %get-tuple-element.18), channel_id=1, source_target_pairs={{0,2},{2,0},{4,6},{6,4},{8,10},{10,8},{12,14},{14,12},{16,18},{18,... | collective-permute-start | bytes 589832 | tf_op jit(solution)/shard_map/ppermute | solution.py:609
  125.8 0.0 collective-permute-start.4
  125.8 1.3 collective-permute-start.5
  127.1 1.1 collective-permute-start.6
  128.2 1.8 collective-permute-done.3.refs_3_
  129.9 2.6 %collective-permute-start.7 = (bf16[6,32,512]{2,1,0:T(8,128)(2,1)S(1)}, bf16[6,32,512]{2,1,0:T(8,128)(2,1)S(1)}, u32[]{:S(2)}, u32[]{:S(2)}) collective-permute-start(bf16[6,32,512]{2,1,0:T(8,128)(2,1)S(1)} %get-tuple-element.22), channel_id=1, source_target_pairs={{0,10},{2,8},{4,14},{6,12},{8,2},{10,0},{12,6},{14,4},{16,26},{18,... | collective-permute-start | bytes 589832 | tf_op jit(solution)/shard_map/ppermute | solution.py:609
  132.6 2.6 %collective-permute-done.4.refs_4_ = bf16[6,32,512]{2,1,0:T(8,128)(2,1)S(1)} collective-permute-done((bf16[6,32,512]{2,1,0:T(8,128)(2,1)S(1)}, bf16[6,32,512]{2,1,0:T(8,128)(2,1)S(1)}, u32[]{:S(2)}, u32[]{:S(2)}) %collective-permute-start.4) | collective-permute-done | bytes 196640 | tf_op jit(solution)/shard_map/ppermute | solution.py:609
  135.2 0.0 collective-permute-start.8
  135.2 0.0 collective-permute-done.5.refs_5_
  135.2 4.6 %collective-permute-start.9 = (bf16[6,32,512]{2,1,0:T(8,128)(2,1)S(1)}, bf16[6,32,512]{2,1,0:T(8,128)(2,1)S(1)}, u32[]{:S(2)}, u32[]{:S(2)}) collective-permute-start(bf16[6,32,512]{2,1,0:T(8,128)(2,1)S(1)} %get-tuple-element.24), channel_id=1, source_target_pairs={{0,14},{2,12},{4,10},{6,8},{8,6},{10,4},{12,2},{14,0},{16,30},{18,... | collective-permute-start | bytes 589832 | tf_op jit(solution)/shard_map/ppermute | solution.py:609
  139.8 0.0 collective-permute-done.6.refs_6_
  139.8 2.5 %collective-permute-start.10 = (bf16[6,32,512]{2,1,0:T(8,128)(2,1)S(1)}, bf16[6,32,512]{2,1,0:T(8,128)(2,1)S(1)}, u32[]{:S(2)}, u32[]{:S(2)}) collective-permute-start(bf16[6,32,512]{2,1,0:T(8,128)(2,1)S(1)} %get-tuple-element.17.refs_2_), channel_id=1, source_target_pairs={{1,0},{0,1},{3,2},{2,3},{5,4},{4,5},{7,6},{6,7},{9,8},{8,9},{11,10... | collective-permute-start | bytes 589832 | tf_op jit(solution)/shard_map/ppermute | solution.py:589
  142.3 0.0 collective-permute-done.7.refs_7_
  142.3 0.1 collective-permute-start.11
  142.4 0.0 collective-permute-done.8.refs_8_
  142.4 3.9 %collective-permute-start.12 = (bf16[6,32,512]{2,1,0:T(8,128)(2,1)S(1)}, bf16[6,32,512]{2,1,0:T(8,128)(2,1)S(1)}, u32[]{:S(2)}, u32[]{:S(2)}) collective-permute-start(bf16[6,32,512]{2,1,0:T(8,128)(2,1)S(1)} %collective-permute-done.4.refs_4_), channel_id=1, source_target_pairs={{1,0},{0,1},{3,2},{2,3},{5,4},{4,5},{7,6},{6,7},{9,8},{8,9},{11,10... | collective-permute-start | bytes 589832 | tf_op jit(solution)/shard_map/ppermute | solution.py:589
  146.3 1.1 mark.1.t
  147.4 0.0 collective-permute-done.9.refs_9_
  147.5 1.0 collective-permute-start.13
  148.5 0.0 collective-permute-done.10.refs_10_
  148.5 0.0 collective-permute-start.14
  148.5 0.0 collective-permute-done.11.refs_11_
  148.5 0.5 collective-permute-start.15
  149.0 0.0 collective-permute-done.12.refs_12_
  149.0 0.1 collective-permute-start.16
  149.1 0.0 collective-permute-done.1.refs_1_
  149.1 0.4 collective-permute-start.17
  149.5 9.9 %inverse.1 = (bf16[512,512]{1,0:T(8,128)(2,1)S(1)}, f32[36,256,512]{2,1,0:T(8,128)S(1)}) custom-call(s32[8]{0:T(128)S(1)} %mark.1.t, bf16[8,7,32,512]{3,2,1,0:T(8,128)(2,1)S(1)} %all-to-all-done.1.refs_0_, bf16[8,7,32,512]{3,2,1,0:T(8,128)(2,1)} %collective-permute-done.1.refs_1_, f32[36,256,512]{2,1,0:T(8,128)} %bitcast.4), custom_call_target="tpu_custom_call" | custom-call | flops 16106127360 | bytes 1048576 | tf_op jit(solution)/shard_map/inverse/pallas_call | solution.py:466
  159.4 0.0 collective-permute-done.13.refs_13_
  159.4 0.0 collective-permute-done.14.refs_14_
  159.4 0.0 collective-permute-done.15.refs_15_
  159.4 0.0 collective-permute-done.16.refs_16_
  159.4 0.0 collective-permute-done.17.refs_17_
  159.4 19.0 %update.1 = f32[36,256,512]{2,1,0:T(8,128)} custom-call(s32[256]{0:T(256)S(1)} %copy-done.1, f32[36,256,512]{2,1,0:T(8,128)S(1)} %get-tuple-element.15.tiles, bf16[512,512]{1,0:T(8,128)(2,1)S(1)} %get-tuple-element.16.high, bf16[8,7,32,512]{3,2,1,0:T(8,128)(2,1)S(1)} %all-to-all-done.1.refs_0_, bf16[8,7,32,512]{3,2,1,0:T(8,128)(2,1)} %collective-permute-done.1.refs_1_, ...), custom_call_target="tpu_custom_call" | custom-call | tf_op jit(solution)/shard_map/update/pallas_call | solution.py:550
Async XLA Ops:
  0.0 55.2 %copy-start.3 = (s32[16]{0:T(128)S(1)}, s32[16]{0:T(128)}, u32[]{:S(2)}) copy-start(s32[16]{0:T(128)} %owner.5) | copy-start | bytes 196
  0.0 0.7 copy-start.2
  3.8 19.1 %all-to-all-start = ((bf16[8,4,32,512]{3,2,1,0:T(8,128)(2,1)}), bf16[8,4,32,512]{3,2,1,0:T(8,128)(2,1)S(1)}, u32[]{:S(2)}, u32[]{:S(2)}) async-start(bf16[8,4,32,512]{3,2,1,0:T(8,128)(2,1)} %extract.2), calls=%async_computation | async-start | bytes 2097152 | tf_op jit(solution)/shard_map/all_to_all | solution.py:583
  23.0 0.6 copy-start
  23.6 72.8 %copy-start.1 = (s32[256]{0:T(256)S(1)}, s32[256]{0:T(256)}, u32[]{:S(2)}) copy-start(s32[256]{0:T(256)} %table.1.t) | copy-start | bytes 3076
  24.2 24.0 %collective-permute-start = (bf16[4,4,32,512]{3,2,1,0:T(8,128)(2,1)S(1)}, bf16[4,4,32,512]{3,2,1,0:T(8,128)(2,1)S(1)}, u32[]{:S(2)}, u32[]{:S(2)}) collective-permute-start(bf16[4,4,32,512]{3,2,1,0:T(8,128)(2,1)S(1)} %pick.2.near_ref), channel_id=1, source_target_pairs={{0,16},{2,18},{4,20},{6,22},{8,24},{10,26},{12,28},{14,30},{16,0},... | collective-permute-start | bytes 1572872 | tf_op jit(solution)/shard_map/ppermute | solution.py:599
  50.5 27.5 %all-to-all-start.1 = ((bf16[8,7,32,512]{3,2,1,0:T(8,128)(2,1)}), bf16[8,7,32,512]{3,2,1,0:T(8,128)(2,1)S(1)}, u32[]{:S(2)}, u32[]{:S(2)}) async-start(bf16[8,7,32,512]{3,2,1,0:T(8,128)(2,1)} %build.2), calls=%async_computation.1 | async-start | bytes 3670016 | tf_op jit(solution)/shard_map/all_to_all | solution.py:583
  78.0 18.4 %all-to-all-start.2 = ((bf16[8,4,32,512]{3,2,1,0:T(8,128)(2,1)}), bf16[8,4,32,512]{3,2,1,0:T(8,128)(2,1)S(1)}, u32[]{:S(2)}, u32[]{:S(2)}) async-start(bf16[8,4,32,512]{3,2,1,0:T(8,128)(2,1)} %extract.3), calls=%async_computation.2 | async-start | bytes 2097152 | tf_op jit(solution)/shard_map/all_to_all | solution.py:583
  82.8 66.3 %collective-permute-start.1 = (bf16[8,7,32,512]{3,2,1,0:T(8,128)(2,1)S(1)}, bf16[8,7,32,512]{3,2,1,0:T(8,128)(2,1)}, u32[]{:S(2)}, u32[]{:S(2)}) collective-permute-start(bf16[8,7,32,512]{3,2,1,0:T(8,128)(2,1)S(1)} %all-to-all-done.1.refs_0_), channel_id=1, source_target_pairs={{1,0},{0,1},{3,2},{2,3},{5,4},{4,5},{7,6},{6,7},{9,8},{8,9},{11,10... | collective-permute-start | bytes 5505032 | tf_op jit(solution)/shard_map/ppermute | solution.py:589
  97.0 24.6 %collective-permute-start.2 = (bf16[4,4,32,512]{3,2,1,0:T(8,128)(2,1)S(1)}, bf16[4,4,32,512]{3,2,1,0:T(8,128)(2,1)S(1)}, u32[]{:S(2)}, u32[]{:S(2)}) collective-permute-start(bf16[4,4,32,512]{3,2,1,0:T(8,128)(2,1)S(1)} %pick.3.near_ref), channel_id=1, source_target_pairs={{0,16},{2,18},{4,20},{6,22},{8,24},{10,26},{12,28},{14,30},{16,0},... | collective-permute-start | bytes 1572872 | tf_op jit(solution)/shard_map/ppermute | solution.py:599
  122.6 7.3 %collective-permute-start.3 = (bf16[6,32,512]{2,1,0:T(8,128)(2,1)S(1)}, bf16[6,32,512]{2,1,0:T(8,128)(2,1)S(1)}, u32[]{:S(2)}, u32[]{:S(2)}) collective-permute-start(bf16[6,32,512]{2,1,0:T(8,128)(2,1)S(1)} %get-tuple-element.18), channel_id=1, source_target_pairs={{0,2},{2,0},{4,6},{6,4},{8,10},{10,8},{12,14},{14,12},{16,18},{18,... | collective-permute-start | bytes 589832 | tf_op jit(solution)/shard_map/ppermute | solution.py:609
  125.8 9.4 %collective-permute-start.4 = (bf16[6,32,512]{2,1,0:T(8,128)(2,1)S(1)}, bf16[6,32,512]{2,1,0:T(8,128)(2,1)S(1)}, u32[]{:S(2)}, u32[]{:S(2)}) collective-permute-start(bf16[6,32,512]{2,1,0:T(8,128)(2,1)S(1)} %get-tuple-element.19), channel_id=1, source_target_pairs={{0,4},{2,6},{4,0},{6,2},{8,12},{10,14},{12,8},{14,10},{16,20},{18,... | collective-permute-start | bytes 589832 | tf_op jit(solution)/shard_map/ppermute | solution.py:609
  125.8 9.4 %collective-permute-start.5 = (bf16[6,32,512]{2,1,0:T(8,128)(2,1)S(1)}, bf16[6,32,512]{2,1,0:T(8,128)(2,1)S(1)}, u32[]{:S(2)}, u32[]{:S(2)}) collective-permute-start(bf16[6,32,512]{2,1,0:T(8,128)(2,1)S(1)} %get-tuple-element.20), channel_id=1, source_target_pairs={{0,6},{2,4},{4,2},{6,0},{8,14},{10,12},{12,10},{14,8},{16,22},{18,... | collective-permute-start | bytes 589832 | tf_op jit(solution)/shard_map/ppermute | solution.py:609
  127.1 12.7 %collective-permute-start.6 = (bf16[6,32,512]{2,1,0:T(8,128)(2,1)S(1)}, bf16[6,32,512]{2,1,0:T(8,128)(2,1)S(1)}, u32[]{:S(2)}, u32[]{:S(2)}) collective-permute-start(bf16[6,32,512]{2,1,0:T(8,128)(2,1)S(1)} %get-tuple-element.21), channel_id=1, source_target_pairs={{0,8},{2,10},{4,12},{6,14},{8,0},{10,2},{12,4},{14,6},{16,24},{18,... | collective-permute-start | bytes 589832 | tf_op jit(solution)/shard_map/ppermute | solution.py:609
  129.9 12.4 %collective-permute-start.7 = (bf16[6,32,512]{2,1,0:T(8,128)(2,1)S(1)}, bf16[6,32,512]{2,1,0:T(8,128)(2,1)S(1)}, u32[]{:S(2)}, u32[]{:S(2)}) collective-permute-start(bf16[6,32,512]{2,1,0:T(8,128)(2,1)S(1)} %get-tuple-element.22), channel_id=1, source_target_pairs={{0,10},{2,8},{4,14},{6,12},{8,2},{10,0},{12,6},{14,4},{16,26},{18,... | collective-permute-start | bytes 589832 | tf_op jit(solution)/shard_map/ppermute | solution.py:609
  135.2 7.2 %collective-permute-start.8 = (bf16[6,32,512]{2,1,0:T(8,128)(2,1)S(1)}, bf16[6,32,512]{2,1,0:T(8,128)(2,1)S(1)}, u32[]{:S(2)}, u32[]{:S(2)}) collective-permute-start(bf16[6,32,512]{2,1,0:T(8,128)(2,1)S(1)} %get-tuple-element.23), channel_id=1, source_target_pairs={{0,12},{2,14},{4,8},{6,10},{8,4},{10,6},{12,0},{14,2},{16,28},{18,... | collective-permute-start | bytes 589832 | tf_op jit(solution)/shard_map/ppermute | solution.py:609
  135.2 12.3 %collective-permute-start.9 = (bf16[6,32,512]{2,1,0:T(8,128)(2,1)S(1)}, bf16[6,32,512]{2,1,0:T(8,128)(2,1)S(1)}, u32[]{:S(2)}, u32[]{:S(2)}) collective-permute-start(bf16[6,32,512]{2,1,0:T(8,128)(2,1)S(1)} %get-tuple-element.24), channel_id=1, source_target_pairs={{0,14},{2,12},{4,10},{6,8},{8,6},{10,4},{12,2},{14,0},{16,30},{18,... | collective-permute-start | bytes 589832 | tf_op jit(solution)/shard_map/ppermute | solution.py:609
  139.8 8.7 %collective-permute-start.10 = (bf16[6,32,512]{2,1,0:T(8,128)(2,1)S(1)}, bf16[6,32,512]{2,1,0:T(8,128)(2,1)S(1)}, u32[]{:S(2)}, u32[]{:S(2)}) collective-permute-start(bf16[6,32,512]{2,1,0:T(8,128)(2,1)S(1)} %get-tuple-element.17.refs_2_), channel_id=1, source_target_pairs={{1,0},{0,1},{3,2},{2,3},{5,4},{4,5},{7,6},{6,7},{9,8},{8,9},{11,10... | collective-permute-start | bytes 589832 | tf_op jit(solution)/shard_map/ppermute | solution.py:589
  142.3 6.1 %collective-permute-start.11 = (bf16[6,32,512]{2,1,0:T(8,128)(2,1)S(1)}, bf16[6,32,512]{2,1,0:T(8,128)(2,1)S(1)}, u32[]{:S(2)}, u32[]{:S(2)}) collective-permute-start(bf16[6,32,512]{2,1,0:T(8,128)(2,1)S(1)} %collective-permute-done.3.refs_3_), channel_id=1, source_target_pairs={{1,0},{0,1},{3,2},{2,3},{5,4},{4,5},{7,6},{6,7},{9,8},{8,9},{11,10... | collective-permute-start | bytes 589832 | tf_op jit(solution)/shard_map/ppermute | solution.py:589
  142.4 6.6 %collective-permute-start.12 = (bf16[6,32,512]{2,1,0:T(8,128)(2,1)S(1)}, bf16[6,32,512]{2,1,0:T(8,128)(2,1)S(1)}, u32[]{:S(2)}, u32[]{:S(2)}) collective-permute-start(bf16[6,32,512]{2,1,0:T(8,128)(2,1)S(1)} %collective-permute-done.4.refs_4_), channel_id=1, source_target_pairs={{1,0},{0,1},{3,2},{2,3},{5,4},{4,5},{7,6},{6,7},{9,8},{8,9},{11,10... | collective-permute-start | bytes 589832 | tf_op jit(solution)/shard_map/ppermute | solution.py:589
  147.5 11.9 %collective-permute-start.13 = (bf16[6,32,512]{2,1,0:T(8,128)(2,1)S(1)}, bf16[6,32,512]{2,1,0:T(8,128)(2,1)S(1)}, u32[]{:S(2)}, u32[]{:S(2)}) collective-permute-start(bf16[6,32,512]{2,1,0:T(8,128)(2,1)S(1)} %collective-permute-done.5.refs_5_), channel_id=1, source_target_pairs={{1,0},{0,1},{3,2},{2,3},{5,4},{4,5},{7,6},{6,7},{9,8},{8,9},{11,10... | collective-permute-start | bytes 589832 | tf_op jit(solution)/shard_map/ppermute | solution.py:589
  148.5 10.9 %collective-permute-start.14 = (bf16[6,32,512]{2,1,0:T(8,128)(2,1)S(1)}, bf16[6,32,512]{2,1,0:T(8,128)(2,1)S(1)}, u32[]{:S(2)}, u32[]{:S(2)}) collective-permute-start(bf16[6,32,512]{2,1,0:T(8,128)(2,1)S(1)} %collective-permute-done.6.refs_6_), channel_id=1, source_target_pairs={{1,0},{0,1},{3,2},{2,3},{5,4},{4,5},{7,6},{6,7},{9,8},{8,9},{11,10... | collective-permute-start | bytes 589832 | tf_op jit(solution)/shard_map/ppermute | solution.py:589
  148.5 10.9 %collective-permute-start.15 = (bf16[6,32,512]{2,1,0:T(8,128)(2,1)S(1)}, bf16[6,32,512]{2,1,0:T(8,128)(2,1)S(1)}, u32[]{:S(2)}, u32[]{:S(2)}) collective-permute-start(bf16[6,32,512]{2,1,0:T(8,128)(2,1)S(1)} %collective-permute-done.7.refs_7_), channel_id=1, source_target_pairs={{1,0},{0,1},{3,2},{2,3},{5,4},{4,5},{7,6},{6,7},{9,8},{8,9},{11,10... | collective-permute-start | bytes 589832 | tf_op jit(solution)/shard_map/ppermute | solution.py:589
  149.0 10.4 %collective-permute-start.16 = (bf16[6,32,512]{2,1,0:T(8,128)(2,1)S(1)}, bf16[6,32,512]{2,1,0:T(8,128)(2,1)S(1)}, u32[]{:S(2)}, u32[]{:S(2)}) collective-permute-start(bf16[6,32,512]{2,1,0:T(8,128)(2,1)S(1)} %collective-permute-done.8.refs_8_), channel_id=1, source_target_pairs={{1,0},{0,1},{3,2},{2,3},{5,4},{4,5},{7,6},{6,7},{9,8},{8,9},{11,10... | collective-permute-start | bytes 589832 | tf_op jit(solution)/shard_map/ppermute | solution.py:589
  149.1 10.4 %collective-permute-start.17 = (bf16[6,32,512]{2,1,0:T(8,128)(2,1)S(1)}, bf16[6,32,512]{2,1,0:T(8,128)(2,1)S(1)}, u32[]{:S(2)}, u32[]{:S(2)}) collective-permute-start(bf16[6,32,512]{2,1,0:T(8,128)(2,1)S(1)} %collective-permute-done.9.refs_9_), channel_id=1, source_target_pairs={{1,0},{0,1},{3,2},{2,3},{5,4},{4,5},{7,6},{6,7},{9,8},{8,9},{11,10... | collective-permute-start | bytes 589832 | tf_op jit(solution)/shard_map/ppermute | solution.py:589

commit v5 on v4

--- a/solution.py
+++ b/solution.py
@@ -129,50 +129,52 @@
 
 
 class Plan:
-    def __init__(self, tri, subs, slots, strip, order, chunks):
+    def __init__(self, tri, subs, slots, strip, order):
         self.tri, self.subs, self.slots, self.strip, self.order = tri, subs, slots, strip, order
-        self.chunks = chunks
         self.groups = math.isqrt(tri)
         self.per_group = NB // self.groups
         self.half_group = self.per_group // 2
         self.half_tri = tri // 2
         self.piece = strip // self.half_tri
-        self.wide = self.half_group // chunks
-        self.in_chunk = 2 * self.wide
+        quarter = self.half_group // 4
+        self.wides = [2 * quarter, quarter, quarter]
+        self.firsts = [0, 2 * quarter, 3 * quarter]
+        self.spreads = [[0], [1, 2]]
         self.o_sub = 0
         self.o_diag = 1
         self.o_me = 2
+        self.o_dead = 3
         self.o_src = 8
         self.o_here = self.o_src + self.groups
         self.o_rg = self.o_here + self.groups
         self.o_cg = self.o_rg + self.half_tri
         self.o_hf = self.o_cg + self.half_tri
-        self.o_row_chunk = self.o_hf + self.half_tri
-        self.o_row_place = self.o_row_chunk + slots
-        self.o_col_chunk = self.o_row_place + slots
-        self.o_col_place = self.o_col_chunk + slots
-        self.o_live = self.o_col_place + slots
-        self.o_new = self.o_live + slots
-        self.size = self.o_new + slots
+        self.size = self.o_hf + self.half_tri
 
     def tiled(self):
         return (
             self.piece % 16 == 0
             and self.order % 128 == 0
-            and self.half_group % self.chunks == 0
+            and self.half_group % 4 == 0
             and self.groups * self.groups == self.tri
             and self.half_tri & (self.half_tri - 1) == 0
             and self.subs * self.strip == self.order
+            and self.slots == self.per_group * (self.per_group + 1) // 2
         )
 
+    def tiles_of(self, chunk):
+        inner = range(self.firsts[chunk], self.firsts[chunk] + self.wides[chunk])
+        return [half * self.half_group + n for half in range(2) for n in inner]
+
     def place_of(self, member):
-        half, inner = divmod(member, self.half_group)
-        chunk, rest = divmod(inner, self.wide)
-        return chunk, half * self.wide + rest
-
-    def tile_of(self, chunk, place):
-        half, inner = divmod(place, self.wide)
-        return half * self.half_group + chunk * self.wide + inner
+        for chunk in range(len(self.wides)):
+            if member in self.tiles_of(chunk):
+                return chunk, self.tiles_of(chunk).index(member)
+        raise ValueError(member)
+
+    def column_of(self, inner):
+        chunk, place = self.place_of(inner)
+        return chunk, 2 * self.wides[chunk] + place
 
 
 def table_call(p, cell_owner):
@@ -187,7 +189,6 @@
             return down, across
 
         down, across = split(cell_of[position])
-        row_group = jnp.maximum(down, across)
         col_group = jnp.minimum(down, across)
         diag = down == across
         my_half = position // p.half_tri
@@ -204,28 +205,7 @@
             out[p.o_rg + end] = jnp.maximum(there_down, there_across)
             out[p.o_cg + end] = jnp.minimum(there_down, there_across)
             out[p.o_hf + end] = jnp.where(there_down < there_across, 1, 0)
-        col_shift = jnp.where(down < across, p.half_group, 0)
-        triangle = [(i, j) for i in range(p.per_group) for j in range(i + 1)]
-        for slot in range(p.slots):
-            tri_i, tri_j = triangle[slot] if slot < len(triangle) else (0, -1)
-            box_i, box_j = divmod(slot, p.half_group)
-            if box_i >= p.per_group:
-                box_i, box_j = 0, -1
-            inner_i = jnp.where(diag, tri_i, box_i)
-            inner_j = jnp.where(diag, tri_j, box_j)
-            row = row_group * p.per_group + inner_i
-            col = col_group * p.per_group + jnp.where(diag, 0, col_shift) + inner_j
-            live = (inner_j >= 0) & (row > 0) & (col > 0)
-            tri_row, tri_col = p.place_of(tri_i), p.place_of(max(tri_j, 0))
-            box_row, box_col = p.place_of(box_i), p.place_of(max(box_j, 0))
-            out[p.o_row_chunk + slot] = jnp.where(diag, tri_row[0], box_row[0])
-            out[p.o_row_place + slot] = jnp.where(diag, tri_row[1], box_row[1])
-            out[p.o_col_chunk + slot] = jnp.where(diag, tri_col[0], box_col[0])
-            out[p.o_col_place + slot] = jnp.where(diag, tri_col[1], p.in_chunk + box_col[1])
-            out[p.o_live + slot] = jnp.where(live, 1, 0)
-            new_tri = 1 if tri_j == 0 else 0
-            new_box = 1 if box_j == 0 else 0
-            out[p.o_new + slot] = jnp.where(diag, new_tri, new_box)
+        out[p.o_dead] = jnp.where((col_group == 0) & (down >= across), 1, 0)
 
     return pl.pallas_call(
         kernel,
@@ -272,7 +252,7 @@
     )(table)
 
 
-def extract_call(p, cell_owner, current, chunk):
+def extract_call(p, cell_owner, current, members):
     def kernel(owner, tiles, out, wide, sems):
         position = lax.axis_index("tri")
         cell = jnp.int32(0)
@@ -280,8 +260,7 @@
             cell = jnp.where(owner[n] == position, n, cell)
         down = cell // p.groups
         copies = []
-        for place in range(p.in_chunk):
-            member = p.tile_of(chunk, place)
+        for place, member in enumerate(members):
             slot = jnp.where(down > 0, member * p.half_group, member * (member + 1) // 2)
             copies.append(
                 pltpu.make_async_copy(tiles.at[slot], wide.at[place], sems.at[place])
@@ -295,39 +274,48 @@
 
     return pl.pallas_call(
         kernel,
-        out_shape=pltpu.VMEM((p.half_tri, p.in_chunk, p.piece, p.order), jnp.bfloat16),
+        out_shape=pltpu.VMEM((p.half_tri, len(members), p.piece, p.order), jnp.bfloat16),
         in_specs=[
             pl.BlockSpec(memory_space=pltpu.SMEM),
             pl.BlockSpec(memory_space=pltpu.HBM),
         ],
         out_specs=IN_VMEM,
         scratch_shapes=[
-            pltpu.VMEM((p.in_chunk, p.strip, p.order), jnp.float32),
-            pltpu.SemaphoreType.DMA((p.in_chunk,)),
+            pltpu.VMEM((len(members), p.strip, p.order), jnp.float32),
+            pltpu.SemaphoreType.DMA((len(members),)),
         ],
         compiler_params=limit(8),
         name="extract",
     )(cell_owner, in_hbm(current))
 
 
-def pick_call(p, table, spread):
-    def kernel(t, spread_ref, out):
+def pick_call(p, table, spread, chunks):
+    def kernel(t, spread_ref, *outs):
         for g in range(p.groups):
-            out[g] = spread_ref[t[p.o_src + g]]
+            first = 0
+            for out in outs:
+                count = out.shape[1]
+                out[g] = spread_ref[t[p.o_src + g], first : first + count]
+                first += count
 
     return pl.pallas_call(
         kernel,
-        out_shape=pltpu.VMEM((p.groups,) + spread.shape[1:], jnp.bfloat16),
+        out_shape=[
+            pltpu.VMEM((p.groups, 2 * p.wides[k], p.piece, p.order), jnp.bfloat16) for k in chunks
+        ],
         grid_spec=pltpu.PrefetchScalarGridSpec(
-            num_scalar_prefetch=1, grid=(), in_specs=[IN_VMEM], out_specs=IN_VMEM
+            num_scalar_prefetch=1,
+            grid=(),
+            in_specs=[IN_VMEM],
+            out_specs=[IN_VMEM] * len(chunks),
         ),
         compiler_params=limit(8),
         name="pick",
     )(table, in_vmem(spread))
 
 
-def build_call(p, table, near, far, with_pivot, apart):
-    rows = p.in_chunk + p.wide + (1 if with_pivot else 0)
+def build_call(p, table, near, far, wide, with_pivot, apart):
+    rows = 3 * wide + (1 if with_pivot else 0)
 
     def kernel(t, near_ref, far_ref, *outs):
         def part(group, first, count, n, place):
@@ -350,10 +338,10 @@
 
         for n in range(p.half_tri):
             end = t[p.o_me] ^ n if apart else n
-            part(t[p.o_rg + end], 0, p.in_chunk, n, 0)
-            part(t[p.o_cg + end], t[p.o_hf + end] * p.wide, p.wide, n, p.in_chunk)
+            part(t[p.o_rg + end], 0, 2 * wide, n, 0)
+            part(t[p.o_cg + end], t[p.o_hf + end] * wide, wide, n, 2 * wide)
             if with_pivot:
-                part(0, 0, 1, n, p.in_chunk + p.wide)
+                part(0, 0, 1, n, 3 * wide)
 
     one = (rows, p.piece, p.order)
     if apart:
@@ -378,7 +366,7 @@
 def inverse_call(p, table, arrived, current):
     loads = next(n for n in (6, 5, 4, 3, 2, 1) if p.slots % n == 0)
     each = p.slots // loads
-    place = p.in_chunk + p.wide
+    place = 3 * p.wides[0]
     order = p.order
 
     def kernel(t, *refs):
@@ -488,89 +476,136 @@
 
 
 def update_call(p, table, held, together, apart, inverse):
-    per_step = next(n for n in (4, 3, 2, 1) if p.slots % n == 0)
-    last = p.chunks - 1
-    n_together = last * p.subs
-    n_apart = p.subs * p.half_tri
-
-    def kernel(t, tiles, high, *refs):
-        sources = [refs[k * p.subs : (k + 1) * p.subs] for k in range(last)]
-        loose = refs[n_together : n_together + n_apart]
-        out, scaled, packed = refs[n_together + n_apart :]
-        sources.append([packed.at[shift] for shift in range(p.subs)])
-        step = pl.program_id(0)
+    ring_size = 8
+    chunks = len(p.wides)
+    rows_in_box = p.per_group * p.half_group
+
+    def kernel(t, tiles, inv, *refs):
+        sources = [list(refs[: p.subs])]
+        at = p.subs
+        loose = []
+        for _ in range(1, chunks):
+            loose.append(refs[at : at + p.subs * p.half_tri])
+            at += p.subs * p.half_tri
+        out, column, ring, ring_sems, rest_sem, *packed = refs[at:]
         sub = t[p.o_sub]
-
-        @pl.when(step == 0)
-        def _():
+        diag = t[p.o_diag] == 1
+        dead = t[p.o_dead] == 1
+
+        for k in range(chunks - 1):
             for shift in range(p.subs):
                 for n in range(p.half_tri):
-                    packed[shift, t[p.o_me] ^ n] = loose[shift * p.half_tri + n][...]
-
-        for u in range(per_step):
-            slot = step * per_step + u
-            for k in range(p.chunks):
-
-                @pl.when((t[p.o_new + slot] == 1) & (t[p.o_row_chunk + slot] == k))
-                def _():
-                    strip = sources[k][0][:, t[p.o_row_place + slot]].reshape(p.strip, p.order)
-                    dims = (((1,), (0,)), ((), ()))
-                    product = lax.dot_general(
-                        strip, high[...], dims, preferred_element_type=jnp.float32
-                    )
-                    scaled[...] = product.astype(jnp.bfloat16)
-
-            live = t[p.o_live + slot] == 1
-            for k in range(p.chunks):
-
-                @pl.when(live & (t[p.o_col_chunk + slot] == k))
-                def _():
-                    strips = [
-                        sources[k][shift][:, t[p.o_col_place + slot]].reshape(p.strip, p.order)
-                        for shift in range(p.subs)
-                    ]
-                    for place in range(p.subs):
-                        strip = strips[0]
-                        for shift in range(1, p.subs):
-                            here = lax.rem(sub + shift, p.subs) == place
-                            strip = jnp.where(here, strips[shift], strip)
-                        at = slice(place * p.strip, (place + 1) * p.strip)
-                        out[u, :, at] = tiles[slot, :, at] + lax.dot_general(
-                            scaled[...],
-                            strip,
-                            (((1,), (1,)), ((), ())),
-                            preferred_element_type=jnp.float32,
-                        )
-
-            @pl.when(jnp.logical_not(live))
-            def _():
-                out[u] = tiles[slot]
-
-    loose = [in_vmem(ref) for shift in apart for ref in shift]
+                    packed[k][shift, t[p.o_me] ^ n] = loose[k][shift * p.half_tri + n][...]
+            sources.append([packed[k].at[shift] for shift in range(p.subs)])
+
+        def strip_of(shift, chunk, place):
+            return sources[chunk][shift][:, place].reshape(p.strip, p.order)
+
+        def gather_column(j, chunk, place):
+            strips = [strip_of(shift, chunk, place) for shift in range(p.subs)]
+            for at in range(p.subs):
+                strip = strips[0]
+                for shift in range(1, p.subs):
+                    here = lax.rem(sub + shift, p.subs) == at
+                    strip = jnp.where(here, strips[shift], strip)
+                if j == 0:
+                    strip = jnp.where(dead, jnp.zeros_like(strip), strip)
+                column[j, at * p.strip : (at + 1) * p.strip] = strip
+
+        def scale(members):
+            strips = [strip_of(0, *p.place_of(member)) for member in members]
+            product = lax.dot_general(
+                jnp.concatenate(strips, axis=0),
+                inv[...],
+                (((1,), (0,)), ((), ())),
+                preferred_element_type=jnp.float32,
+            )
+            return product.astype(jnp.bfloat16)
+
+        def times(left, j):
+            return lax.dot_general(
+                left, column[j], (((1,), (1,)), ((), ())), preferred_element_type=jnp.float32
+            )
+
+        class Writer:
+            def __init__(self):
+                self.copies = []
+
+            def put(self, slot, product):
+                n = len(self.copies)
+                if n >= ring_size:
+                    self.copies[n - ring_size].wait()
+                ring[n % ring_size] = tiles[slot] + product
+                copy = pltpu.make_async_copy(
+                    ring.at[n % ring_size], out.at[slot], ring_sems.at[n % ring_size]
+                )
+                copy.start()
+                self.copies.append(copy)
+
+            def finish(self):
+                for copy in self.copies[-ring_size:]:
+                    copy.wait()
+
+        @pl.when(diag)
+        def _():
+            writer = Writer()
+            for i in range(0, p.per_group, 2):
+                left = scale([i, i + 1])
+                for j in range(i + 1):
+                    if j == i:
+                        gather_column(j, *p.place_of(j))
+                    product = times(left, j)
+                    for r in range(2):
+                        slot = (i + r) * (i + r + 1) // 2 + j
+                        writer.put(slot, product[r * p.strip : (r + 1) * p.strip])
+                gather_column(i + 1, *p.place_of(i + 1))
+                slot = (i + 1) * (i + 2) // 2 + i + 1
+                writer.put(slot, times(left[p.strip :], i + 1))
+            writer.finish()
+
+        @pl.when(jnp.logical_not(diag))
+        def _():
+            if p.slots > rows_in_box:
+                empty = pl.ds(rows_in_box, p.slots - rows_in_box)
+                rest = pltpu.make_async_copy(tiles.at[empty], out.at[empty], rest_sem)
+                rest.start()
+            writer = Writer()
+            for i in range(0, p.per_group, 2):
+                left = scale([i, i + 1])
+                for j in range(p.half_group):
+                    if i == 0:
+                        gather_column(j, *p.column_of(j))
+                    product = times(left, j)
+                    for r in range(2):
+                        slot = (i + r) * p.half_group + j
+                        writer.put(slot, product[r * p.strip : (r + 1) * p.strip])
+            writer.finish()
+            if p.slots > rows_in_box:
+                rest.wait()
+
+    loose = [in_vmem(ref) for chunk in apart for shift in chunk for ref in shift]
     return pl.pallas_call(
         kernel,
         out_shape=jax.ShapeDtypeStruct(held.shape, jnp.float32),
         grid_spec=pltpu.PrefetchScalarGridSpec(
             num_scalar_prefetch=1,
-            grid=(p.slots // per_step,),
-            in_specs=[IN_VMEM] * (2 + n_together + n_apart),
-            out_specs=pl.BlockSpec((per_step, p.strip, p.order), lambda i, t: (i, 0, 0)),
+            grid=(),
+            in_specs=[IN_VMEM] * (2 + p.subs + len(loose)),
+            out_specs=pl.BlockSpec(memory_space=pltpu.HBM),
             scratch_shapes=[
-                pltpu.VMEM((p.strip, p.order), jnp.bfloat16),
-                pltpu.VMEM((p.subs, p.half_tri) + loose[0].shape, jnp.bfloat16),
+                pltpu.VMEM((p.per_group, p.order, p.order), jnp.bfloat16),
+                pltpu.VMEM((ring_size, p.strip, p.order), jnp.float32),
+                pltpu.SemaphoreType.DMA((ring_size,)),
+                pltpu.SemaphoreType.DMA,
+            ]
+            + [
+                pltpu.VMEM((p.subs, p.half_tri) + chunk[0][0].shape, jnp.bfloat16)
+                for chunk in apart
             ],
         ),
-        compiler_params=pltpu.CompilerParams(
-            dimension_semantics=("arbitrary",), vmem_limit_bytes=16 * 2**20
-        ),
+        compiler_params=limit(24),
         name="update",
-    )(
-        table,
-        in_vmem(held),
-        in_vmem(inverse),
-        *[in_vmem(ref) for chunk in together for ref in chunk],
-        *loose,
-    )
+    )(table, in_vmem(held), in_vmem(inverse), *[in_vmem(ref) for ref in together], *loose)
 
 
 def planned(p, stored_tiles, cell_owner):
@@ -590,28 +625,30 @@
             for shift in range(1, p.subs)
         ]
 
-    near, far, arrived = [], [], []
-    for chunk in range(p.chunks):
-        pieces = extract_call(p, cell_owner, current, chunk)
+    chunks = len(p.wides)
+    near, far = [], []
+    for members in p.spreads:
+        tiles = [tile for chunk in members for tile in p.tiles_of(chunk)]
+        pieces = extract_call(p, cell_owner, current, tiles)
         spread = exchange(pieces)
-        near.append(pick_call(p, table, spread))
-    for chunk in range(p.chunks):
+        near.extend(pick_call(p, table, spread, members))
+    for chunk in range(chunks):
         far.append(lax.ppermute(near[chunk], "tri", swap))
-    last = p.chunks - 1
-    for chunk in range(last):
-        built = build_call(p, table, near[chunk], far[chunk], chunk == 0, False)
-        whole = exchange(built)
-        arrived.append(arrivals(whole))
-    built = build_call(p, table, near[last], far[last], last == 0, True)
-    loose = [built[0]]
-    for n in range(1, p.half_tri):
-        pairs = [(i, i ^ n) for i in range(p.tri)]
-        loose.append(lax.ppermute(built[n], "tri", pairs))
-    pieces = [arrivals(x) for x in loose]
-    apart = [[piece[shift] for piece in pieces] for shift in range(p.subs)]
+    built = build_call(p, table, near[0], far[0], p.wides[0], True, False)
+    whole = exchange(built)
+    together = arrivals(whole)
+    apart = []
+    for chunk in range(1, chunks):
+        built = build_call(p, table, near[chunk], far[chunk], p.wides[chunk], False, True)
+        loose = [built[0]]
+        for n in range(1, p.half_tri):
+            pairs = [(i, i ^ n) for i in range(p.tri)]
+            loose.append(lax.ppermute(built[n], "tri", pairs))
+        sides = [arrivals(x) for x in loose]
+        apart.append([[piece[shift] for piece in sides] for shift in range(p.subs)])
     marked = mark_call(p, table)
-    inverse, held = inverse_call(p, marked, arrived[0], current)
-    return update_call(p, table, held, arrived, apart, inverse)[None]
+    inverse, held = inverse_call(p, marked, together, current)
+    return update_call(p, table, held, together, apart, inverse)[None]
 
 
 def shards(stored_tiles, cell_owner):
@@ -621,7 +658,6 @@
         stored_tiles.shape[1],
         stored_tiles.shape[2],
         stored_tiles.shape[3],
-        2,
     )
     if p.tiled():
         return planned(p, stored_tiles, cell_owner)

time: 179 us -> 177 us (0.989)
  starting transfers between devices: 42.4 us -> 54.4 us
  waiting for transfers between devices: 92.5 us -> 84.5 us
  Pallas kernels: 42.1 us -> 35.9 us
    pallas_call x1, Pallas kernels: 19 us -> 12.3 us  [update_call(): pl.pallas_call(kernel, out_shape=jax.ShapeDtypeStruct(held.shape, jnp.flo...]
    ppermute x7 -> x14, starting transfers between devices: 12.8 us -> 19.4 us  [planned(): loose.append(lax.ppermute(built[n], 'tri', pairs))]
    ppermute x2 -> x3, waiting for transfers between devices: 43.2 us -> 37.8 us  [planned(): far.append(lax.ppermute(near[chunk], 'tri', swap))]
    ppermute x9 -> x17, starting transfers between devices: 9.29 us -> 14.6 us  [arrivals(): lax.ppermute(x, 'sub', [((i + shift) % p.subs, i) for i in range(p.subs)])]
    ppermute x7 -> x14, waiting for transfers between devices: 4.39 us -> 1.22 us  [planned(): loose.append(lax.ppermute(built[n], 'tri', pairs))]
    pallas_call x2 -> x3, Pallas kernels: 3.14 us -> 3.95 us  [build_call(): pl.pallas_call(kernel, out_shape=out_shape, grid_spec=pltpu.PrefetchScala...]
    ppermute x2 -> x3, starting transfers between devices: 5.46 us -> 5.54 us  [planned(): far.append(lax.ppermute(near[chunk], 'tri', swap))]
  transfers between devices with their start and end apart: 21 -> 37, of which waited for: 7 -> 9; matrix products, arithmetic and copies ran while one was open for 0% -> 0% of each run, Pallas kernels for 10% -> 10%
where the time goes in v5:
time: 177 us; the launch traced here: 176 us
  waiting for transfers between devices  84.5 us (48%)
  starting transfers between devices  54.4 us (31%)
  Pallas kernels  35.9 us (20%)
    all_to_all x3, waiting for transfers between devices, exchange(): lax.all_to_all(x, 'tri', split_axis=0, concat_axis=0, tiled=True, axis_in...  45.1 us
    ppermute x3, waiting for transfers between devices, planned(): far.append(lax.ppermute(near[chunk], 'tri', swap))  37.8 us
    ppermute x14, starting transfers between devices, planned(): loose.append(lax.ppermute(built[n], 'tri', pairs))  19.4 us
    all_to_all x3, starting transfers between devices, exchange(): lax.all_to_all(x, 'tri', split_axis=0, concat_axis=0, tiled=True, axis_in...  14.8 us
    ppermute x17, starting transfers between devices, arrivals(): lax.ppermute(x, 'sub', [((i + shift) % p.subs, i) for i in range(p.subs)])  14.6 us
    pallas_call x1, Pallas kernels, update_call(): pl.pallas_call(kernel, out_shape=jax.ShapeDtypeStruct(held.shape, jnp.flo...  12.3 us
    pallas_call x1, Pallas kernels, inverse_call(): pl.pallas_call(kernel, out_shape=(square_shape, pltpu.VMEM(current.shape,...  9.86 us
    pallas_call x2, Pallas kernels, extract_call(): pl.pallas_call(kernel, out_shape=pltpu.VMEM((p.half_tri, len(members), p....  6.22 us
  transfers between devices with their start and end apart: 37, of which 9 were waited for; matrix products, arithmetic and copies ran while one was open for 0% of the time, Pallas kernels for 10%

profile of v5, /device:TPU:1, one launch (start us, length us, event | category | flops | bytes accessed | tf_op | source)
XLA Modules:
  0.0 176.4 jit_solution(18288022251398040916)
XLA Ops:
  0.0 0.7 copy-done.2
  0.7 3.1 %extract.2 = bf16[8,4,32,512]{3,2,1,0:T(8,128)(2,1)} custom-call(s32[16]{0:T(128)S(1)} %copy-done.2, f32[36,256,512]{2,1,0:T(8,128)} %bitcast.2), custom_call_target="tpu_custom_call" | custom-call | tf_op jit(solution)/shard_map/extract/pallas_call | solution.py:275
  3.8 5.3 %all-to-all-start = ((bf16[8,4,32,512]{3,2,1,0:T(8,128)(2,1)}), bf16[8,4,32,512]{3,2,1,0:T(8,128)(2,1)S(1)}, u32[]{:S(2)}, u32[]{:S(2)}) async-start(bf16[8,4,32,512]{3,2,1,0:T(8,128)(2,1)} %extract.2), calls=%async_computation | async-start | bytes 2097152 | tf_op jit(solution)/shard_map/all_to_all | solution.py:618
  9.1 1.3 table.1.t
  10.4 12.5 %all-to-all-done.spread_ref = bf16[8,4,32,512]{3,2,1,0:T(8,128)(2,1)S(1)} async-done(((bf16[8,4,32,512]{3,2,1,0:T(8,128)(2,1)}), bf16[8,4,32,512]{3,2,1,0:T(8,128)(2,1)S(1)}, u32[]{:S(2)}, u32[]{:S(2)}) %all-to-all-start) | async-done | bytes 1048608 | tf_op jit(solution)/shard_map/all_to_all | solution.py:618
  23.0 0.6 copy-done
  23.6 0.6 pick.2.near_ref
  24.2 2.4 %collective-permute-start = (bf16[4,4,32,512]{3,2,1,0:T(8,128)(2,1)S(1)}, bf16[4,4,32,512]{3,2,1,0:T(8,128)(2,1)S(1)}, u32[]{:S(2)}, u32[]{:S(2)}) collective-permute-start(bf16[4,4,32,512]{3,2,1,0:T(8,128)(2,1)S(1)} %pick.2.near_ref), channel_id=1, source_target_pairs={{0,16},{2,18},{4,20},{6,22},{8,24},{10,26},{12,28},{14,30},{16,0},... | collective-permute-start | bytes 1572872 | tf_op jit(solution)/shard_map/ppermute | solution.py:636
  26.5 21.7 %collective-permute-done.far_ref = bf16[4,4,32,512]{3,2,1,0:T(8,128)(2,1)S(1)} collective-permute-done((bf16[4,4,32,512]{3,2,1,0:T(8,128)(2,1)S(1)}, bf16[4,4,32,512]{3,2,1,0:T(8,128)(2,1)S(1)}, u32[]{:S(2)}, u32[]{:S(2)}) %collective-permute-start) | collective-permute-done | bytes 524320 | tf_op jit(solution)/shard_map/ppermute | solution.py:636
  48.2 2.2 %build.3 = bf16[8,7,32,512]{3,2,1,0:T(8,128)(2,1)} custom-call(s32[40]{0:T(128)S(1)} %copy-done, bf16[4,4,32,512]{3,2,1,0:T(8,128)(2,1)S(1)} %pick.2.near_ref, bf16[4,4,32,512]{3,2,1,0:T(8,128)(2,1)S(1)} %collective-permute-done.far_ref), custom_call_target="tpu_custom_call" | custom-call | tf_op jit(solution)/shard_map/build/pallas_call | solution.py:351
  50.4 4.8 %all-to-all-start.1 = ((bf16[8,7,32,512]{3,2,1,0:T(8,128)(2,1)}), bf16[8,7,32,512]{3,2,1,0:T(8,128)(2,1)S(1)}, u32[]{:S(2)}, u32[]{:S(2)}) async-start(bf16[8,7,32,512]{3,2,1,0:T(8,128)(2,1)} %build.3), calls=%async_computation.1 | async-start | bytes 3670016 | tf_op jit(solution)/shard_map/all_to_all | solution.py:618
  55.2 3.1 %extract.3 = bf16[8,4,32,512]{3,2,1,0:T(8,128)(2,1)} custom-call(s32[16]{0:T(128)S(1)} %copy-done.3, f32[36,256,512]{2,1,0:T(8,128)} %bitcast.3), custom_call_target="tpu_custom_call" | custom-call | tf_op jit(solution)/shard_map/extract/pallas_call | solution.py:275
  58.3 19.6 %all-to-all-done.1.refs_0_ = bf16[8,7,32,512]{3,2,1,0:T(8,128)(2,1)S(1)} async-done(((bf16[8,7,32,512]{3,2,1,0:T(8,128)(2,1)}), bf16[8,7,32,512]{3,2,1,0:T(8,128)(2,1)S(1)}, u32[]{:S(2)}, u32[]{:S(2)}) %all-to-all-start.1) | async-done | bytes 1835040 | tf_op jit(solution)/shard_map/all_to_all | solution.py:618
  78.0 4.8 %all-to-all-start.2 = ((bf16[8,4,32,512]{3,2,1,0:T(8,128)(2,1)}), bf16[8,4,32,512]{3,2,1,0:T(8,128)(2,1)S(1)}, u32[]{:S(2)}, u32[]{:S(2)}) async-start(bf16[8,4,32,512]{3,2,1,0:T(8,128)(2,1)} %extract.3), calls=%async_computation.2 | async-start | bytes 2097152 | tf_op jit(solution)/shard_map/all_to_all | solution.py:618
  82.7 0.8 collective-permute-start.1
  83.5 12.9 %all-to-all-done.2.spread_ref = bf16[8,4,32,512]{3,2,1,0:T(8,128)(2,1)S(1)} async-done(((bf16[8,4,32,512]{3,2,1,0:T(8,128)(2,1)}), bf16[8,4,32,512]{3,2,1,0:T(8,128)(2,1)S(1)}, u32[]{:S(2)}, u32[]{:S(2)}) %all-to-all-start.2) | async-done | bytes 1048608 | tf_op jit(solution)/shard_map/all_to_all | solution.py:618
  96.4 0.6 pick.3
  97.0 3.1 %collective-permute-start.2 = (bf16[4,2,32,512]{3,2,1,0:T(8,128)(2,1)S(1)}, bf16[4,2,32,512]{3,2,1,0:T(8,128)(2,1)S(1)}, u32[]{:S(2)}, u32[]{:S(2)}) collective-permute-start(bf16[4,2,32,512]{3,2,1,0:T(8,128)(2,1)S(1)} %get-tuple-element.27.near_ref), channel_id=1, source_target_pairs={{0,16},{2,18},{4,20},{6,22},{8,24},{10,26},{12,28},{14,30},{16,0},... | collective-permute-start | bytes 786440 | tf_op jit(solution)/shard_map/ppermute | solution.py:636
  100.1 0.1 collective-permute-start.18
  100.1 15.8 %collective-permute-done.2.far_ref = bf16[4,2,32,512]{3,2,1,0:T(8,128)(2,1)S(1)} collective-permute-done((bf16[4,2,32,512]{3,2,1,0:T(8,128)(2,1)S(1)}, bf16[4,2,32,512]{3,2,1,0:T(8,128)(2,1)S(1)}, u32[]{:S(2)}, u32[]{:S(2)}) %collective-permute-start.2) | collective-permute-done | bytes 262176 | tf_op jit(solution)/shard_map/ppermute | solution.py:636
  116.0 0.9 build.4
  116.9 3.2 %collective-permute-start.3 = (bf16[3,32,512]{2,1,0:T(8,128)(2,1)S(1)}, bf16[3,32,512]{2,1,0:T(8,128)(2,1)S(1)}, u32[]{:S(2)}, u32[]{:S(2)}) collective-permute-start(bf16[3,32,512]{2,1,0:T(8,128)(2,1)S(1)} %get-tuple-element.29), channel_id=1, source_target_pairs={{0,2},{2,0},{4,6},{6,4},{8,10},{10,8},{12,14},{14,12},{16,18},{18,... | collective-permute-start | bytes 294920 | tf_op jit(solution)/shard_map/ppermute | solution.py:646
  120.1 0.0 collective-permute-start.4
  120.1 1.3 collective-permute-start.5
  121.4 0.3 collective-permute-done.18.far_ref
  121.6 2.5 %collective-permute-start.6 = (bf16[3,32,512]{2,1,0:T(8,128)(2,1)S(1)}, bf16[3,32,512]{2,1,0:T(8,128)(2,1)S(1)}, u32[]{:S(2)}, u32[]{:S(2)}) collective-permute-start(bf16[3,32,512]{2,1,0:T(8,128)(2,1)S(1)} %get-tuple-element.32), channel_id=1, source_target_pairs={{0,8},{2,10},{4,12},{6,14},{8,0},{10,2},{12,4},{14,6},{16,24},{18,... | collective-permute-start | bytes 294920 | tf_op jit(solution)/shard_map/ppermute | solution.py:646
  124.1 0.0 collective-permute-done.3.refs_3_
  124.1 1.8 %collective-permute-start.7 = (bf16[3,32,512]{2,1,0:T(8,128)(2,1)S(1)}, bf16[3,32,512]{2,1,0:T(8,128)(2,1)S(1)}, u32[]{:S(2)}, u32[]{:S(2)}) collective-permute-start(bf16[3,32,512]{2,1,0:T(8,128)(2,1)S(1)} %get-tuple-element.33), channel_id=1, source_target_pairs={{0,10},{2,8},{4,14},{6,12},{8,2},{10,0},{12,6},{14,4},{16,26},{18,... | collective-permute-start | bytes 294920 | tf_op jit(solution)/shard_map/ppermute | solution.py:646
  126.0 0.9 build.5
  126.8 0.0 collective-permute-done.4.refs_4_
  126.8 0.9 collective-permute-start.8
  127.7 0.0 collective-permute-done.5.refs_5_
  127.7 1.2 collective-permute-start.9
  128.9 3.1 %collective-permute-start.10 = (bf16[3,32,512]{2,1,0:T(8,128)(2,1)S(1)}, bf16[3,32,512]{2,1,0:T(8,128)(2,1)S(1)}, u32[]{:S(2)}, u32[]{:S(2)}) collective-permute-start(bf16[3,32,512]{2,1,0:T(8,128)(2,1)S(1)} %get-tuple-element.28.refs_2_), channel_id=1, source_target_pairs={{1,0},{0,1},{3,2},{2,3},{5,4},{4,5},{7,6},{6,7},{9,8},{8,9},{11,10... | collective-permute-start | bytes 294920 | tf_op jit(solution)/shard_map/ppermute | solution.py:624
  132.0 0.7 collective-permute-start.19
  132.7 0.6 collective-permute-start.20
  133.3 0.2 collective-permute-done.9.refs_9_
  133.5 2.8 %collective-permute-start.21 = (bf16[3,32,512]{2,1,0:T(8,128)(2,1)S(1)}, bf16[3,32,512]{2,1,0:T(8,128)(2,1)S(1)}, u32[]{:S(2)}, u32[]{:S(2)}) collective-permute-start(bf16[3,32,512]{2,1,0:T(8,128)(2,1)S(1)} %get-tuple-element.40), channel_id=1, source_target_pairs={{0,6},{2,4},{4,2},{6,0},{8,14},{10,12},{12,10},{14,8},{16,22},{18,... | collective-permute-start | bytes 294920 | tf_op jit(solution)/shard_map/ppermute | solution.py:646
  136.3 0.0 collective-permute-start.22
  136.3 1.0 collective-permute-done.19.refs_19_
  137.3 0.9 collective-permute-start.23
  138.3 1.6 collective-permute-start.24
  139.9 1.9 %collective-permute-start.25 = (bf16[3,32,512]{2,1,0:T(8,128)(2,1)S(1)}, bf16[3,32,512]{2,1,0:T(8,128)(2,1)S(1)}, u32[]{:S(2)}, u32[]{:S(2)}) collective-permute-start(bf16[3,32,512]{2,1,0:T(8,128)(2,1)S(1)} %get-tuple-element.44), channel_id=1, source_target_pairs={{0,14},{2,12},{4,10},{6,8},{8,6},{10,4},{12,2},{14,0},{16,30},{18,... | collective-permute-start | bytes 294920 | tf_op jit(solution)/shard_map/ppermute | solution.py:646
  141.8 3.4 %collective-permute-start.26 = (bf16[3,32,512]{2,1,0:T(8,128)(2,1)S(1)}, bf16[3,32,512]{2,1,0:T(8,128)(2,1)S(1)}, u32[]{:S(2)}, u32[]{:S(2)}) collective-permute-start(bf16[3,32,512]{2,1,0:T(8,128)(2,1)S(1)} %get-tuple-element.37.refs_18_), channel_id=1, source_target_pairs={{1,0},{0,1},{3,2},{2,3},{5,4},{4,5},{7,6},{6,7},{9,8},{8,9},{11,10... | collective-permute-start | bytes 294920 | tf_op jit(solution)/shard_map/ppermute | solution.py:624
  145.1 1.2 collective-permute-start.11
  146.3 1.6 collective-permute-start.12
  147.9 1.9 %collective-permute-start.13 = (bf16[3,32,512]{2,1,0:T(8,128)(2,1)S(1)}, bf16[3,32,512]{2,1,0:T(8,128)(2,1)S(1)}, u32[]{:S(2)}, u32[]{:S(2)}) collective-permute-start(bf16[3,32,512]{2,1,0:T(8,128)(2,1)S(1)} %collective-permute-done.5.refs_5_), channel_id=1, source_target_pairs={{1,0},{0,1},{3,2},{2,3},{5,4},{4,5},{7,6},{6,7},{9,8},{8,9},{11,10... | collective-permute-start | bytes 294920 | tf_op jit(solution)/shard_map/ppermute | solution.py:624
  149.8 0.0 collective-permute-start.14
  149.8 0.5 collective-permute-start.15
  150.3 0.1 collective-permute-start.16
  150.4 0.4 collective-permute-done.13.refs_13_
  150.8 0.4 collective-permute-start.17
  151.1 0.0 collective-permute-done.14.refs_14_
  151.1 0.2 collective-permute-start.27
  151.3 0.0 collective-permute-done.15.refs_15_
  151.3 0.4 collective-permute-start.28
  151.6 1.1 mark.1.t
  152.8 0.2 collective-permute-start.29
  153.0 0.4 collective-permute-start.30
  153.4 0.2 collective-permute-start.31
  153.5 0.4 collective-permute-start.32
  153.9 0.2 collective-permute-start.33
  154.0 9.9 %inverse.1 = (bf16[512,512]{1,0:T(8,128)(2,1)S(1)}, f32[36,256,512]{2,1,0:T(8,128)S(1)}) custom-call(s32[8]{0:T(128)S(1)} %mark.1.t, bf16[8,7,32,512]{3,2,1,0:T(8,128)(2,1)S(1)} %all-to-all-done.1.refs_0_, bf16[8,7,32,512]{3,2,1,0:T(8,128)(2,1)} %collective-permute-done.1.refs_1_, f32[36,256,512]{2,1,0:T(8,128)} %bitcast.4), custom_call_target="tpu_custom_call" | custom-call | flops 16106127360 | bytes 1048576 | tf_op jit(solution)/shard_map/inverse/pallas_call | solution.py:454
  164.0 12.3 %update.1 = f32[36,256,512]{2,1,0:T(8,128)} custom-call(s32[40]{0:T(128)S(1)} %copy-done.1, f32[36,256,512]{2,1,0:T(8,128)S(1)} %get-tuple-element.25.tiles, bf16[512,512]{1,0:T(8,128)(2,1)S(1)} %get-tuple-element.26.inv, bf16[8,7,32,512]{3,2,1,0:T(8,128)(2,1)S(1)} %all-to-all-done.1.refs_0_, bf16[8,7,32,512]{3,2,1,0:T(8,128)(2,1)} %collective-permute-done.1.refs_1_, ...), custom_call_target="tpu_custom_call" | custom-call | tf_op jit(solution)/shard_map/update/pallas_call | solution.py:587
  (29 shorter events, 0.1 us)
Async XLA Ops:
  0.0 55.2 %copy-start.3 = (s32[16]{0:T(128)S(1)}, s32[16]{0:T(128)}, u32[]{:S(2)}) copy-start(s32[16]{0:T(128)} %owner.5) | copy-start | bytes 196
  0.0 0.7 copy-start.2
  3.8 19.1 %all-to-all-start = ((bf16[8,4,32,512]{3,2,1,0:T(8,128)(2,1)}), bf16[8,4,32,512]{3,2,1,0:T(8,128)(2,1)S(1)}, u32[]{:S(2)}, u32[]{:S(2)}) async-start(bf16[8,4,32,512]{3,2,1,0:T(8,128)(2,1)} %extract.2), calls=%async_computation | async-start | bytes 2097152 | tf_op jit(solution)/shard_map/all_to_all | solution.py:618
  23.0 0.6 copy-start
  23.6 72.8 %copy-start.1 = (s32[40]{0:T(128)S(1)}, s32[40]{0:T(128)}, u32[]{:S(2)}) copy-start(s32[40]{0:T(128)} %table.1.t) | copy-start | bytes 484
  24.2 24.0 %collective-permute-start = (bf16[4,4,32,512]{3,2,1,0:T(8,128)(2,1)S(1)}, bf16[4,4,32,512]{3,2,1,0:T(8,128)(2,1)S(1)}, u32[]{:S(2)}, u32[]{:S(2)}) collective-permute-start(bf16[4,4,32,512]{3,2,1,0:T(8,128)(2,1)S(1)} %pick.2.near_ref), channel_id=1, source_target_pairs={{0,16},{2,18},{4,20},{6,22},{8,24},{10,26},{12,28},{14,30},{16,0},... | collective-permute-start | bytes 1572872 | tf_op jit(solution)/shard_map/ppermute | solution.py:636
  50.4 27.5 %all-to-all-start.1 = ((bf16[8,7,32,512]{3,2,1,0:T(8,128)(2,1)}), bf16[8,7,32,512]{3,2,1,0:T(8,128)(2,1)S(1)}, u32[]{:S(2)}, u32[]{:S(2)}) async-start(bf16[8,7,32,512]{3,2,1,0:T(8,128)(2,1)} %build.3), calls=%async_computation.1 | async-start | bytes 3670016 | tf_op jit(solution)/shard_map/all_to_all | solution.py:618
  78.0 18.4 %all-to-all-start.2 = ((bf16[8,4,32,512]{3,2,1,0:T(8,128)(2,1)}), bf16[8,4,32,512]{3,2,1,0:T(8,128)(2,1)S(1)}, u32[]{:S(2)}, u32[]{:S(2)}) async-start(bf16[8,4,32,512]{3,2,1,0:T(8,128)(2,1)} %extract.3), calls=%async_computation.2 | async-start | bytes 2097152 | tf_op jit(solution)/shard_map/all_to_all | solution.py:618
  82.7 71.2 %collective-permute-start.1 = (bf16[8,7,32,512]{3,2,1,0:T(8,128)(2,1)S(1)}, bf16[8,7,32,512]{3,2,1,0:T(8,128)(2,1)}, u32[]{:S(2)}, u32[]{:S(2)}) collective-permute-start(bf16[8,7,32,512]{3,2,1,0:T(8,128)(2,1)S(1)} %all-to-all-done.1.refs_0_), channel_id=1, source_target_pairs={{1,0},{0,1},{3,2},{2,3},{5,4},{4,5},{7,6},{6,7},{9,8},{8,9},{11,10... | collective-permute-start | bytes 5505032 | tf_op jit(solution)/shard_map/ppermute | solution.py:624
  97.0 19.0 %collective-permute-start.2 = (bf16[4,2,32,512]{3,2,1,0:T(8,128)(2,1)S(1)}, bf16[4,2,32,512]{3,2,1,0:T(8,128)(2,1)S(1)}, u32[]{:S(2)}, u32[]{:S(2)}) collective-permute-start(bf16[4,2,32,512]{3,2,1,0:T(8,128)(2,1)S(1)} %get-tuple-element.27.near_ref), channel_id=1, source_target_pairs={{0,16},{2,18},{4,20},{6,22},{8,24},{10,26},{12,28},{14,30},{16,0},... | collective-permute-start | bytes 786440 | tf_op jit(solution)/shard_map/ppermute | solution.py:636
  100.1 21.5 %collective-permute-start.18 = (bf16[4,2,32,512]{3,2,1,0:T(8,128)(2,1)S(1)}, bf16[4,2,32,512]{3,2,1,0:T(8,128)(2,1)S(1)}, u32[]{:S(2)}, u32[]{:S(2)}) collective-permute-start(bf16[4,2,32,512]{3,2,1,0:T(8,128)(2,1)S(1)} %get-tuple-element.36.near_ref), channel_id=1, source_target_pairs={{0,16},{2,18},{4,20},{6,22},{8,24},{10,26},{12,28},{14,30},{16,0},... | collective-permute-start | bytes 786440 | tf_op jit(solution)/shard_map/ppermute | solution.py:636
  116.9 7.3 %collective-permute-start.3 = (bf16[3,32,512]{2,1,0:T(8,128)(2,1)S(1)}, bf16[3,32,512]{2,1,0:T(8,128)(2,1)S(1)}, u32[]{:S(2)}, u32[]{:S(2)}) collective-permute-start(bf16[3,32,512]{2,1,0:T(8,128)(2,1)S(1)} %get-tuple-element.29), channel_id=1, source_target_pairs={{0,2},{2,0},{4,6},{6,4},{8,10},{10,8},{12,14},{14,12},{16,18},{18,... | collective-permute-start | bytes 294920 | tf_op jit(solution)/shard_map/ppermute | solution.py:646
  120.1 6.7 %collective-permute-start.4 = (bf16[3,32,512]{2,1,0:T(8,128)(2,1)S(1)}, bf16[3,32,512]{2,1,0:T(8,128)(2,1)S(1)}, u32[]{:S(2)}, u32[]{:S(2)}) collective-permute-start(bf16[3,32,512]{2,1,0:T(8,128)(2,1)S(1)} %get-tuple-element.30), channel_id=1, source_target_pairs={{0,4},{2,6},{4,0},{6,2},{8,12},{10,14},{12,8},{14,10},{16,20},{18,... | collective-permute-start | bytes 294920 | tf_op jit(solution)/shard_map/ppermute | solution.py:646
  120.1 7.6 %collective-permute-start.5 = (bf16[3,32,512]{2,1,0:T(8,128)(2,1)S(1)}, bf16[3,32,512]{2,1,0:T(8,128)(2,1)S(1)}, u32[]{:S(2)}, u32[]{:S(2)}) collective-permute-start(bf16[3,32,512]{2,1,0:T(8,128)(2,1)S(1)} %get-tuple-element.31), channel_id=1, source_target_pairs={{0,6},{2,4},{4,2},{6,0},{8,14},{10,12},{12,10},{14,8},{16,22},{18,... | collective-permute-start | bytes 294920 | tf_op jit(solution)/shard_map/ppermute | solution.py:646
  121.6 7.3 %collective-permute-start.6 = (bf16[3,32,512]{2,1,0:T(8,128)(2,1)S(1)}, bf16[3,32,512]{2,1,0:T(8,128)(2,1)S(1)}, u32[]{:S(2)}, u32[]{:S(2)}) collective-permute-start(bf16[3,32,512]{2,1,0:T(8,128)(2,1)S(1)} %get-tuple-element.32), channel_id=1, source_target_pairs={{0,8},{2,10},{4,12},{6,14},{8,0},{10,2},{12,4},{14,6},{16,24},{18,... | collective-permute-start | bytes 294920 | tf_op jit(solution)/shard_map/ppermute | solution.py:646
  124.1 7.9 %collective-permute-start.7 = (bf16[3,32,512]{2,1,0:T(8,128)(2,1)S(1)}, bf16[3,32,512]{2,1,0:T(8,128)(2,1)S(1)}, u32[]{:S(2)}, u32[]{:S(2)}) collective-permute-start(bf16[3,32,512]{2,1,0:T(8,128)(2,1)S(1)} %get-tuple-element.33), channel_id=1, source_target_pairs={{0,10},{2,8},{4,14},{6,12},{8,2},{10,0},{12,6},{14,4},{16,26},{18,... | collective-permute-start | bytes 294920 | tf_op jit(solution)/shard_map/ppermute | solution.py:646
  126.8 5.9 %collective-permute-start.8 = (bf16[3,32,512]{2,1,0:T(8,128)(2,1)S(1)}, bf16[3,32,512]{2,1,0:T(8,128)(2,1)S(1)}, u32[]{:S(2)}, u32[]{:S(2)}) collective-permute-start(bf16[3,32,512]{2,1,0:T(8,128)(2,1)S(1)} %get-tuple-element.34), channel_id=1, source_target_pairs={{0,12},{2,14},{4,8},{6,10},{8,4},{10,6},{12,0},{14,2},{16,28},{18,... | collective-permute-start | bytes 294920 | tf_op jit(solution)/shard_map/ppermute | solution.py:646
  127.7 5.8 %collective-permute-start.9 = (bf16[3,32,512]{2,1,0:T(8,128)(2,1)S(1)}, bf16[3,32,512]{2,1,0:T(8,128)(2,1)S(1)}, u32[]{:S(2)}, u32[]{:S(2)}) collective-permute-start(bf16[3,32,512]{2,1,0:T(8,128)(2,1)S(1)} %get-tuple-element.35), channel_id=1, source_target_pairs={{0,14},{2,12},{4,10},{6,8},{8,6},{10,4},{12,2},{14,0},{16,30},{18,... | collective-permute-start | bytes 294920 | tf_op jit(solution)/shard_map/ppermute | solution.py:646
  128.9 7.4 %collective-permute-start.10 = (bf16[3,32,512]{2,1,0:T(8,128)(2,1)S(1)}, bf16[3,32,512]{2,1,0:T(8,128)(2,1)S(1)}, u32[]{:S(2)}, u32[]{:S(2)}) collective-permute-start(bf16[3,32,512]{2,1,0:T(8,128)(2,1)S(1)} %get-tuple-element.28.refs_2_), channel_id=1, source_target_pairs={{1,0},{0,1},{3,2},{2,3},{5,4},{4,5},{7,6},{6,7},{9,8},{8,9},{11,10... | collective-permute-start | bytes 294920 | tf_op jit(solution)/shard_map/ppermute | solution.py:624
  132.0 5.3 %collective-permute-start.19 = (bf16[3,32,512]{2,1,0:T(8,128)(2,1)S(1)}, bf16[3,32,512]{2,1,0:T(8,128)(2,1)S(1)}, u32[]{:S(2)}, u32[]{:S(2)}) collective-permute-start(bf16[3,32,512]{2,1,0:T(8,128)(2,1)S(1)} %get-tuple-element.38), channel_id=1, source_target_pairs={{0,2},{2,0},{4,6},{6,4},{8,10},{10,8},{12,14},{14,12},{16,18},{18,... | collective-permute-start | bytes 294920 | tf_op jit(solution)/shard_map/ppermute | solution.py:646
  132.7 5.6 %collective-permute-start.20 = (bf16[3,32,512]{2,1,0:T(8,128)(2,1)S(1)}, bf16[3,32,512]{2,1,0:T(8,128)(2,1)S(1)}, u32[]{:S(2)}, u32[]{:S(2)}) collective-permute-start(bf16[3,32,512]{2,1,0:T(8,128)(2,1)S(1)} %get-tuple-element.39), channel_id=1, source_target_pairs={{0,4},{2,6},{4,0},{6,2},{8,12},{10,14},{12,8},{14,10},{16,20},{18,... | collective-permute-start | bytes 294920 | tf_op jit(solution)/shard_map/ppermute | solution.py:646
  133.5 6.3 %collective-permute-start.21 = (bf16[3,32,512]{2,1,0:T(8,128)(2,1)S(1)}, bf16[3,32,512]{2,1,0:T(8,128)(2,1)S(1)}, u32[]{:S(2)}, u32[]{:S(2)}) collective-permute-start(bf16[3,32,512]{2,1,0:T(8,128)(2,1)S(1)} %get-tuple-element.40), channel_id=1, source_target_pairs={{0,6},{2,4},{4,2},{6,0},{8,14},{10,12},{12,10},{14,8},{16,22},{18,... | collective-permute-start | bytes 294920 | tf_op jit(solution)/shard_map/ppermute | solution.py:646
  136.3 5.5 %collective-permute-start.22 = (bf16[3,32,512]{2,1,0:T(8,128)(2,1)S(1)}, bf16[3,32,512]{2,1,0:T(8,128)(2,1)S(1)}, u32[]{:S(2)}, u32[]{:S(2)}) collective-permute-start(bf16[3,32,512]{2,1,0:T(8,128)(2,1)S(1)} %get-tuple-element.41), channel_id=1, source_target_pairs={{0,8},{2,10},{4,12},{6,14},{8,0},{10,2},{12,4},{14,6},{16,24},{18,... | collective-permute-start | bytes 294920 | tf_op jit(solution)/shard_map/ppermute | solution.py:646
  137.3 7.8 %collective-permute-start.23 = (bf16[3,32,512]{2,1,0:T(8,128)(2,1)S(1)}, bf16[3,32,512]{2,1,0:T(8,128)(2,1)S(1)}, u32[]{:S(2)}, u32[]{:S(2)}) collective-permute-start(bf16[3,32,512]{2,1,0:T(8,128)(2,1)S(1)} %get-tuple-element.42), channel_id=1, source_target_pairs={{0,10},{2,8},{4,14},{6,12},{8,2},{10,0},{12,6},{14,4},{16,26},{18,... | collective-permute-start | bytes 294920 | tf_op jit(solution)/shard_map/ppermute | solution.py:646
  138.3 8.0 %collective-permute-start.24 = (bf16[3,32,512]{2,1,0:T(8,128)(2,1)S(1)}, bf16[3,32,512]{2,1,0:T(8,128)(2,1)S(1)}, u32[]{:S(2)}, u32[]{:S(2)}) collective-permute-start(bf16[3,32,512]{2,1,0:T(8,128)(2,1)S(1)} %get-tuple-element.43), channel_id=1, source_target_pairs={{0,12},{2,14},{4,8},{6,10},{8,4},{10,6},{12,0},{14,2},{16,28},{18,... | collective-permute-start | bytes 294920 | tf_op jit(solution)/shard_map/ppermute | solution.py:646
  139.9 8.1 %collective-permute-start.25 = (bf16[3,32,512]{2,1,0:T(8,128)(2,1)S(1)}, bf16[3,32,512]{2,1,0:T(8,128)(2,1)S(1)}, u32[]{:S(2)}, u32[]{:S(2)}) collective-permute-start(bf16[3,32,512]{2,1,0:T(8,128)(2,1)S(1)} %get-tuple-element.44), channel_id=1, source_target_pairs={{0,14},{2,12},{4,10},{6,8},{8,6},{10,4},{12,2},{14,0},{16,30},{18,... | collective-permute-start | bytes 294920 | tf_op jit(solution)/shard_map/ppermute | solution.py:646
  141.8 8.0 %collective-permute-start.26 = (bf16[3,32,512]{2,1,0:T(8,128)(2,1)S(1)}, bf16[3,32,512]{2,1,0:T(8,128)(2,1)S(1)}, u32[]{:S(2)}, u32[]{:S(2)}) collective-permute-start(bf16[3,32,512]{2,1,0:T(8,128)(2,1)S(1)} %get-tuple-element.37.refs_18_), channel_id=1, source_target_pairs={{1,0},{0,1},{3,2},{2,3},{5,4},{4,5},{7,6},{6,7},{9,8},{8,9},{11,10... | collective-permute-start | bytes 294920 | tf_op jit(solution)/shard_map/ppermute | solution.py:624
  145.1 4.7 %collective-permute-start.11 = (bf16[3,32,512]{2,1,0:T(8,128)(2,1)S(1)}, bf16[3,32,512]{2,1,0:T(8,128)(2,1)S(1)}, u32[]{:S(2)}, u32[]{:S(2)}) collective-permute-start(bf16[3,32,512]{2,1,0:T(8,128)(2,1)S(1)} %collective-permute-done.3.refs_3_), channel_id=1, source_target_pairs={{1,0},{0,1},{3,2},{2,3},{5,4},{4,5},{7,6},{6,7},{9,8},{8,9},{11,10... | collective-permute-start | bytes 294920 | tf_op jit(solution)/shard_map/ppermute | solution.py:624
  146.3 4.0 %collective-permute-start.12 = (bf16[3,32,512]{2,1,0:T(8,128)(2,1)S(1)}, bf16[3,32,512]{2,1,0:T(8,128)(2,1)S(1)}, u32[]{:S(2)}, u32[]{:S(2)}) collective-permute-start(bf16[3,32,512]{2,1,0:T(8,128)(2,1)S(1)} %collective-permute-done.4.refs_4_), channel_id=1, source_target_pairs={{1,0},{0,1},{3,2},{2,3},{5,4},{4,5},{7,6},{6,7},{9,8},{8,9},{11,10... | collective-permute-start | bytes 294920 | tf_op jit(solution)/shard_map/ppermute | solution.py:624
  147.9 2.8 %collective-permute-start.13 = (bf16[3,32,512]{2,1,0:T(8,128)(2,1)S(1)}, bf16[3,32,512]{2,1,0:T(8,128)(2,1)S(1)}, u32[]{:S(2)}, u32[]{:S(2)}) collective-permute-start(bf16[3,32,512]{2,1,0:T(8,128)(2,1)S(1)} %collective-permute-done.5.refs_5_), channel_id=1, source_target_pairs={{1,0},{0,1},{3,2},{2,3},{5,4},{4,5},{7,6},{6,7},{9,8},{8,9},{11,10... | collective-permute-start | bytes 294920 | tf_op jit(solution)/shard_map/ppermute | solution.py:624
  149.8 1.3 collective-permute-start.14
  149.8 1.5 collective-permute-start.15
  150.3 2.4 %collective-permute-start.16 = (bf16[3,32,512]{2,1,0:T(8,128)(2,1)S(1)}, bf16[3,32,512]{2,1,0:T(8,128)(2,1)S(1)}, u32[]{:S(2)}, u32[]{:S(2)}) collective-permute-start(bf16[3,32,512]{2,1,0:T(8,128)(2,1)S(1)} %collective-permute-done.8.refs_8_), channel_id=1, source_target_pairs={{1,0},{0,1},{3,2},{2,3},{5,4},{4,5},{7,6},{6,7},{9,8},{8,9},{11,10... | collective-permute-start | bytes 294920 | tf_op jit(solution)/shard_map/ppermute | solution.py:624
  150.8 2.3 %collective-permute-start.17 = (bf16[3,32,512]{2,1,0:T(8,128)(2,1)S(1)}, bf16[3,32,512]{2,1,0:T(8,128)(2,1)S(1)}, u32[]{:S(2)}, u32[]{:S(2)}) collective-permute-start(bf16[3,32,512]{2,1,0:T(8,128)(2,1)S(1)} %collective-permute-done.9.refs_9_), channel_id=1, source_target_pairs={{1,0},{0,1},{3,2},{2,3},{5,4},{4,5},{7,6},{6,7},{9,8},{8,9},{11,10... | collective-permute-start | bytes 294920 | tf_op jit(solution)/shard_map/ppermute | solution.py:624
  151.1 2.3 %collective-permute-start.27 = (bf16[3,32,512]{2,1,0:T(8,128)(2,1)S(1)}, bf16[3,32,512]{2,1,0:T(8,128)(2,1)S(1)}, u32[]{:S(2)}, u32[]{:S(2)}) collective-permute-start(bf16[3,32,512]{2,1,0:T(8,128)(2,1)S(1)} %collective-permute-done.19.refs_19_), channel_id=1, source_target_pairs={{1,0},{0,1},{3,2},{2,3},{5,4},{4,5},{7,6},{6,7},{9,8},{8,9},{11,10... | collective-permute-start | bytes 294920 | tf_op jit(solution)/shard_map/ppermute | solution.py:624
  151.3 2.3 %collective-permute-start.28 = (bf16[3,32,512]{2,1,0:T(8,128)(2,1)S(1)}, bf16[3,32,512]{2,1,0:T(8,128)(2,1)S(1)}, u32[]{:S(2)}, u32[]{:S(2)}) collective-permute-start(bf16[3,32,512]{2,1,0:T(8,128)(2,1)S(1)} %collective-permute-done.20.refs_20_), channel_id=1, source_target_pairs={{1,0},{0,1},{3,2},{2,3},{5,4},{4,5},{7,6},{6,7},{9,8},{8,9},{11,10... | collective-permute-start | bytes 294920 | tf_op jit(solution)/shard_map/ppermute | solution.py:624
  152.8 11.1 %collective-permute-start.29 = (bf16[3,32,512]{2,1,0:T(8,128)(2,1)S(1)}, bf16[3,32,512]{2,1,0:T(8,128)(2,1)S(1)}, u32[]{:S(2)}, u32[]{:S(2)}) collective-permute-start(bf16[3,32,512]{2,1,0:T(8,128)(2,1)S(1)} %collective-permute-done.21.refs_21_), channel_id=1, source_target_pairs={{1,0},{0,1},{3,2},{2,3},{5,4},{4,5},{7,6},{6,7},{9,8},{8,9},{11,10... | collective-permute-start | bytes 294920 | tf_op jit(solution)/shard_map/ppermute | solution.py:624
  153.0 10.9 %collective-permute-start.30 = (bf16[3,32,512]{2,1,0:T(8,128)(2,1)S(1)}, bf16[3,32,512]{2,1,0:T(8,128)(2,1)S(1)}, u32[]{:S(2)}, u32[]{:S(2)}) collective-permute-start(bf16[3,32,512]{2,1,0:T(8,128)(2,1)S(1)} %collective-permute-done.22.refs_22_), channel_id=1, source_target_pairs={{1,0},{0,1},{3,2},{2,3},{5,4},{4,5},{7,6},{6,7},{9,8},{8,9},{11,10... | collective-permute-start | bytes 294920 | tf_op jit(solution)/shard_map/ppermute | solution.py:624
  153.4 10.6 %collective-permute-start.31 = (bf16[3,32,512]{2,1,0:T(8,128)(2,1)S(1)}, bf16[3,32,512]{2,1,0:T(8,128)(2,1)S(1)}, u32[]{:S(2)}, u32[]{:S(2)}) collective-permute-start(bf16[3,32,512]{2,1,0:T(8,128)(2,1)S(1)} %collective-permute-done.23.refs_23_), channel_id=1, source_target_pairs={{1,0},{0,1},{3,2},{2,3},{5,4},{4,5},{7,6},{6,7},{9,8},{8,9},{11,10... | collective-permute-start | bytes 294920 | tf_op jit(solution)/shard_map/ppermute | solution.py:624
  153.5 10.4 %collective-permute-start.32 = (bf16[3,32,512]{2,1,0:T(8,128)(2,1)S(1)}, bf16[3,32,512]{2,1,0:T(8,128)(2,1)S(1)}, u32[]{:S(2)}, u32[]{:S(2)}) collective-permute-start(bf16[3,32,512]{2,1,0:T(8,128)(2,1)S(1)} %collective-permute-done.24.refs_24_), channel_id=1, source_target_pairs={{1,0},{0,1},{3,2},{2,3},{5,4},{4,5},{7,6},{6,7},{9,8},{8,9},{11,10... | collective-permute-start | bytes 294920 | tf_op jit(solution)/shard_map/ppermute | solution.py:624
  153.9 10.1 %collective-permute-start.33 = (bf16[3,32,512]{2,1,0:T(8,128)(2,1)S(1)}, bf16[3,32,512]{2,1,0:T(8,128)(2,1)S(1)}, u32[]{:S(2)}, u32[]{:S(2)}) collective-permute-start(bf16[3,32,512]{2,1,0:T(8,128)(2,1)S(1)} %collective-permute-done.25.refs_25_), channel_id=1, source_target_pairs={{1,0},{0,1},{3,2},{2,3},{5,4},{4,5},{7,6},{6,7},{9,8},{8,9},{11,10... | collective-permute-start | bytes 294920 | tf_op jit(solution)/shard_map/ppermute | solution.py:624

commit v6 on v5

--- a/solution.py
+++ b/solution.py
@@ -137,9 +137,9 @@
         self.half_tri = tri // 2
         self.piece = strip // self.half_tri
         quarter = self.half_group // 4
-        self.wides = [2 * quarter, quarter, quarter]
-        self.firsts = [0, 2 * quarter, 3 * quarter]
-        self.spreads = [[0], [1, 2]]
+        self.wides = [quarter, quarter, 2 * quarter]
+        self.firsts = [0, quarter, 2 * quarter]
+        self.spreads = [[0, 1], [2]]
         self.o_sub = 0
         self.o_diag = 1
         self.o_me = 2
@@ -314,53 +314,60 @@
     )(table, in_vmem(spread))
 
 
-def build_call(p, table, near, far, wide, with_pivot, apart):
+def build_call(p, table, near, far, wide, with_pivot):
     rows = 3 * wide + (1 if with_pivot else 0)
 
     def kernel(t, near_ref, far_ref, *outs):
-        def part(group, first, count, n, place):
+        def part(group, first, count, out, place):
             here = t[p.o_here + group] == 1
-            at = pl.ds(place, count)
-
-            def store(value):
-                if apart:
-                    outs[n][at] = value
-                else:
-                    outs[0][n, at] = value
 
             @pl.when(here)
             def _():
-                store(near_ref[group, pl.ds(first, count)])
+                out[place : place + count] = near_ref[group, pl.ds(first, count)]
 
             @pl.when(jnp.logical_not(here))
             def _():
-                store(far_ref[group, pl.ds(first, count)])
-
-        for n in range(p.half_tri):
-            end = t[p.o_me] ^ n if apart else n
-            part(t[p.o_rg + end], 0, 2 * wide, n, 0)
-            part(t[p.o_cg + end], t[p.o_hf + end] * wide, wide, n, 2 * wide)
+                out[place : place + count] = far_ref[group, pl.ds(first, count)]
+
+        for n, out in enumerate(outs):
+            end = t[p.o_me] ^ n
+            part(t[p.o_rg + end], 0, 2 * wide, out, 0)
+            part(t[p.o_cg + end], t[p.o_hf + end] * wide, wide, out, 2 * wide)
             if with_pivot:
-                part(0, 0, 1, n, 3 * wide)
-
-    one = (rows, p.piece, p.order)
-    if apart:
-        out_shape = [pltpu.VMEM(one, jnp.bfloat16)] * p.half_tri
-    else:
-        out_shape = [pltpu.VMEM((p.half_tri,) + one, jnp.bfloat16)]
-    outs = pl.pallas_call(
-        kernel,
-        out_shape=out_shape,
+                part(0, 0, 1, out, 3 * wide)
+
+    return pl.pallas_call(
+        kernel,
+        out_shape=[pltpu.VMEM((rows, p.piece, p.order), jnp.bfloat16)] * p.half_tri,
         grid_spec=pltpu.PrefetchScalarGridSpec(
             num_scalar_prefetch=1,
             grid=(),
             in_specs=[IN_VMEM, IN_VMEM],
-            out_specs=[IN_VMEM] * len(out_shape),
+            out_specs=[IN_VMEM] * p.half_tri,
         ),
         compiler_params=limit(8),
         name="build",
     )(table, in_vmem(near), in_vmem(far))
-    return outs if apart else outs[0]
+
+
+def pack_call(p, table, pieces):
+    def kernel(t, *refs):
+        out = refs[-1]
+        for n in range(p.half_tri):
+            out[t[p.o_me] ^ n] = refs[n][...]
+
+    return pl.pallas_call(
+        kernel,
+        out_shape=pltpu.VMEM((p.half_tri,) + pieces[0].shape, jnp.bfloat16),
+        grid_spec=pltpu.PrefetchScalarGridSpec(
+            num_scalar_prefetch=1,
+            grid=(),
+            in_specs=[IN_VMEM] * p.half_tri,
+            out_specs=IN_VMEM,
+        ),
+        compiler_params=limit(8),
+        name="pack",
+    )(table, *[in_vmem(x) for x in pieces])
 
 
 def inverse_call(p, table, arrived, current):
@@ -475,28 +482,17 @@
     )(table, *[in_vmem(x) for x in arrived], in_hbm(current))
 
 
-def update_call(p, table, held, together, apart, inverse):
+def update_call(p, table, held, arrived, inverse):
     ring_size = 8
     chunks = len(p.wides)
     rows_in_box = p.per_group * p.half_group
 
     def kernel(t, tiles, inv, *refs):
-        sources = [list(refs[: p.subs])]
-        at = p.subs
-        loose = []
-        for _ in range(1, chunks):
-            loose.append(refs[at : at + p.subs * p.half_tri])
-            at += p.subs * p.half_tri
-        out, column, ring, ring_sems, rest_sem, *packed = refs[at:]
+        sources = [refs[k * p.subs : (k + 1) * p.subs] for k in range(chunks)]
+        out, column, ring, ring_sems, rest_sem = refs[chunks * p.subs :]
         sub = t[p.o_sub]
         diag = t[p.o_diag] == 1
         dead = t[p.o_dead] == 1
-
-        for k in range(chunks - 1):
-            for shift in range(p.subs):
-                for n in range(p.half_tri):
-                    packed[k][shift, t[p.o_me] ^ n] = loose[k][shift * p.half_tri + n][...]
-            sources.append([packed[k].at[shift] for shift in range(p.subs)])
 
         def strip_of(shift, chunk, place):
             return sources[chunk][shift][:, place].reshape(p.strip, p.order)
@@ -583,29 +579,29 @@
             if p.slots > rows_in_box:
                 rest.wait()
 
-    loose = [in_vmem(ref) for chunk in apart for shift in chunk for ref in shift]
     return pl.pallas_call(
         kernel,
         out_shape=jax.ShapeDtypeStruct(held.shape, jnp.float32),
         grid_spec=pltpu.PrefetchScalarGridSpec(
             num_scalar_prefetch=1,
             grid=(),
-            in_specs=[IN_VMEM] * (2 + p.subs + len(loose)),
+            in_specs=[IN_VMEM] * (2 + chunks * p.subs),
             out_specs=pl.BlockSpec(memory_space=pltpu.HBM),
             scratch_shapes=[
                 pltpu.VMEM((p.per_group, p.order, p.order), jnp.bfloat16),
                 pltpu.VMEM((ring_size, p.strip, p.order), jnp.float32),
                 pltpu.SemaphoreType.DMA((ring_size,)),
                 pltpu.SemaphoreType.DMA,
-            ]
-            + [
-                pltpu.VMEM((p.subs, p.half_tri) + chunk[0][0].shape, jnp.bfloat16)
-                for chunk in apart
             ],
         ),
-        compiler_params=limit(24),
+        compiler_params=limit(20),
         name="update",
-    )(table, in_vmem(held), in_vmem(inverse), *[in_vmem(ref) for ref in together], *loose)
+    )(
+        table,
+        in_vmem(held),
+        in_vmem(inverse),
+        *[in_vmem(ref) for chunk in arrived for ref in chunk],
+    )
 
 
 def planned(p, stored_tiles, cell_owner):
@@ -634,21 +630,19 @@
         near.extend(pick_call(p, table, spread, members))
     for chunk in range(chunks):
         far.append(lax.ppermute(near[chunk], "tri", swap))
-    built = build_call(p, table, near[0], far[0], p.wides[0], True, False)
-    whole = exchange(built)
-    together = arrivals(whole)
-    apart = []
-    for chunk in range(1, chunks):
-        built = build_call(p, table, near[chunk], far[chunk], p.wides[chunk], False, True)
-        loose = [built[0]]
+    arrived = []
+    for chunk in range(chunks):
+        built = build_call(p, table, near[chunk], far[chunk], p.wides[chunk], chunk == 0)
+        pieces = [built[0]]
         for n in range(1, p.half_tri):
             pairs = [(i, i ^ n) for i in range(p.tri)]
-            loose.append(lax.ppermute(built[n], "tri", pairs))
-        sides = [arrivals(x) for x in loose]
-        apart.append([[piece[shift] for piece in sides] for shift in range(p.subs)])
-    marked = mark_call(p, table)
-    inverse, held = inverse_call(p, marked, together, current)
-    return update_call(p, table, held, together, apart, inverse)[None]
+            pieces.append(lax.ppermute(built[n], "tri", pairs))
+        if chunk == 0:
+            table_after = mark_call(p, table)
+        packed = pack_call(p, table_after, pieces)
+        arrived.append(arrivals(packed))
+    inverse, held = inverse_call(p, table_after, arrived[0], current)
+    return update_call(p, table, held, arrived, inverse)[None]
 
 
 def shards(stored_tiles, cell_owner):

time: 177 us -> 172 us (0.972)
  starting transfers between devices: 54.4 us -> 50.6 us
  Pallas kernels: 35.9 us -> 33.4 us
    all_to_all x3 -> x2, waiting for transfers between devices: 45.1 us -> 10.7 us  [exchange(): lax.all_to_all(x, 'tri', split_axis=0, concat_axis=0, tiled=True, axis_in...]
    ppermute x14 -> x21, waiting for transfers between devices: 1.22 us -> 27.7 us  [planned(): pieces.append(lax.ppermute(built[n], 'tri', pairs))]
    ppermute x3, waiting for transfers between devices: 37.8 us -> 45.9 us  [planned(): far.append(lax.ppermute(near[chunk], 'tri', swap))]
    all_to_all x3 -> x2, starting transfers between devices: 14.8 us -> 9.53 us  [exchange(): lax.all_to_all(x, 'tri', split_axis=0, concat_axis=0, tiled=True, axis_in...]
    ppermute x14 -> x21, starting transfers between devices: 19.4 us -> 23.7 us  [planned(): pieces.append(lax.ppermute(built[n], 'tri', pairs))]
    ppermute x17 -> x3, starting transfers between devices: 14.6 us -> 12.5 us  [arrivals(): lax.ppermute(x, 'sub', [((i + shift) % p.subs, i) for i in range(p.subs)])]
    pallas_call x3 -> x6, Pallas kernels: 3.95 us -> 4.61 us  [the longest x3 2.76 us: build_call(): pl.pallas_call(kernel, out_shape=[pltpu.VMEM((rows, p.piece, p.order), jn...]
  transfers between devices with their start and end apart: 37 -> 29, of which waited for: 9 -> 10; matrix products, arithmetic and copies ran while one was open for 0% -> 0% of each run, Pallas kernels for 10% -> 11%
where the time goes in v6:
time: 172 us; the launch traced here: 171 us
  waiting for transfers between devices  84.3 us (49%)
  starting transfers between devices  50.6 us (29%)
  Pallas kernels  33.4 us (19%)
  local copies, waits for them, and re-layouts  2.7 us (2%)
    ppermute x3, waiting for transfers between devices, planned(): far.append(lax.ppermute(near[chunk], 'tri', swap))  45.9 us
    ppermute x21, waiting for transfers between devices, planned(): pieces.append(lax.ppermute(built[n], 'tri', pairs))  27.7 us
    ppermute x21, starting transfers between devices, planned(): pieces.append(lax.ppermute(built[n], 'tri', pairs))  23.7 us
    ppermute x3, starting transfers between devices, arrivals(): lax.ppermute(x, 'sub', [((i + shift) % p.subs, i) for i in range(p.subs)])  12.5 us
    all_to_all x2, waiting for transfers between devices, exchange(): lax.all_to_all(x, 'tri', split_axis=0, concat_axis=0, tiled=True, axis_in...  10.7 us
    pallas_call x1, Pallas kernels, update_call(): pl.pallas_call(kernel, out_shape=jax.ShapeDtypeStruct(held.shape, jnp.flo...  10.6 us
    all_to_all x2, starting transfers between devices, exchange(): lax.all_to_all(x, 'tri', split_axis=0, concat_axis=0, tiled=True, axis_in...  9.53 us
    pallas_call x1, Pallas kernels, inverse_call(): pl.pallas_call(kernel, out_shape=(square_shape, pltpu.VMEM(current.shape,...  8.36 us
  transfers between devices with their start and end apart: 29, of which 10 were waited for; matrix products, arithmetic and copies ran while one was open for 0% of the time, Pallas kernels for 11%

profile of v6, /device:TPU:1, one launch (start us, length us, event | category | flops | bytes accessed | tf_op | source)
XLA Modules:
  0.0 171.3 jit_solution(15257306572291807230)
XLA Ops:
  0.0 0.7 copy-done.4
  0.7 3.1 %extract.2 = bf16[8,4,32,512]{3,2,1,0:T(8,128)(2,1)} custom-call(s32[16]{0:T(128)S(1)} %copy-done.4, f32[36,256,512]{2,1,0:T(8,128)} %bitcast.2), custom_call_target="tpu_custom_call" | custom-call | tf_op jit(solution)/shard_map/extract/pallas_call | solution.py:275
  3.8 5.3 %all-to-all-start = ((bf16[8,4,32,512]{3,2,1,0:T(8,128)(2,1)}), bf16[8,4,32,512]{3,2,1,0:T(8,128)(2,1)S(1)}, u32[]{:S(2)}, u32[]{:S(2)}) async-start(bf16[8,4,32,512]{3,2,1,0:T(8,128)(2,1)} %extract.2), calls=%async_computation | async-start | bytes 2097152 | tf_op jit(solution)/shard_map/all_to_all | solution.py:614
  9.1 3.1 %extract.3 = bf16[8,4,32,512]{3,2,1,0:T(8,128)(2,1)} custom-call(s32[16]{0:T(128)S(1)} %copy-done.5, f32[36,256,512]{2,1,0:T(8,128)} %bitcast.3), custom_call_target="tpu_custom_call" | custom-call | tf_op jit(solution)/shard_map/extract/pallas_call | solution.py:275
  12.3 10.7 %all-to-all-done.spread_ref = bf16[8,4,32,512]{3,2,1,0:T(8,128)(2,1)S(1)} async-done(((bf16[8,4,32,512]{3,2,1,0:T(8,128)(2,1)}), bf16[8,4,32,512]{3,2,1,0:T(8,128)(2,1)S(1)}, u32[]{:S(2)}, u32[]{:S(2)}) %all-to-all-start) | async-done | bytes 1048608 | tf_op jit(solution)/shard_map/all_to_all | solution.py:614
  23.0 4.2 %all-to-all-start.1 = ((bf16[8,4,32,512]{3,2,1,0:T(8,128)(2,1)}), bf16[8,4,32,512]{3,2,1,0:T(8,128)(2,1)S(1)}, u32[]{:S(2)}, u32[]{:S(2)}) async-start(bf16[8,4,32,512]{3,2,1,0:T(8,128)(2,1)} %extract.3), calls=%async_computation.1 | async-start | bytes 2097152 | tf_op jit(solution)/shard_map/all_to_all | solution.py:614
  27.2 1.3 table.1.t
  28.5 0.0 copy-start
  28.5 0.6 copy-done
  29.2 0.6 pick.2
  29.8 2.4 %collective-permute-start = (bf16[4,2,32,512]{3,2,1,0:T(8,128)(2,1)S(1)}, bf16[4,2,32,512]{3,2,1,0:T(8,128)(2,1)S(1)}, u32[]{:S(2)}, u32[]{:S(2)}) collective-permute-start(bf16[4,2,32,512]{3,2,1,0:T(8,128)(2,1)S(1)} %get-tuple-element.33.near_ref), channel_id=1, source_target_pairs={{0,16},{2,18},{4,20},{6,22},{8,24},{10,26},{12,28},{14,30},{16,0},... | collective-permute-start | bytes 786440 | tf_op jit(solution)/shard_map/ppermute | solution.py:632
  32.1 11.4 %collective-permute-done.far_ref = bf16[4,2,32,512]{3,2,1,0:T(8,128)(2,1)S(1)} collective-permute-done((bf16[4,2,32,512]{3,2,1,0:T(8,128)(2,1)S(1)}, bf16[4,2,32,512]{3,2,1,0:T(8,128)(2,1)S(1)}, u32[]{:S(2)}, u32[]{:S(2)}) %collective-permute-start) | collective-permute-done | bytes 262176 | tf_op jit(solution)/shard_map/ppermute | solution.py:632
  43.5 0.7 copy-done.1
  44.2 1.0 build.3
  45.2 1.3 collective-permute-start.1
  46.5 1.2 collective-permute-start.2
  47.6 0.2 collective-permute-start.3
  47.9 4.4 %collective-permute-start.4 = (bf16[4,32,512]{2,1,0:T(8,128)(2,1)S(1)}, bf16[4,32,512]{2,1,0:T(8,128)(2,1)S(1)}, u32[]{:S(2)}, u32[]{:S(2)}) collective-permute-start(bf16[4,32,512]{2,1,0:T(8,128)(2,1)S(1)} %get-tuple-element.38), channel_id=1, source_target_pairs={{0,8},{2,10},{4,12},{6,14},{8,0},{10,2},{12,4},{14,6},{16,24},{18,... | collective-permute-start | bytes 393224 | tf_op jit(solution)/shard_map/ppermute | solution.py:639
  52.3 0.8 collective-permute-start.5
  53.1 0.0 collective-permute-done.1.refs_1_
  53.1 2.4 %collective-permute-start.6 = (bf16[4,32,512]{2,1,0:T(8,128)(2,1)S(1)}, bf16[4,32,512]{2,1,0:T(8,128)(2,1)S(1)}, u32[]{:S(2)}, u32[]{:S(2)}) collective-permute-start(bf16[4,32,512]{2,1,0:T(8,128)(2,1)S(1)} %get-tuple-element.40), channel_id=1, source_target_pairs={{0,12},{2,14},{4,8},{6,10},{8,4},{10,6},{12,0},{14,2},{16,28},{18,... | collective-permute-start | bytes 393224 | tf_op jit(solution)/shard_map/ppermute | solution.py:639
  55.5 1.2 collective-permute-start.7
  56.7 1.1 mark.1.t
  57.9 0.0 collective-permute-done.5.refs_5_
  57.9 3.8 %collective-permute-done.6.refs_6_ = bf16[4,32,512]{2,1,0:T(8,128)(2,1)S(1)} collective-permute-done((bf16[4,32,512]{2,1,0:T(8,128)(2,1)S(1)}, bf16[4,32,512]{2,1,0:T(8,128)(2,1)S(1)}, u32[]{:S(2)}, u32[]{:S(2)}) %collective-permute-start.6) | collective-permute-done | bytes 131104 | tf_op jit(solution)/shard_map/ppermute | solution.py:639
  61.7 1.7 %collective-permute-done.7.refs_7_ = bf16[4,32,512]{2,1,0:T(8,128)(2,1)S(1)} collective-permute-done((bf16[4,32,512]{2,1,0:T(8,128)(2,1)S(1)}, bf16[4,32,512]{2,1,0:T(8,128)(2,1)S(1)}, u32[]{:S(2)}, u32[]{:S(2)}) %collective-permute-start.7) | collective-permute-done | bytes 131104 | tf_op jit(solution)/shard_map/ppermute | solution.py:639
  63.5 0.6 pack.3.refs_0_
  64.1 3.7 %collective-permute-start.8 = (bf16[8,4,32,512]{3,2,1,0:T(8,128)(2,1)S(1)}, bf16[8,4,32,512]{3,2,1,0:T(8,128)(2,1)S(1)}, u32[]{:S(2)}, u32[]{:S(2)}) collective-permute-start(bf16[8,4,32,512]{3,2,1,0:T(8,128)(2,1)S(1)} %pack.3.refs_0_), channel_id=1, source_target_pairs={{1,0},{0,1},{3,2},{2,3},{5,4},{4,5},{7,6},{6,7},{9,8},{8,9},{11,10... | collective-permute-start | bytes 3145736 | tf_op jit(solution)/shard_map/ppermute | solution.py:620
  67.8 0.0 all-to-all-done.1.spread_ref
  67.8 0.7 copy-done.2
  68.5 0.6 pick.3.near_ref
  69.1 0.1 collective-permute-start.18
  69.2 2.3 %collective-permute-start.9 = (bf16[4,2,32,512]{3,2,1,0:T(8,128)(2,1)S(1)}, bf16[4,2,32,512]{3,2,1,0:T(8,128)(2,1)S(1)}, u32[]{:S(2)}, u32[]{:S(2)}) collective-permute-start(bf16[4,2,32,512]{3,2,1,0:T(8,128)(2,1)S(1)} %get-tuple-element.44.near_ref), channel_id=1, source_target_pairs={{0,16},{2,18},{4,20},{6,22},{8,24},{10,26},{12,28},{14,30},{16,0},... | collective-permute-start | bytes 786440 | tf_op jit(solution)/shard_map/ppermute | solution.py:632
  71.5 34.5 %collective-permute-done.9.far_ref = bf16[4,2,32,512]{3,2,1,0:T(8,128)(2,1)S(1)} collective-permute-done((bf16[4,2,32,512]{3,2,1,0:T(8,128)(2,1)S(1)}, bf16[4,2,32,512]{3,2,1,0:T(8,128)(2,1)S(1)}, u32[]{:S(2)}, u32[]{:S(2)}) %collective-permute-start.9) | collective-permute-done | bytes 262176 | tf_op jit(solution)/shard_map/ppermute | solution.py:632
  106.0 0.9 build.4
  106.8 1.1 collective-permute-start.10
  107.9 0.3 collective-permute-start.11
  108.2 0.0 collective-permute-done.18.far_ref
  108.2 0.9 build.5
  109.1 0.6 collective-permute-start.19
  109.7 1.1 collective-permute-start.20
  110.8 1.0 collective-permute-start.21
  111.9 0.0 collective-permute-done.11.refs_2_
  111.9 1.3 collective-permute-start.12
  113.2 8.3 %collective-permute-done.12.refs_3_ = bf16[3,32,512]{2,1,0:T(8,128)(2,1)S(1)} collective-permute-done((bf16[3,32,512]{2,1,0:T(8,128)(2,1)S(1)}, bf16[3,32,512]{2,1,0:T(8,128)(2,1)S(1)}, u32[]{:S(2)}, u32[]{:S(2)}) %collective-permute-start.12) | collective-permute-done | bytes 98336 | tf_op jit(solution)/shard_map/ppermute | solution.py:639
  121.5 0.0 collective-permute-start.22
  121.5 1.6 collective-permute-start.23
  123.1 1.3 collective-permute-start.24
  124.4 1.8 %collective-permute-start.25 = (bf16[6,32,512]{2,1,0:T(8,128)(2,1)S(1)}, bf16[6,32,512]{2,1,0:T(8,128)(2,1)S(1)}, u32[]{:S(2)}, u32[]{:S(2)}) collective-permute-start(bf16[6,32,512]{2,1,0:T(8,128)(2,1)S(1)} %get-tuple-element.60), channel_id=1, source_target_pairs={{0,14},{2,12},{4,10},{6,8},{8,6},{10,4},{12,2},{14,0},{16,30},{18,... | collective-permute-start | bytes 589832 | tf_op jit(solution)/shard_map/ppermute | solution.py:639
  126.2 0.0 collective-permute-start.13
  126.3 3.4 %collective-permute-done.23.refs_5_ = bf16[6,32,512]{2,1,0:T(8,128)(2,1)S(1)} collective-permute-done((bf16[6,32,512]{2,1,0:T(8,128)(2,1)S(1)}, bf16[6,32,512]{2,1,0:T(8,128)(2,1)S(1)}, u32[]{:S(2)}, u32[]{:S(2)}) %collective-permute-start.23) | collective-permute-done | bytes 196640 | tf_op jit(solution)/shard_map/ppermute | solution.py:639
  129.7 1.0 collective-permute-start.14
  130.7 3.6 %collective-permute-done.24.refs_6_ = bf16[6,32,512]{2,1,0:T(8,128)(2,1)S(1)} collective-permute-done((bf16[6,32,512]{2,1,0:T(8,128)(2,1)S(1)}, bf16[6,32,512]{2,1,0:T(8,128)(2,1)S(1)}, u32[]{:S(2)}, u32[]{:S(2)}) %collective-permute-start.24) | collective-permute-done | bytes 196640 | tf_op jit(solution)/shard_map/ppermute | solution.py:639
  134.3 0.9 collective-permute-start.15
  135.2 4.7 %collective-permute-done.25.refs_7_ = bf16[6,32,512]{2,1,0:T(8,128)(2,1)S(1)} collective-permute-done((bf16[6,32,512]{2,1,0:T(8,128)(2,1)S(1)}, bf16[6,32,512]{2,1,0:T(8,128)(2,1)S(1)}, u32[]{:S(2)}, u32[]{:S(2)}) %collective-permute-start.25) | collective-permute-done | bytes 196640 | tf_op jit(solution)/shard_map/ppermute | solution.py:639
  140.0 0.1 collective-permute-start.16
  140.1 0.6 pack.5.refs_4_
  140.7 6.1 %collective-permute-start.26 = (bf16[8,6,32,512]{3,2,1,0:T(8,128)(2,1)S(1)}, bf16[8,6,32,512]{3,2,1,0:T(8,128)(2,1)S(1)}, u32[]{:S(2)}, u32[]{:S(2)}) collective-permute-start(bf16[8,6,32,512]{3,2,1,0:T(8,128)(2,1)S(1)} %pack.5.refs_4_), channel_id=1, source_target_pairs={{1,0},{0,1},{3,2},{2,3},{5,4},{4,5},{7,6},{6,7},{9,8},{8,9},{11,10... | collective-permute-start | bytes 4718600 | tf_op jit(solution)/shard_map/ppermute | solution.py:620
  146.8 2.1 %collective-permute-done.16.refs_7_ = bf16[3,32,512]{2,1,0:T(8,128)(2,1)S(1)} collective-permute-done((bf16[3,32,512]{2,1,0:T(8,128)(2,1)S(1)}, bf16[3,32,512]{2,1,0:T(8,128)(2,1)S(1)}, u32[]{:S(2)}, u32[]{:S(2)}) %collective-permute-start.16) | collective-permute-done | bytes 98336 | tf_op jit(solution)/shard_map/ppermute | solution.py:639
  148.9 0.6 pack.4.refs_2_
  149.5 0.0 copy-start.3
  149.5 2.7 %collective-permute-start.17 = (bf16[8,3,32,512]{3,2,1,0:T(8,128)(2,1)S(1)}, bf16[8,3,32,512]{3,2,1,0:T(8,128)(2,1)S(1)}, u32[]{:S(2)}, u32[]{:S(2)}) collective-permute-start(bf16[8,3,32,512]{3,2,1,0:T(8,128)(2,1)S(1)} %pack.4.refs_2_), channel_id=1, source_target_pairs={{1,0},{0,1},{3,2},{2,3},{5,4},{4,5},{7,6},{6,7},{9,8},{8,9},{11,10... | collective-permute-start | bytes 2359304 | tf_op jit(solution)/shard_map/ppermute | solution.py:620
  152.2 8.4 %inverse.1 = (bf16[512,512]{1,0:T(8,128)(2,1)S(1)}, f32[36,256,512]{2,1,0:T(8,128)S(1)}) custom-call(s32[8]{0:T(128)S(1)} %mark.1.t, bf16[8,4,32,512]{3,2,1,0:T(8,128)(2,1)S(1)} %pack.3.refs_0_, bf16[8,4,32,512]{3,2,1,0:T(8,128)(2,1)S(1)} %collective-permute-done.8.refs_1_, f32[36,256,512]{2,1,0:T(8,128)} %bitcast.4), custom_call_target="tpu_custom_call" | custom-call | flops 16106127360 | bytes 1048576 | tf_op jit(solution)/shard_map/inverse/pallas_call | solution.py:461
  160.6 10.6 %update.1 = f32[36,256,512]{2,1,0:T(8,128)} custom-call(s32[40]{0:T(128)S(1)} %copy-done.3, f32[36,256,512]{2,1,0:T(8,128)S(1)} %get-tuple-element.42.tiles, bf16[512,512]{1,0:T(8,128)(2,1)S(1)} %get-tuple-element.43.inv, bf16[8,4,32,512]{3,2,1,0:T(8,128)(2,1)S(1)} %pack.3.refs_0_, bf16[8,4,32,512]{3,2,1,0:T(8,128)(2,1)S(1)} %collective-permute-done.8.refs_1_, ...), custom_call_target="tpu_custom_call" | custom-call | tf_op jit(solution)/shard_map/update/pallas_call | solution.py:582
  (20 shorter events, 0.0 us)
Async XLA Ops:
  0.0 9.1 %copy-start.5 = (s32[16]{0:T(128)S(1)}, s32[16]{0:T(128)}, u32[]{:S(2)}) copy-start(s32[16]{0:T(128)} %owner.5) | copy-start | bytes 196
  0.0 0.7 copy-start.4
  3.8 19.1 %all-to-all-start = ((bf16[8,4,32,512]{3,2,1,0:T(8,128)(2,1)}), bf16[8,4,32,512]{3,2,1,0:T(8,128)(2,1)S(1)}, u32[]{:S(2)}, u32[]{:S(2)}) async-start(bf16[8,4,32,512]{3,2,1,0:T(8,128)(2,1)} %extract.2), calls=%async_computation | async-start | bytes 2097152 | tf_op jit(solution)/shard_map/all_to_all | solution.py:614
  23.0 44.8 %all-to-all-start.1 = ((bf16[8,4,32,512]{3,2,1,0:T(8,128)(2,1)}), bf16[8,4,32,512]{3,2,1,0:T(8,128)(2,1)S(1)}, u32[]{:S(2)}, u32[]{:S(2)}) async-start(bf16[8,4,32,512]{3,2,1,0:T(8,128)(2,1)} %extract.3), calls=%async_computation.1 | async-start | bytes 2097152 | tf_op jit(solution)/shard_map/all_to_all | solution.py:614
  28.5 0.7 copy-start
  29.8 13.8 %collective-permute-start = (bf16[4,2,32,512]{3,2,1,0:T(8,128)(2,1)S(1)}, bf16[4,2,32,512]{3,2,1,0:T(8,128)(2,1)S(1)}, u32[]{:S(2)}, u32[]{:S(2)}) collective-permute-start(bf16[4,2,32,512]{3,2,1,0:T(8,128)(2,1)S(1)} %get-tuple-element.33.near_ref), channel_id=1, source_target_pairs={{0,16},{2,18},{4,20},{6,22},{8,24},{10,26},{12,28},{14,30},{16,0},... | collective-permute-start | bytes 786440 | tf_op jit(solution)/shard_map/ppermute | solution.py:632
  43.5 0.7 copy-start.1
  45.2 8.0 %collective-permute-start.1 = (bf16[4,32,512]{2,1,0:T(8,128)(2,1)S(1)}, bf16[4,32,512]{2,1,0:T(8,128)(2,1)S(1)}, u32[]{:S(2)}, u32[]{:S(2)}) collective-permute-start(bf16[4,32,512]{2,1,0:T(8,128)(2,1)S(1)} %get-tuple-element.35), channel_id=1, source_target_pairs={{0,2},{2,0},{4,6},{6,4},{8,10},{10,8},{12,14},{14,12},{16,18},{18,... | collective-permute-start | bytes 393224 | tf_op jit(solution)/shard_map/ppermute | solution.py:639
  46.5 9.0 %collective-permute-start.2 = (bf16[4,32,512]{2,1,0:T(8,128)(2,1)S(1)}, bf16[4,32,512]{2,1,0:T(8,128)(2,1)S(1)}, u32[]{:S(2)}, u32[]{:S(2)}) collective-permute-start(bf16[4,32,512]{2,1,0:T(8,128)(2,1)S(1)} %get-tuple-element.36), channel_id=1, source_target_pairs={{0,4},{2,6},{4,0},{6,2},{8,12},{10,14},{12,8},{14,10},{16,20},{18,... | collective-permute-start | bytes 393224 | tf_op jit(solution)/shard_map/ppermute | solution.py:639
  47.6 10.2 %collective-permute-start.3 = (bf16[4,32,512]{2,1,0:T(8,128)(2,1)S(1)}, bf16[4,32,512]{2,1,0:T(8,128)(2,1)S(1)}, u32[]{:S(2)}, u32[]{:S(2)}) collective-permute-start(bf16[4,32,512]{2,1,0:T(8,128)(2,1)S(1)} %get-tuple-element.37), channel_id=1, source_target_pairs={{0,6},{2,4},{4,2},{6,0},{8,14},{10,12},{12,10},{14,8},{16,22},{18,... | collective-permute-start | bytes 393224 | tf_op jit(solution)/shard_map/ppermute | solution.py:639
  47.9 10.0 %collective-permute-start.4 = (bf16[4,32,512]{2,1,0:T(8,128)(2,1)S(1)}, bf16[4,32,512]{2,1,0:T(8,128)(2,1)S(1)}, u32[]{:S(2)}, u32[]{:S(2)}) collective-permute-start(bf16[4,32,512]{2,1,0:T(8,128)(2,1)S(1)} %get-tuple-element.38), channel_id=1, source_target_pairs={{0,8},{2,10},{4,12},{6,14},{8,0},{10,2},{12,4},{14,6},{16,24},{18,... | collective-permute-start | bytes 393224 | tf_op jit(solution)/shard_map/ppermute | solution.py:639
  52.3 5.6 %collective-permute-start.5 = (bf16[4,32,512]{2,1,0:T(8,128)(2,1)S(1)}, bf16[4,32,512]{2,1,0:T(8,128)(2,1)S(1)}, u32[]{:S(2)}, u32[]{:S(2)}) collective-permute-start(bf16[4,32,512]{2,1,0:T(8,128)(2,1)S(1)} %get-tuple-element.39), channel_id=1, source_target_pairs={{0,10},{2,8},{4,14},{6,12},{8,2},{10,0},{12,6},{14,4},{16,26},{18,... | collective-permute-start | bytes 393224 | tf_op jit(solution)/shard_map/ppermute | solution.py:639
  53.1 8.6 %collective-permute-start.6 = (bf16[4,32,512]{2,1,0:T(8,128)(2,1)S(1)}, bf16[4,32,512]{2,1,0:T(8,128)(2,1)S(1)}, u32[]{:S(2)}, u32[]{:S(2)}) collective-permute-start(bf16[4,32,512]{2,1,0:T(8,128)(2,1)S(1)} %get-tuple-element.40), channel_id=1, source_target_pairs={{0,12},{2,14},{4,8},{6,10},{8,4},{10,6},{12,0},{14,2},{16,28},{18,... | collective-permute-start | bytes 393224 | tf_op jit(solution)/shard_map/ppermute | solution.py:639
  55.5 8.0 %collective-permute-start.7 = (bf16[4,32,512]{2,1,0:T(8,128)(2,1)S(1)}, bf16[4,32,512]{2,1,0:T(8,128)(2,1)S(1)}, u32[]{:S(2)}, u32[]{:S(2)}) collective-permute-start(bf16[4,32,512]{2,1,0:T(8,128)(2,1)S(1)} %get-tuple-element.41), channel_id=1, source_target_pairs={{0,14},{2,12},{4,10},{6,8},{8,6},{10,4},{12,2},{14,0},{16,30},{18,... | collective-permute-start | bytes 393224 | tf_op jit(solution)/shard_map/ppermute | solution.py:639
  64.1 88.1 %collective-permute-start.8 = (bf16[8,4,32,512]{3,2,1,0:T(8,128)(2,1)S(1)}, bf16[8,4,32,512]{3,2,1,0:T(8,128)(2,1)S(1)}, u32[]{:S(2)}, u32[]{:S(2)}) collective-permute-start(bf16[8,4,32,512]{3,2,1,0:T(8,128)(2,1)S(1)} %pack.3.refs_0_), channel_id=1, source_target_pairs={{1,0},{0,1},{3,2},{2,3},{5,4},{4,5},{7,6},{6,7},{9,8},{8,9},{11,10... | collective-permute-start | bytes 3145736 | tf_op jit(solution)/shard_map/ppermute | solution.py:620
  67.8 0.7 copy-start.2
  69.1 39.1 %collective-permute-start.18 = (bf16[4,4,32,512]{3,2,1,0:T(8,128)(2,1)S(1)}, bf16[4,4,32,512]{3,2,1,0:T(8,128)(2,1)S(1)}, u32[]{:S(2)}, u32[]{:S(2)}) collective-permute-start(bf16[4,4,32,512]{3,2,1,0:T(8,128)(2,1)S(1)} %pick.3.near_ref), channel_id=1, source_target_pairs={{0,16},{2,18},{4,20},{6,22},{8,24},{10,26},{12,28},{14,30},{16,0},... | collective-permute-start | bytes 1572872 | tf_op jit(solution)/shard_map/ppermute | solution.py:632
  69.2 36.8 %collective-permute-start.9 = (bf16[4,2,32,512]{3,2,1,0:T(8,128)(2,1)S(1)}, bf16[4,2,32,512]{3,2,1,0:T(8,128)(2,1)S(1)}, u32[]{:S(2)}, u32[]{:S(2)}) collective-permute-start(bf16[4,2,32,512]{3,2,1,0:T(8,128)(2,1)S(1)} %get-tuple-element.44.near_ref), channel_id=1, source_target_pairs={{0,16},{2,18},{4,20},{6,22},{8,24},{10,26},{12,28},{14,30},{16,0},... | collective-permute-start | bytes 786440 | tf_op jit(solution)/shard_map/ppermute | solution.py:632
  106.8 4.0 %collective-permute-start.10 = (bf16[3,32,512]{2,1,0:T(8,128)(2,1)S(1)}, bf16[3,32,512]{2,1,0:T(8,128)(2,1)S(1)}, u32[]{:S(2)}, u32[]{:S(2)}) collective-permute-start(bf16[3,32,512]{2,1,0:T(8,128)(2,1)S(1)} %get-tuple-element.46), channel_id=1, source_target_pairs={{0,2},{2,0},{4,6},{6,4},{8,10},{10,8},{12,14},{14,12},{16,18},{18,... | collective-permute-start | bytes 294920 | tf_op jit(solution)/shard_map/ppermute | solution.py:639
  107.9 3.9 %collective-permute-start.11 = (bf16[3,32,512]{2,1,0:T(8,128)(2,1)S(1)}, bf16[3,32,512]{2,1,0:T(8,128)(2,1)S(1)}, u32[]{:S(2)}, u32[]{:S(2)}) collective-permute-start(bf16[3,32,512]{2,1,0:T(8,128)(2,1)S(1)} %get-tuple-element.47), channel_id=1, source_target_pairs={{0,4},{2,6},{4,0},{6,2},{8,12},{10,14},{12,8},{14,10},{16,20},{18,... | collective-permute-start | bytes 294920 | tf_op jit(solution)/shard_map/ppermute | solution.py:639
  109.1 12.4 %collective-permute-start.19 = (bf16[6,32,512]{2,1,0:T(8,128)(2,1)S(1)}, bf16[6,32,512]{2,1,0:T(8,128)(2,1)S(1)}, u32[]{:S(2)}, u32[]{:S(2)}) collective-permute-start(bf16[6,32,512]{2,1,0:T(8,128)(2,1)S(1)} %get-tuple-element.54), channel_id=1, source_target_pairs={{0,2},{2,0},{4,6},{6,4},{8,10},{10,8},{12,14},{14,12},{16,18},{18,... | collective-permute-start | bytes 589832 | tf_op jit(solution)/shard_map/ppermute | solution.py:639
  109.7 13.4 %collective-permute-start.20 = (bf16[6,32,512]{2,1,0:T(8,128)(2,1)S(1)}, bf16[6,32,512]{2,1,0:T(8,128)(2,1)S(1)}, u32[]{:S(2)}, u32[]{:S(2)}) collective-permute-start(bf16[6,32,512]{2,1,0:T(8,128)(2,1)S(1)} %get-tuple-element.55), channel_id=1, source_target_pairs={{0,4},{2,6},{4,0},{6,2},{8,12},{10,14},{12,8},{14,10},{16,20},{18,... | collective-permute-start | bytes 589832 | tf_op jit(solution)/shard_map/ppermute | solution.py:639
  110.8 13.6 %collective-permute-start.21 = (bf16[6,32,512]{2,1,0:T(8,128)(2,1)S(1)}, bf16[6,32,512]{2,1,0:T(8,128)(2,1)S(1)}, u32[]{:S(2)}, u32[]{:S(2)}) collective-permute-start(bf16[6,32,512]{2,1,0:T(8,128)(2,1)S(1)} %get-tuple-element.56), channel_id=1, source_target_pairs={{0,6},{2,4},{4,2},{6,0},{8,14},{10,12},{12,10},{14,8},{16,22},{18,... | collective-permute-start | bytes 589832 | tf_op jit(solution)/shard_map/ppermute | solution.py:639
  111.9 9.6 %collective-permute-start.12 = (bf16[3,32,512]{2,1,0:T(8,128)(2,1)S(1)}, bf16[3,32,512]{2,1,0:T(8,128)(2,1)S(1)}, u32[]{:S(2)}, u32[]{:S(2)}) collective-permute-start(bf16[3,32,512]{2,1,0:T(8,128)(2,1)S(1)} %get-tuple-element.48), channel_id=1, source_target_pairs={{0,6},{2,4},{4,2},{6,0},{8,14},{10,12},{12,10},{14,8},{16,22},{18,... | collective-permute-start | bytes 294920 | tf_op jit(solution)/shard_map/ppermute | solution.py:639
  121.5 4.7 %collective-permute-start.22 = (bf16[6,32,512]{2,1,0:T(8,128)(2,1)S(1)}, bf16[6,32,512]{2,1,0:T(8,128)(2,1)S(1)}, u32[]{:S(2)}, u32[]{:S(2)}) collective-permute-start(bf16[6,32,512]{2,1,0:T(8,128)(2,1)S(1)} %get-tuple-element.57), channel_id=1, source_target_pairs={{0,8},{2,10},{4,12},{6,14},{8,0},{10,2},{12,4},{14,6},{16,24},{18,... | collective-permute-start | bytes 589832 | tf_op jit(solution)/shard_map/ppermute | solution.py:639
  121.5 8.2 %collective-permute-start.23 = (bf16[6,32,512]{2,1,0:T(8,128)(2,1)S(1)}, bf16[6,32,512]{2,1,0:T(8,128)(2,1)S(1)}, u32[]{:S(2)}, u32[]{:S(2)}) collective-permute-start(bf16[6,32,512]{2,1,0:T(8,128)(2,1)S(1)} %get-tuple-element.58), channel_id=1, source_target_pairs={{0,10},{2,8},{4,14},{6,12},{8,2},{10,0},{12,6},{14,4},{16,26},{18,... | collective-permute-start | bytes 589832 | tf_op jit(solution)/shard_map/ppermute | solution.py:639
  123.1 11.2 %collective-permute-start.24 = (bf16[6,32,512]{2,1,0:T(8,128)(2,1)S(1)}, bf16[6,32,512]{2,1,0:T(8,128)(2,1)S(1)}, u32[]{:S(2)}, u32[]{:S(2)}) collective-permute-start(bf16[6,32,512]{2,1,0:T(8,128)(2,1)S(1)} %get-tuple-element.59), channel_id=1, source_target_pairs={{0,12},{2,14},{4,8},{6,10},{8,4},{10,6},{12,0},{14,2},{16,28},{18,... | collective-permute-start | bytes 589832 | tf_op jit(solution)/shard_map/ppermute | solution.py:639
  124.4 15.6 %collective-permute-start.25 = (bf16[6,32,512]{2,1,0:T(8,128)(2,1)S(1)}, bf16[6,32,512]{2,1,0:T(8,128)(2,1)S(1)}, u32[]{:S(2)}, u32[]{:S(2)}) collective-permute-start(bf16[6,32,512]{2,1,0:T(8,128)(2,1)S(1)} %get-tuple-element.60), channel_id=1, source_target_pairs={{0,14},{2,12},{4,10},{6,8},{8,6},{10,4},{12,2},{14,0},{16,30},{18,... | collective-permute-start | bytes 589832 | tf_op jit(solution)/shard_map/ppermute | solution.py:639
  126.2 14.5 %collective-permute-start.13 = (bf16[3,32,512]{2,1,0:T(8,128)(2,1)S(1)}, bf16[3,32,512]{2,1,0:T(8,128)(2,1)S(1)}, u32[]{:S(2)}, u32[]{:S(2)}) collective-permute-start(bf16[3,32,512]{2,1,0:T(8,128)(2,1)S(1)} %get-tuple-element.49), channel_id=1, source_target_pairs={{0,8},{2,10},{4,12},{6,14},{8,0},{10,2},{12,4},{14,6},{16,24},{18,... | collective-permute-start | bytes 294920 | tf_op jit(solution)/shard_map/ppermute | solution.py:639
  129.7 17.1 %collective-permute-start.14 = (bf16[3,32,512]{2,1,0:T(8,128)(2,1)S(1)}, bf16[3,32,512]{2,1,0:T(8,128)(2,1)S(1)}, u32[]{:S(2)}, u32[]{:S(2)}) collective-permute-start(bf16[3,32,512]{2,1,0:T(8,128)(2,1)S(1)} %get-tuple-element.50), channel_id=1, source_target_pairs={{0,10},{2,8},{4,14},{6,12},{8,2},{10,0},{12,6},{14,4},{16,26},{18,... | collective-permute-start | bytes 294920 | tf_op jit(solution)/shard_map/ppermute | solution.py:639
  134.3 12.5 %collective-permute-start.15 = (bf16[3,32,512]{2,1,0:T(8,128)(2,1)S(1)}, bf16[3,32,512]{2,1,0:T(8,128)(2,1)S(1)}, u32[]{:S(2)}, u32[]{:S(2)}) collective-permute-start(bf16[3,32,512]{2,1,0:T(8,128)(2,1)S(1)} %get-tuple-element.51), channel_id=1, source_target_pairs={{0,12},{2,14},{4,8},{6,10},{8,4},{10,6},{12,0},{14,2},{16,28},{18,... | collective-permute-start | bytes 294920 | tf_op jit(solution)/shard_map/ppermute | solution.py:639
  140.0 8.9 %collective-permute-start.16 = (bf16[3,32,512]{2,1,0:T(8,128)(2,1)S(1)}, bf16[3,32,512]{2,1,0:T(8,128)(2,1)S(1)}, u32[]{:S(2)}, u32[]{:S(2)}) collective-permute-start(bf16[3,32,512]{2,1,0:T(8,128)(2,1)S(1)} %get-tuple-element.52), channel_id=1, source_target_pairs={{0,14},{2,12},{4,10},{6,8},{8,6},{10,4},{12,2},{14,0},{16,30},{18,... | collective-permute-start | bytes 294920 | tf_op jit(solution)/shard_map/ppermute | solution.py:639
  140.7 19.8 %collective-permute-start.26 = (bf16[8,6,32,512]{3,2,1,0:T(8,128)(2,1)S(1)}, bf16[8,6,32,512]{3,2,1,0:T(8,128)(2,1)S(1)}, u32[]{:S(2)}, u32[]{:S(2)}) collective-permute-start(bf16[8,6,32,512]{3,2,1,0:T(8,128)(2,1)S(1)} %pack.5.refs_4_), channel_id=1, source_target_pairs={{1,0},{0,1},{3,2},{2,3},{5,4},{4,5},{7,6},{6,7},{9,8},{8,9},{11,10... | collective-permute-start | bytes 4718600 | tf_op jit(solution)/shard_map/ppermute | solution.py:620
  149.5 11.1 %copy-start.3 = (s32[40]{0:T(128)S(1)}, s32[40]{0:T(128)}, u32[]{:S(2)}) copy-start(s32[40]{0:T(128)} %table.1.t) | copy-start | bytes 484
  149.5 11.0 %collective-permute-start.17 = (bf16[8,3,32,512]{3,2,1,0:T(8,128)(2,1)S(1)}, bf16[8,3,32,512]{3,2,1,0:T(8,128)(2,1)S(1)}, u32[]{:S(2)}, u32[]{:S(2)}) collective-permute-start(bf16[8,3,32,512]{3,2,1,0:T(8,128)(2,1)S(1)} %pack.4.refs_2_), channel_id=1, source_target_pairs={{1,0},{0,1},{3,2},{2,3},{5,4},{4,5},{7,6},{6,7},{9,8},{8,9},{11,10... | collective-permute-start | bytes 2359304 | tf_op jit(solution)/shard_map/ppermute | solution.py:620

commit v7 on v6

--- a/solution.py
+++ b/solution.py
@@ -236,25 +236,13 @@
     return pltpu.with_memory_space_constraint(x, pltpu.HBM)
 
 
-def mark_call(p, table):
-    def kernel(t, out):
-        for i in (p.o_sub, p.o_diag, p.o_me):
-            out[i] = t[i]
-
-    smem = pl.BlockSpec(memory_space=pltpu.SMEM)
-    return pl.pallas_call(
-        kernel,
-        out_shape=jax.ShapeDtypeStruct((p.o_src,), jnp.int32),
-        in_specs=[smem],
-        out_specs=smem,
-        compiler_params=limit(1),
-        name="mark",
-    )(table)
-
-
-def extract_call(p, cell_owner, current, members):
-    def kernel(owner, tiles, out, wide, sems):
+def extract_call(p, cell_owner, current, members, apart):
+    one = (len(members), p.piece, p.order)
+
+    def kernel(owner, tiles, *refs):
+        outs, (wide, sems) = refs[:-2], refs[-2:]
         position = lax.axis_index("tri")
+        me = lax.rem(position, p.half_tri)
         cell = jnp.int32(0)
         for n in range(1, p.tri):
             cell = jnp.where(owner[n] == position, n, cell)
@@ -269,17 +257,26 @@
             copy.start()
         for place, copy in enumerate(copies):
             copy.wait()
-            rounded = wide[place].astype(jnp.bfloat16)
-            out[:, place] = rounded.reshape(p.half_tri, p.piece, p.order)
-
+            if apart:
+                for n, out in enumerate(outs):
+                    at = pl.multiple_of((me ^ n) * p.piece, p.piece)
+                    out[place] = wide[place, pl.ds(at, p.piece)].astype(jnp.bfloat16)
+            else:
+                rounded = wide[place].astype(jnp.bfloat16)
+                outs[0][:, place] = rounded.reshape(p.half_tri, p.piece, p.order)
+
+    if apart:
+        out_shape = [pltpu.VMEM(one, jnp.bfloat16)] * p.half_tri
+    else:
+        out_shape = [pltpu.VMEM((p.half_tri,) + one, jnp.bfloat16)]
     return pl.pallas_call(
         kernel,
-        out_shape=pltpu.VMEM((p.half_tri, len(members), p.piece, p.order), jnp.bfloat16),
+        out_shape=out_shape,
         in_specs=[
             pl.BlockSpec(memory_space=pltpu.SMEM),
             pl.BlockSpec(memory_space=pltpu.HBM),
         ],
-        out_specs=IN_VMEM,
+        out_specs=[IN_VMEM] * len(out_shape),
         scratch_shapes=[
             pltpu.VMEM((len(members), p.strip, p.order), jnp.float32),
             pltpu.SemaphoreType.DMA((len(members),)),
@@ -290,13 +287,22 @@
 
 
 def pick_call(p, table, spread, chunks):
-    def kernel(t, spread_ref, *outs):
+    def kernel(t, *refs):
+        sources, outs = refs[: len(spread)], refs[len(spread) :]
         for g in range(p.groups):
             first = 0
             for out in outs:
                 count = out.shape[1]
-                out[g] = spread_ref[t[p.o_src + g], first : first + count]
+                part = slice(first, first + count)
                 first += count
+                if len(sources) == 1:
+                    out[g] = sources[0][t[p.o_src + g], part]
+                    continue
+                for n, source in enumerate(sources):
+
+                    @pl.when(t[p.o_src + g] == t[p.o_me] ^ n)
+                    def _():
+                        out[g] = source[part]
 
     return pl.pallas_call(
         kernel,
@@ -306,12 +312,12 @@
         grid_spec=pltpu.PrefetchScalarGridSpec(
             num_scalar_prefetch=1,
             grid=(),
-            in_specs=[IN_VMEM],
+            in_specs=[IN_VMEM] * len(spread),
             out_specs=[IN_VMEM] * len(chunks),
         ),
         compiler_params=limit(8),
         name="pick",
-    )(table, in_vmem(spread))
+    )(table, *[in_vmem(x) for x in spread])
 
 
 def build_call(p, table, near, far, wide, with_pivot):
@@ -605,15 +611,17 @@
 
 
 def planned(p, stored_tiles, cell_owner):
-    table = table_call(p, cell_owner)
     current = stored_tiles[0]
     halves = [list(range(h * p.half_tri, (h + 1) * p.half_tri)) for h in range(2)]
     swap = [(i, (i + p.half_tri) % p.tri) for i in range(p.tri)]
-
-    def exchange(x):
-        return lax.all_to_all(
-            x, "tri", split_axis=0, concat_axis=0, tiled=True, axis_index_groups=halves
-        )
+    chunks = len(p.wides)
+
+    def send(pieces):
+        arrived = {0: pieces[0]}
+        for n in reversed(range(1, p.half_tri)):
+            pairs = [(i, i ^ n) for i in range(p.tri)]
+            arrived[n] = lax.ppermute(pieces[n], "tri", pairs)
+        return [arrived[n] for n in range(p.half_tri)]
 
     def arrivals(x):
         return [x] + [
@@ -621,27 +629,33 @@
             for shift in range(1, p.subs)
         ]
 
-    chunks = len(p.wides)
-    near, far = [], []
-    for members in p.spreads:
+    table = table_call(p, cell_owner)
+    near, far, arrived = [], [], []
+    for number, members in enumerate(p.spreads):
         tiles = [tile for chunk in members for tile in p.tiles_of(chunk)]
-        pieces = extract_call(p, cell_owner, current, tiles)
-        spread = exchange(pieces)
+        pieces = extract_call(p, cell_owner, current, tiles, number > 0)
+        if number == 0:
+            spread = [
+                lax.all_to_all(
+                    pieces[0],
+                    "tri",
+                    split_axis=0,
+                    concat_axis=0,
+                    tiled=True,
+                    axis_index_groups=halves,
+                )
+            ]
+        else:
+            spread = send(pieces)
         near.extend(pick_call(p, table, spread, members))
     for chunk in range(chunks):
         far.append(lax.ppermute(near[chunk], "tri", swap))
-    arrived = []
     for chunk in range(chunks):
         built = build_call(p, table, near[chunk], far[chunk], p.wides[chunk], chunk == 0)
-        pieces = [built[0]]
-        for n in range(1, p.half_tri):
-            pairs = [(i, i ^ n) for i in range(p.tri)]
-            pieces.append(lax.ppermute(built[n], "tri", pairs))
-        if chunk == 0:
-            table_after = mark_call(p, table)
-        packed = pack_call(p, table_after, pieces)
+        pieces = send(built)
+        packed = pack_call(p, table, pieces)
         arrived.append(arrivals(packed))
-    inverse, held = inverse_call(p, table_after, arrived[0], current)
+    inverse, held = inverse_call(p, table, arrived[0], current)
     return update_call(p, table, held, arrived, inverse)[None]
 
 

time: 172 us -> 151 us (0.88)
  waiting for transfers between devices: 84.3 us -> 53.6 us
  starting transfers between devices: 50.6 us -> 63.8 us
  Pallas kernels: 33.4 us -> 31.5 us
    ppermute x3, waiting for transfers between devices: 45.9 us -> 24.4 us  [planned(): far.append(lax.ppermute(near[chunk], 'tri', swap))]
    ppermute x21 -> x28, waiting for transfers between devices: 27.7 us -> 16.6 us  [send(): arrived[n] = lax.ppermute(pieces[n], 'tri', pairs)]
    ppermute x21 -> x28, starting transfers between devices: 23.7 us -> 33.6 us  [send(): arrived[n] = lax.ppermute(pieces[n], 'tri', pairs)]
    ppermute x3, starting transfers between devices: 4.8 us -> 12.1 us  [planned(): far.append(lax.ppermute(near[chunk], 'tri', swap))]
    all_to_all x2 -> x1, starting transfers between devices: 9.53 us -> 5.29 us  [planned(): lax.all_to_all(pieces[0], 'tri', split_axis=0, concat_axis=0, tiled=True,...]
    pallas_call x3 -> x2, Pallas kernels: 7.36 us -> 5.23 us  [extract_call(): pl.pallas_call(kernel, out_shape=out_shape, in_specs=[pl.BlockSpec(memory...]
    all_to_all x2 -> x1, waiting for transfers between devices: 10.7 us -> 12.5 us  [planned(): lax.all_to_all(pieces[0], 'tri', split_axis=0, concat_axis=0, tiled=True,...]
  transfers between devices with their start and end apart: 29 -> 35, of which waited for: 10 -> 13; matrix products, arithmetic and copies ran while one was open for 0% -> 0% of each run, Pallas kernels for 11% -> 11%
where the time goes in v7:
time: 151 us
  starting transfers between devices  63.8 us (42%)
  waiting for transfers between devices  53.6 us (35%)
  Pallas kernels  31.5 us (21%)
    ppermute x28, starting transfers between devices, send(): arrived[n] = lax.ppermute(pieces[n], 'tri', pairs)  33.6 us
    ppermute x3, waiting for transfers between devices, planned(): far.append(lax.ppermute(near[chunk], 'tri', swap))  24.4 us
    ppermute x28, waiting for transfers between devices, send(): arrived[n] = lax.ppermute(pieces[n], 'tri', pairs)  16.6 us
    ppermute x3, starting transfers between devices, arrivals(): lax.ppermute(x, 'sub', [((i + shift) % p.subs, i) for i in range(p.subs)])  12.9 us
    all_to_all x1, waiting for transfers between devices, planned(): lax.all_to_all(pieces[0], 'tri', split_axis=0, concat_axis=0, tiled=True,...  12.5 us
    ppermute x3, starting transfers between devices, planned(): far.append(lax.ppermute(near[chunk], 'tri', swap))  12.1 us
    pallas_call x1, Pallas kernels, update_call(): pl.pallas_call(kernel, out_shape=jax.ShapeDtypeStruct(held.shape, jnp.flo...  10.6 us
    pallas_call x1, Pallas kernels, inverse_call(): pl.pallas_call(kernel, out_shape=(square_shape, pltpu.VMEM(current.shape,...  8.36 us
  transfers between devices with their start and end apart: 35, of which 13 were waited for; matrix products, arithmetic and copies ran while one was open for 0% of the time, Pallas kernels for 11%

profile of v7, /device:TPU:1, one launch (start us, length us, event | category | flops | bytes accessed | tf_op | source)
XLA Modules:
  0.0 150.6 jit_solution(7600432378616040794)
XLA Ops:
  0.0 0.7 copy-done.2
  0.7 3.1 %extract.2 = bf16[8,4,32,512]{3,2,1,0:T(8,128)(2,1)} custom-call(s32[16]{0:T(128)S(1)} %copy-done.2, f32[36,256,512]{2,1,0:T(8,128)} %bitcast.2), custom_call_target="tpu_custom_call" | custom-call | tf_op jit(solution)/shard_map/extract/pallas_call | solution.py:272
  3.8 5.3 %all-to-all-start = ((bf16[8,4,32,512]{3,2,1,0:T(8,128)(2,1)}), bf16[8,4,32,512]{3,2,1,0:T(8,128)(2,1)S(1)}, u32[]{:S(2)}, u32[]{:S(2)}) async-start(bf16[8,4,32,512]{3,2,1,0:T(8,128)(2,1)} %extract.2), calls=%async_computation | async-start | bytes 2097152 | tf_op jit(solution)/shard_map/all_to_all | solution.py:639
  9.1 1.3 table.1.t
  10.4 12.5 %all-to-all-done.refs_0_ = bf16[8,4,32,512]{3,2,1,0:T(8,128)(2,1)S(1)} async-done(((bf16[8,4,32,512]{3,2,1,0:T(8,128)(2,1)}), bf16[8,4,32,512]{3,2,1,0:T(8,128)(2,1)S(1)}, u32[]{:S(2)}, u32[]{:S(2)}) %all-to-all-start) | async-done | bytes 1048608 | tf_op jit(solution)/shard_map/all_to_all | solution.py:639
  23.0 0.7 copy-done
  23.6 0.6 pick.2
  24.2 2.4 %collective-permute-start = (bf16[4,2,32,512]{3,2,1,0:T(8,128)(2,1)S(1)}, bf16[4,2,32,512]{3,2,1,0:T(8,128)(2,1)S(1)}, u32[]{:S(2)}, u32[]{:S(2)}) collective-permute-start(bf16[4,2,32,512]{3,2,1,0:T(8,128)(2,1)S(1)} %get-tuple-element.41.near_ref), channel_id=1, source_target_pairs={{0,16},{2,18},{4,20},{6,22},{8,24},{10,26},{12,28},{14,30},{16,0},... | collective-permute-start | bytes 786440 | tf_op jit(solution)/shard_map/ppermute | solution.py:652
  26.6 2.1 %extract.3 = (bf16[4,32,512]{2,1,0:T(8,128)(2,1)S(1)}, bf16[4,32,512]{2,1,0:T(8,128)(2,1)S(1)}, bf16[4,32,512]{2,1,0:T(8,128)(2,1)S(1)}, bf16[4,32,512]{2,1,0:T(...) custom-call(s32[16]{0:T(128)S(1)} %copy-done.3, ...), custom_call_target="tpu_custom_call" | custom-call | tf_op jit(solution)/shard_map/extract/pallas_call | solution.py:272
  28.8 1.4 collective-permute-start.18
  30.2 0.1 collective-permute-start.19
  30.3 1.2 collective-permute-start.20
  31.5 2.3 %collective-permute-start.21 = (bf16[4,32,512]{2,1,0:T(8,128)(2,1)S(1)}, bf16[4,32,512]{2,1,0:T(8,128)(2,1)S(1)}, u32[]{:S(2)}, u32[]{:S(2)}) collective-permute-start(bf16[4,32,512]{2,1,0:T(8,128)(2,1)S(1)} %get-tuple-element.65), channel_id=1, source_target_pairs={{0,8},{2,10},{4,12},{6,14},{8,0},{10,2},{12,4},{14,6},{16,24},{18,... | collective-permute-start | bytes 393224 | tf_op jit(solution)/shard_map/ppermute | solution.py:623
  33.7 3.3 %collective-permute-done.far_ref = bf16[4,2,32,512]{3,2,1,0:T(8,128)(2,1)S(1)} collective-permute-done((bf16[4,2,32,512]{3,2,1,0:T(8,128)(2,1)S(1)}, bf16[4,2,32,512]{3,2,1,0:T(8,128)(2,1)S(1)}, u32[]{:S(2)}, u32[]{:S(2)}) %collective-permute-start) | collective-permute-done | bytes 262176 | tf_op jit(solution)/shard_map/ppermute | solution.py:652
  37.0 3.5 %collective-permute-start.22 = (bf16[4,32,512]{2,1,0:T(8,128)(2,1)S(1)}, bf16[4,32,512]{2,1,0:T(8,128)(2,1)S(1)}, u32[]{:S(2)}, u32[]{:S(2)}) collective-permute-start(bf16[4,32,512]{2,1,0:T(8,128)(2,1)S(1)} %get-tuple-element.66), channel_id=1, source_target_pairs={{0,10},{2,8},{4,14},{6,12},{8,2},{10,0},{12,6},{14,4},{16,26},{18,... | collective-permute-start | bytes 393224 | tf_op jit(solution)/shard_map/ppermute | solution.py:623
  40.6 1.0 build.3
  41.5 0.0 collective-permute-done.18.refs_1_
  41.5 0.1 collective-permute-start.23
  41.6 2.2 %collective-permute-start.24 = (bf16[4,32,512]{2,1,0:T(8,128)(2,1)S(1)}, bf16[4,32,512]{2,1,0:T(8,128)(2,1)S(1)}, u32[]{:S(2)}, u32[]{:S(2)}) collective-permute-start(bf16[4,32,512]{2,1,0:T(8,128)(2,1)S(1)} %get-tuple-element.68), channel_id=1, source_target_pairs={{0,14},{2,12},{4,10},{6,8},{8,6},{10,4},{12,2},{14,0},{16,30},{18,... | collective-permute-start | bytes 393224 | tf_op jit(solution)/shard_map/ppermute | solution.py:623
  43.8 1.4 collective-permute-start.1
  45.2 0.0 collective-permute-done.21.refs_4_
  45.2 0.1 collective-permute-start.2
  45.3 0.0 collective-permute-done.22.refs_5_
  45.3 1.2 collective-permute-start.3
  46.5 0.3 collective-permute-done.23.refs_6_
  46.8 0.2 collective-permute-start.4
  47.0 2.6 %collective-permute-done.24.refs_7_ = bf16[4,32,512]{2,1,0:T(8,128)(2,1)S(1)} collective-permute-done((bf16[4,32,512]{2,1,0:T(8,128)(2,1)S(1)}, bf16[4,32,512]{2,1,0:T(8,128)(2,1)S(1)}, u32[]{:S(2)}, u32[]{:S(2)}) %collective-permute-start.24) | collective-permute-done | bytes 131104 | tf_op jit(solution)/shard_map/ppermute | solution.py:623
  49.5 1.0 collective-permute-start.5
  50.5 0.0 collective-permute-done.1.refs_1_
  50.5 2.5 %collective-permute-start.6 = (bf16[4,32,512]{2,1,0:T(8,128)(2,1)S(1)}, bf16[4,32,512]{2,1,0:T(8,128)(2,1)S(1)}, u32[]{:S(2)}, u32[]{:S(2)}) collective-permute-start(bf16[4,32,512]{2,1,0:T(8,128)(2,1)S(1)} %get-tuple-element.48), channel_id=1, source_target_pairs={{0,12},{2,14},{4,8},{6,10},{8,4},{10,6},{12,0},{14,2},{16,28},{18,... | collective-permute-start | bytes 393224 | tf_op jit(solution)/shard_map/ppermute | solution.py:623
  53.0 3.4 %collective-permute-done.2.refs_2_ = bf16[4,32,512]{2,1,0:T(8,128)(2,1)S(1)} collective-permute-done((bf16[4,32,512]{2,1,0:T(8,128)(2,1)S(1)}, bf16[4,32,512]{2,1,0:T(8,128)(2,1)S(1)}, u32[]{:S(2)}, u32[]{:S(2)}) %collective-permute-start.2) | collective-permute-done | bytes 131104 | tf_op jit(solution)/shard_map/ppermute | solution.py:623
  56.4 0.8 pick.3.near_ref
  57.2 0.0 collective-permute-done.3.refs_3_
  57.2 5.2 %collective-permute-start.25 = (bf16[4,4,32,512]{3,2,1,0:T(8,128)(2,1)S(1)}, bf16[4,4,32,512]{3,2,1,0:T(8,128)(2,1)S(1)}, u32[]{:S(2)}, u32[]{:S(2)}) collective-permute-start(bf16[4,4,32,512]{3,2,1,0:T(8,128)(2,1)S(1)} %pick.3.near_ref), channel_id=1, source_target_pairs={{0,16},{2,18},{4,20},{6,22},{8,24},{10,26},{12,28},{14,30},{16,0},... | collective-permute-start | bytes 1572872 | tf_op jit(solution)/shard_map/ppermute | solution.py:652
  62.5 0.0 collective-permute-done.4.refs_4_
  62.5 0.3 collective-permute-done.7.refs_7_
  62.7 0.6 pack.3.refs_0_
  63.3 1.8 %collective-permute-start.8 = (bf16[8,4,32,512]{3,2,1,0:T(8,128)(2,1)S(1)}, bf16[8,4,32,512]{3,2,1,0:T(8,128)(2,1)S(1)}, u32[]{:S(2)}, u32[]{:S(2)}) collective-permute-start(bf16[8,4,32,512]{3,2,1,0:T(8,128)(2,1)S(1)} %pack.3.refs_0_), channel_id=1, source_target_pairs={{1,0},{0,1},{3,2},{2,3},{5,4},{4,5},{7,6},{6,7},{9,8},{8,9},{11,10... | collective-permute-start | bytes 3145736 | tf_op jit(solution)/shard_map/ppermute | solution.py:628
  65.1 4.5 %collective-permute-start.9 = (bf16[4,2,32,512]{3,2,1,0:T(8,128)(2,1)S(1)}, bf16[4,2,32,512]{3,2,1,0:T(8,128)(2,1)S(1)}, u32[]{:S(2)}, u32[]{:S(2)}) collective-permute-start(bf16[4,2,32,512]{3,2,1,0:T(8,128)(2,1)S(1)} %get-tuple-element.52.near_ref), channel_id=1, source_target_pairs={{0,16},{2,18},{4,20},{6,22},{8,24},{10,26},{12,28},{14,30},{16,0},... | collective-permute-start | bytes 786440 | tf_op jit(solution)/shard_map/ppermute | solution.py:652
  69.6 21.1 %collective-permute-done.25.far_ref = bf16[4,4,32,512]{3,2,1,0:T(8,128)(2,1)S(1)} collective-permute-done((bf16[4,4,32,512]{3,2,1,0:T(8,128)(2,1)S(1)}, bf16[4,4,32,512]{3,2,1,0:T(8,128)(2,1)S(1)}, u32[]{:S(2)}, u32[]{:S(2)}) %collective-permute-start.25) | collective-permute-done | bytes 524320 | tf_op jit(solution)/shard_map/ppermute | solution.py:652
  90.6 0.9 build.5
  91.6 2.0 %collective-permute-start.26 = (bf16[6,32,512]{2,1,0:T(8,128)(2,1)S(1)}, bf16[6,32,512]{2,1,0:T(8,128)(2,1)S(1)}, u32[]{:S(2)}, u32[]{:S(2)}) collective-permute-start(bf16[6,32,512]{2,1,0:T(8,128)(2,1)S(1)} %get-tuple-element.70), channel_id=1, source_target_pairs={{0,2},{2,0},{4,6},{6,4},{8,10},{10,8},{12,14},{14,12},{16,18},{18,... | collective-permute-start | bytes 589832 | tf_op jit(solution)/shard_map/ppermute | solution.py:623
  93.6 1.3 collective-permute-start.28
  94.9 2.1 %collective-permute-done.26.refs_1_ = bf16[6,32,512]{2,1,0:T(8,128)(2,1)S(1)} collective-permute-done((bf16[6,32,512]{2,1,0:T(8,128)(2,1)S(1)}, bf16[6,32,512]{2,1,0:T(8,128)(2,1)S(1)}, u32[]{:S(2)}, u32[]{:S(2)}) %collective-permute-start.26) | collective-permute-done | bytes 196640 | tf_op jit(solution)/shard_map/ppermute | solution.py:623
  97.0 3.6 %collective-permute-done.27.refs_2_ = bf16[6,32,512]{2,1,0:T(8,128)(2,1)S(1)} collective-permute-done((bf16[6,32,512]{2,1,0:T(8,128)(2,1)S(1)}, bf16[6,32,512]{2,1,0:T(8,128)(2,1)S(1)}, u32[]{:S(2)}, u32[]{:S(2)}) %collective-permute-start.27) | collective-permute-done | bytes 196640 | tf_op jit(solution)/shard_map/ppermute | solution.py:623
  100.6 0.8 collective-permute-done.28.refs_3_
  101.4 2.4 %collective-permute-start.32 = (bf16[6,32,512]{2,1,0:T(8,128)(2,1)S(1)}, bf16[6,32,512]{2,1,0:T(8,128)(2,1)S(1)}, u32[]{:S(2)}, u32[]{:S(2)}) collective-permute-start(bf16[6,32,512]{2,1,0:T(8,128)(2,1)S(1)} %get-tuple-element.76), channel_id=1, source_target_pairs={{0,14},{2,12},{4,10},{6,8},{8,6},{10,4},{12,2},{14,0},{16,30},{18,... | collective-permute-start | bytes 589832 | tf_op jit(solution)/shard_map/ppermute | solution.py:623
  103.9 0.9 build.4
  104.7 1.2 collective-permute-start.10
  105.9 0.5 collective-permute-done.30.refs_5_
  106.4 0.7 collective-permute-start.11
  107.1 1.8 %collective-permute-done.31.refs_6_ = bf16[6,32,512]{2,1,0:T(8,128)(2,1)S(1)} collective-permute-done((bf16[6,32,512]{2,1,0:T(8,128)(2,1)S(1)}, bf16[6,32,512]{2,1,0:T(8,128)(2,1)S(1)}, u32[]{:S(2)}, u32[]{:S(2)}) %collective-permute-start.31) | collective-permute-done | bytes 196640 | tf_op jit(solution)/shard_map/ppermute | solution.py:623
  109.0 3.2 %collective-permute-start.12 = (bf16[3,32,512]{2,1,0:T(8,128)(2,1)S(1)}, bf16[3,32,512]{2,1,0:T(8,128)(2,1)S(1)}, u32[]{:S(2)}, u32[]{:S(2)}) collective-permute-start(bf16[3,32,512]{2,1,0:T(8,128)(2,1)S(1)} %get-tuple-element.56), channel_id=1, source_target_pairs={{0,6},{2,4},{4,2},{6,0},{8,14},{10,12},{12,10},{14,8},{16,22},{18,... | collective-permute-start | bytes 294920 | tf_op jit(solution)/shard_map/ppermute | solution.py:623
  112.1 1.2 collective-permute-done.32.refs_7_
  113.3 1.1 collective-permute-start.13
  114.4 2.1 %collective-permute-start.14 = (bf16[3,32,512]{2,1,0:T(8,128)(2,1)S(1)}, bf16[3,32,512]{2,1,0:T(8,128)(2,1)S(1)}, u32[]{:S(2)}, u32[]{:S(2)}) collective-permute-start(bf16[3,32,512]{2,1,0:T(8,128)(2,1)S(1)} %get-tuple-element.58), channel_id=1, source_target_pairs={{0,10},{2,8},{4,14},{6,12},{8,2},{10,0},{12,6},{14,4},{16,26},{18,... | collective-permute-start | bytes 294920 | tf_op jit(solution)/shard_map/ppermute | solution.py:623
  116.5 1.6 %collective-permute-start.15 = (bf16[3,32,512]{2,1,0:T(8,128)(2,1)S(1)}, bf16[3,32,512]{2,1,0:T(8,128)(2,1)S(1)}, u32[]{:S(2)}, u32[]{:S(2)}) collective-permute-start(bf16[3,32,512]{2,1,0:T(8,128)(2,1)S(1)} %get-tuple-element.59), channel_id=1, source_target_pairs={{0,12},{2,14},{4,8},{6,10},{8,4},{10,6},{12,0},{14,2},{16,28},{18,... | collective-permute-start | bytes 294920 | tf_op jit(solution)/shard_map/ppermute | solution.py:623
  118.2 0.9 collective-permute-start.16
  119.1 0.6 pack.5.refs_4_
  119.7 6.4 %collective-permute-start.33 = (bf16[8,6,32,512]{3,2,1,0:T(8,128)(2,1)S(1)}, bf16[8,6,32,512]{3,2,1,0:T(8,128)(2,1)S(1)}, u32[]{:S(2)}, u32[]{:S(2)}) collective-permute-start(bf16[8,6,32,512]{3,2,1,0:T(8,128)(2,1)S(1)} %pack.5.refs_4_), channel_id=1, source_target_pairs={{1,0},{0,1},{3,2},{2,3},{5,4},{4,5},{7,6},{6,7},{9,8},{8,9},{11,10... | collective-permute-start | bytes 4718600 | tf_op jit(solution)/shard_map/ppermute | solution.py:628
  126.1 0.6 pack.4.refs_2_
  126.8 4.7 %collective-permute-start.17 = (bf16[8,3,32,512]{3,2,1,0:T(8,128)(2,1)S(1)}, bf16[8,3,32,512]{3,2,1,0:T(8,128)(2,1)S(1)}, u32[]{:S(2)}, u32[]{:S(2)}) collective-permute-start(bf16[8,3,32,512]{3,2,1,0:T(8,128)(2,1)S(1)} %pack.4.refs_2_), channel_id=1, source_target_pairs={{1,0},{0,1},{3,2},{2,3},{5,4},{4,5},{7,6},{6,7},{9,8},{8,9},{11,10... | collective-permute-start | bytes 2359304 | tf_op jit(solution)/shard_map/ppermute | solution.py:628
  131.5 8.4 %inverse.1 = (bf16[512,512]{1,0:T(8,128)(2,1)S(1)}, f32[36,256,512]{2,1,0:T(8,128)S(1)}) custom-call(s32[40]{0:T(128)S(1)} %copy-done.1, bf16[8,4,32,512]{3,2,1,0:T(8,128)(2,1)S(1)} %pack.3.refs_0_, bf16[8,4,32,512]{3,2,1,0:T(8,128)(2,1)S(1)} %collective-permute-done.8.refs_1_, f32[36,256,512]{2,1,0:T(8,128)} %bitcast.4), custom_call_target="tpu_custom_call" | custom-call | flops 16106127360 | bytes 1048576 | tf_op jit(solution)/shard_map/inverse/pallas_call | solution.py:467
  139.9 10.6 %update.1 = f32[36,256,512]{2,1,0:T(8,128)} custom-call(s32[40]{0:T(128)S(1)} %copy-done.1, f32[36,256,512]{2,1,0:T(8,128)S(1)} %get-tuple-element.50.tiles, bf16[512,512]{1,0:T(8,128)(2,1)S(1)} %get-tuple-element.51.inv, bf16[8,4,32,512]{3,2,1,0:T(8,128)(2,1)S(1)} %pack.3.refs_0_, bf16[8,4,32,512]{3,2,1,0:T(8,128)(2,1)S(1)} %collective-permute-done.8.refs_1_, ...), custom_call_target="tpu_custom_call" | custom-call | tf_op jit(solution)/shard_map/update/pallas_call | solution.py:588
  (27 shorter events, 0.1 us)
Async XLA Ops:
  0.0 26.6 %copy-start.3 = (s32[16]{0:T(128)S(1)}, s32[16]{0:T(128)}, u32[]{:S(2)}) copy-start(s32[16]{0:T(128)} %owner.5) | copy-start | bytes 196
  0.0 0.7 copy-start.2
  3.8 19.1 %all-to-all-start = ((bf16[8,4,32,512]{3,2,1,0:T(8,128)(2,1)}), bf16[8,4,32,512]{3,2,1,0:T(8,128)(2,1)S(1)}, u32[]{:S(2)}, u32[]{:S(2)}) async-start(bf16[8,4,32,512]{3,2,1,0:T(8,128)(2,1)} %extract.2), calls=%async_computation | async-start | bytes 2097152 | tf_op jit(solution)/shard_map/all_to_all | solution.py:639
  23.0 0.7 copy-start
  23.6 80.2 %copy-start.1 = (s32[40]{0:T(128)S(1)}, s32[40]{0:T(128)}, u32[]{:S(2)}) copy-start(s32[40]{0:T(128)} %table.1.t) | copy-start | bytes 484
  24.2 12.8 %collective-permute-start = (bf16[4,2,32,512]{3,2,1,0:T(8,128)(2,1)S(1)}, bf16[4,2,32,512]{3,2,1,0:T(8,128)(2,1)S(1)}, u32[]{:S(2)}, u32[]{:S(2)}) collective-permute-start(bf16[4,2,32,512]{3,2,1,0:T(8,128)(2,1)S(1)} %get-tuple-element.41.near_ref), channel_id=1, source_target_pairs={{0,16},{2,18},{4,20},{6,22},{8,24},{10,26},{12,28},{14,30},{16,0},... | collective-permute-start | bytes 786440 | tf_op jit(solution)/shard_map/ppermute | solution.py:652
  28.8 12.8 %collective-permute-start.18 = (bf16[4,32,512]{2,1,0:T(8,128)(2,1)S(1)}, bf16[4,32,512]{2,1,0:T(8,128)(2,1)S(1)}, u32[]{:S(2)}, u32[]{:S(2)}) collective-permute-start(bf16[4,32,512]{2,1,0:T(8,128)(2,1)S(1)} %get-tuple-element.62), channel_id=1, source_target_pairs={{0,2},{2,0},{4,6},{6,4},{8,10},{10,8},{12,14},{14,12},{16,18},{18,... | collective-permute-start | bytes 393224 | tf_op jit(solution)/shard_map/ppermute | solution.py:623
  30.2 11.4 %collective-permute-start.19 = (bf16[4,32,512]{2,1,0:T(8,128)(2,1)S(1)}, bf16[4,32,512]{2,1,0:T(8,128)(2,1)S(1)}, u32[]{:S(2)}, u32[]{:S(2)}) collective-permute-start(bf16[4,32,512]{2,1,0:T(8,128)(2,1)S(1)} %get-tuple-element.63), channel_id=1, source_target_pairs={{0,4},{2,6},{4,0},{6,2},{8,12},{10,14},{12,8},{14,10},{16,20},{18,... | collective-permute-start | bytes 393224 | tf_op jit(solution)/shard_map/ppermute | solution.py:623
  30.3 13.5 %collective-permute-start.20 = (bf16[4,32,512]{2,1,0:T(8,128)(2,1)S(1)}, bf16[4,32,512]{2,1,0:T(8,128)(2,1)S(1)}, u32[]{:S(2)}, u32[]{:S(2)}) collective-permute-start(bf16[4,32,512]{2,1,0:T(8,128)(2,1)S(1)} %get-tuple-element.64), channel_id=1, source_target_pairs={{0,6},{2,4},{4,2},{6,0},{8,14},{10,12},{12,10},{14,8},{16,22},{18,... | collective-permute-start | bytes 393224 | tf_op jit(solution)/shard_map/ppermute | solution.py:623
  31.5 13.7 %collective-permute-start.21 = (bf16[4,32,512]{2,1,0:T(8,128)(2,1)S(1)}, bf16[4,32,512]{2,1,0:T(8,128)(2,1)S(1)}, u32[]{:S(2)}, u32[]{:S(2)}) collective-permute-start(bf16[4,32,512]{2,1,0:T(8,128)(2,1)S(1)} %get-tuple-element.65), channel_id=1, source_target_pairs={{0,8},{2,10},{4,12},{6,14},{8,0},{10,2},{12,4},{14,6},{16,24},{18,... | collective-permute-start | bytes 393224 | tf_op jit(solution)/shard_map/ppermute | solution.py:623
  37.0 8.2 %collective-permute-start.22 = (bf16[4,32,512]{2,1,0:T(8,128)(2,1)S(1)}, bf16[4,32,512]{2,1,0:T(8,128)(2,1)S(1)}, u32[]{:S(2)}, u32[]{:S(2)}) collective-permute-start(bf16[4,32,512]{2,1,0:T(8,128)(2,1)S(1)} %get-tuple-element.66), channel_id=1, source_target_pairs={{0,10},{2,8},{4,14},{6,12},{8,2},{10,0},{12,6},{14,4},{16,26},{18,... | collective-permute-start | bytes 393224 | tf_op jit(solution)/shard_map/ppermute | solution.py:623
  41.5 5.3 %collective-permute-start.23 = (bf16[4,32,512]{2,1,0:T(8,128)(2,1)S(1)}, bf16[4,32,512]{2,1,0:T(8,128)(2,1)S(1)}, u32[]{:S(2)}, u32[]{:S(2)}) collective-permute-start(bf16[4,32,512]{2,1,0:T(8,128)(2,1)S(1)} %get-tuple-element.67), channel_id=1, source_target_pairs={{0,12},{2,14},{4,8},{6,10},{8,4},{10,6},{12,0},{14,2},{16,28},{18,... | collective-permute-start | bytes 393224 | tf_op jit(solution)/shard_map/ppermute | solution.py:623
  41.6 7.9 %collective-permute-start.24 = (bf16[4,32,512]{2,1,0:T(8,128)(2,1)S(1)}, bf16[4,32,512]{2,1,0:T(8,128)(2,1)S(1)}, u32[]{:S(2)}, u32[]{:S(2)}) collective-permute-start(bf16[4,32,512]{2,1,0:T(8,128)(2,1)S(1)} %get-tuple-element.68), channel_id=1, source_target_pairs={{0,14},{2,12},{4,10},{6,8},{8,6},{10,4},{12,2},{14,0},{16,30},{18,... | collective-permute-start | bytes 393224 | tf_op jit(solution)/shard_map/ppermute | solution.py:623
  43.8 6.7 %collective-permute-start.1 = (bf16[4,32,512]{2,1,0:T(8,128)(2,1)S(1)}, bf16[4,32,512]{2,1,0:T(8,128)(2,1)S(1)}, u32[]{:S(2)}, u32[]{:S(2)}) collective-permute-start(bf16[4,32,512]{2,1,0:T(8,128)(2,1)S(1)} %get-tuple-element.43), channel_id=1, source_target_pairs={{0,2},{2,0},{4,6},{6,4},{8,10},{10,8},{12,14},{14,12},{16,18},{18,... | collective-permute-start | bytes 393224 | tf_op jit(solution)/shard_map/ppermute | solution.py:623
  45.2 11.2 %collective-permute-start.2 = (bf16[4,32,512]{2,1,0:T(8,128)(2,1)S(1)}, bf16[4,32,512]{2,1,0:T(8,128)(2,1)S(1)}, u32[]{:S(2)}, u32[]{:S(2)}) collective-permute-start(bf16[4,32,512]{2,1,0:T(8,128)(2,1)S(1)} %get-tuple-element.44), channel_id=1, source_target_pairs={{0,4},{2,6},{4,0},{6,2},{8,12},{10,14},{12,8},{14,10},{16,20},{18,... | collective-permute-start | bytes 393224 | tf_op jit(solution)/shard_map/ppermute | solution.py:623
  45.3 11.9 %collective-permute-start.3 = (bf16[4,32,512]{2,1,0:T(8,128)(2,1)S(1)}, bf16[4,32,512]{2,1,0:T(8,128)(2,1)S(1)}, u32[]{:S(2)}, u32[]{:S(2)}) collective-permute-start(bf16[4,32,512]{2,1,0:T(8,128)(2,1)S(1)} %get-tuple-element.45), channel_id=1, source_target_pairs={{0,6},{2,4},{4,2},{6,0},{8,14},{10,12},{12,10},{14,8},{16,22},{18,... | collective-permute-start | bytes 393224 | tf_op jit(solution)/shard_map/ppermute | solution.py:623
  46.8 15.7 %collective-permute-start.4 = (bf16[4,32,512]{2,1,0:T(8,128)(2,1)S(1)}, bf16[4,32,512]{2,1,0:T(8,128)(2,1)S(1)}, u32[]{:S(2)}, u32[]{:S(2)}) collective-permute-start(bf16[4,32,512]{2,1,0:T(8,128)(2,1)S(1)} %get-tuple-element.46), channel_id=1, source_target_pairs={{0,8},{2,10},{4,12},{6,14},{8,0},{10,2},{12,4},{14,6},{16,24},{18,... | collective-permute-start | bytes 393224 | tf_op jit(solution)/shard_map/ppermute | solution.py:623
  49.5 12.9 %collective-permute-start.5 = (bf16[4,32,512]{2,1,0:T(8,128)(2,1)S(1)}, bf16[4,32,512]{2,1,0:T(8,128)(2,1)S(1)}, u32[]{:S(2)}, u32[]{:S(2)}) collective-permute-start(bf16[4,32,512]{2,1,0:T(8,128)(2,1)S(1)} %get-tuple-element.47), channel_id=1, source_target_pairs={{0,10},{2,8},{4,14},{6,12},{8,2},{10,0},{12,6},{14,4},{16,26},{18,... | collective-permute-start | bytes 393224 | tf_op jit(solution)/shard_map/ppermute | solution.py:623
  50.5 11.9 %collective-permute-start.6 = (bf16[4,32,512]{2,1,0:T(8,128)(2,1)S(1)}, bf16[4,32,512]{2,1,0:T(8,128)(2,1)S(1)}, u32[]{:S(2)}, u32[]{:S(2)}) collective-permute-start(bf16[4,32,512]{2,1,0:T(8,128)(2,1)S(1)} %get-tuple-element.48), channel_id=1, source_target_pairs={{0,12},{2,14},{4,8},{6,10},{8,4},{10,6},{12,0},{14,2},{16,28},{18,... | collective-permute-start | bytes 393224 | tf_op jit(solution)/shard_map/ppermute | solution.py:623
  56.4 6.4 %collective-permute-start.7 = (bf16[4,32,512]{2,1,0:T(8,128)(2,1)S(1)}, bf16[4,32,512]{2,1,0:T(8,128)(2,1)S(1)}, u32[]{:S(2)}, u32[]{:S(2)}) collective-permute-start(bf16[4,32,512]{2,1,0:T(8,128)(2,1)S(1)} %get-tuple-element.49), channel_id=1, source_target_pairs={{0,14},{2,12},{4,10},{6,8},{8,6},{10,4},{12,2},{14,0},{16,30},{18,... | collective-permute-start | bytes 393224 | tf_op jit(solution)/shard_map/ppermute | solution.py:623
  57.2 33.4 %collective-permute-start.25 = (bf16[4,4,32,512]{3,2,1,0:T(8,128)(2,1)S(1)}, bf16[4,4,32,512]{3,2,1,0:T(8,128)(2,1)S(1)}, u32[]{:S(2)}, u32[]{:S(2)}) collective-permute-start(bf16[4,4,32,512]{3,2,1,0:T(8,128)(2,1)S(1)} %pick.3.near_ref), channel_id=1, source_target_pairs={{0,16},{2,18},{4,20},{6,22},{8,24},{10,26},{12,28},{14,30},{16,0},... | collective-permute-start | bytes 1572872 | tf_op jit(solution)/shard_map/ppermute | solution.py:652
  63.3 68.2 %collective-permute-start.8 = (bf16[8,4,32,512]{3,2,1,0:T(8,128)(2,1)S(1)}, bf16[8,4,32,512]{3,2,1,0:T(8,128)(2,1)S(1)}, u32[]{:S(2)}, u32[]{:S(2)}) collective-permute-start(bf16[8,4,32,512]{3,2,1,0:T(8,128)(2,1)S(1)} %pack.3.refs_0_), channel_id=1, source_target_pairs={{1,0},{0,1},{3,2},{2,3},{5,4},{4,5},{7,6},{6,7},{9,8},{8,9},{11,10... | collective-permute-start | bytes 3145736 | tf_op jit(solution)/shard_map/ppermute | solution.py:628
  65.1 36.3 %collective-permute-start.9 = (bf16[4,2,32,512]{3,2,1,0:T(8,128)(2,1)S(1)}, bf16[4,2,32,512]{3,2,1,0:T(8,128)(2,1)S(1)}, u32[]{:S(2)}, u32[]{:S(2)}) collective-permute-start(bf16[4,2,32,512]{3,2,1,0:T(8,128)(2,1)S(1)} %get-tuple-element.52.near_ref), channel_id=1, source_target_pairs={{0,16},{2,18},{4,20},{6,22},{8,24},{10,26},{12,28},{14,30},{16,0},... | collective-permute-start | bytes 786440 | tf_op jit(solution)/shard_map/ppermute | solution.py:652
  91.6 5.4 %collective-permute-start.26 = (bf16[6,32,512]{2,1,0:T(8,128)(2,1)S(1)}, bf16[6,32,512]{2,1,0:T(8,128)(2,1)S(1)}, u32[]{:S(2)}, u32[]{:S(2)}) collective-permute-start(bf16[6,32,512]{2,1,0:T(8,128)(2,1)S(1)} %get-tuple-element.70), channel_id=1, source_target_pairs={{0,2},{2,0},{4,6},{6,4},{8,10},{10,8},{12,14},{14,12},{16,18},{18,... | collective-permute-start | bytes 589832 | tf_op jit(solution)/shard_map/ppermute | solution.py:623
  93.6 7.0 %collective-permute-start.27 = (bf16[6,32,512]{2,1,0:T(8,128)(2,1)S(1)}, bf16[6,32,512]{2,1,0:T(8,128)(2,1)S(1)}, u32[]{:S(2)}, u32[]{:S(2)}) collective-permute-start(bf16[6,32,512]{2,1,0:T(8,128)(2,1)S(1)} %get-tuple-element.71), channel_id=1, source_target_pairs={{0,4},{2,6},{4,0},{6,2},{8,12},{10,14},{12,8},{14,10},{16,20},{18,... | collective-permute-start | bytes 589832 | tf_op jit(solution)/shard_map/ppermute | solution.py:623
  93.6 7.8 %collective-permute-start.28 = (bf16[6,32,512]{2,1,0:T(8,128)(2,1)S(1)}, bf16[6,32,512]{2,1,0:T(8,128)(2,1)S(1)}, u32[]{:S(2)}, u32[]{:S(2)}) collective-permute-start(bf16[6,32,512]{2,1,0:T(8,128)(2,1)S(1)} %get-tuple-element.72), channel_id=1, source_target_pairs={{0,6},{2,4},{4,2},{6,0},{8,14},{10,12},{12,10},{14,8},{16,22},{18,... | collective-permute-start | bytes 589832 | tf_op jit(solution)/shard_map/ppermute | solution.py:623
  97.0 7.8 %collective-permute-start.29 = (bf16[6,32,512]{2,1,0:T(8,128)(2,1)S(1)}, bf16[6,32,512]{2,1,0:T(8,128)(2,1)S(1)}, u32[]{:S(2)}, u32[]{:S(2)}) collective-permute-start(bf16[6,32,512]{2,1,0:T(8,128)(2,1)S(1)} %get-tuple-element.73), channel_id=1, source_target_pairs={{0,8},{2,10},{4,12},{6,14},{8,0},{10,2},{12,4},{14,6},{16,24},{18,... | collective-permute-start | bytes 589832 | tf_op jit(solution)/shard_map/ppermute | solution.py:623
  100.6 5.8 %collective-permute-start.30 = (bf16[6,32,512]{2,1,0:T(8,128)(2,1)S(1)}, bf16[6,32,512]{2,1,0:T(8,128)(2,1)S(1)}, u32[]{:S(2)}, u32[]{:S(2)}) collective-permute-start(bf16[6,32,512]{2,1,0:T(8,128)(2,1)S(1)} %get-tuple-element.74), channel_id=1, source_target_pairs={{0,10},{2,8},{4,14},{6,12},{8,2},{10,0},{12,6},{14,4},{16,26},{18,... | collective-permute-start | bytes 589832 | tf_op jit(solution)/shard_map/ppermute | solution.py:623
  101.4 7.5 %collective-permute-start.31 = (bf16[6,32,512]{2,1,0:T(8,128)(2,1)S(1)}, bf16[6,32,512]{2,1,0:T(8,128)(2,1)S(1)}, u32[]{:S(2)}, u32[]{:S(2)}) collective-permute-start(bf16[6,32,512]{2,1,0:T(8,128)(2,1)S(1)} %get-tuple-element.75), channel_id=1, source_target_pairs={{0,12},{2,14},{4,8},{6,10},{8,4},{10,6},{12,0},{14,2},{16,28},{18,... | collective-permute-start | bytes 589832 | tf_op jit(solution)/shard_map/ppermute | solution.py:623
  101.4 11.9 %collective-permute-start.32 = (bf16[6,32,512]{2,1,0:T(8,128)(2,1)S(1)}, bf16[6,32,512]{2,1,0:T(8,128)(2,1)S(1)}, u32[]{:S(2)}, u32[]{:S(2)}) collective-permute-start(bf16[6,32,512]{2,1,0:T(8,128)(2,1)S(1)} %get-tuple-element.76), channel_id=1, source_target_pairs={{0,14},{2,12},{4,10},{6,8},{8,6},{10,4},{12,2},{14,0},{16,30},{18,... | collective-permute-start | bytes 589832 | tf_op jit(solution)/shard_map/ppermute | solution.py:623
  104.7 9.6 %collective-permute-start.10 = (bf16[3,32,512]{2,1,0:T(8,128)(2,1)S(1)}, bf16[3,32,512]{2,1,0:T(8,128)(2,1)S(1)}, u32[]{:S(2)}, u32[]{:S(2)}) collective-permute-start(bf16[3,32,512]{2,1,0:T(8,128)(2,1)S(1)} %get-tuple-element.54), channel_id=1, source_target_pairs={{0,2},{2,0},{4,6},{6,4},{8,10},{10,8},{12,14},{14,12},{16,18},{18,... | collective-permute-start | bytes 294920 | tf_op jit(solution)/shard_map/ppermute | solution.py:623
  106.4 10.1 %collective-permute-start.11 = (bf16[3,32,512]{2,1,0:T(8,128)(2,1)S(1)}, bf16[3,32,512]{2,1,0:T(8,128)(2,1)S(1)}, u32[]{:S(2)}, u32[]{:S(2)}) collective-permute-start(bf16[3,32,512]{2,1,0:T(8,128)(2,1)S(1)} %get-tuple-element.55), channel_id=1, source_target_pairs={{0,4},{2,6},{4,0},{6,2},{8,12},{10,14},{12,8},{14,10},{16,20},{18,... | collective-permute-start | bytes 294920 | tf_op jit(solution)/shard_map/ppermute | solution.py:623
  109.0 9.2 %collective-permute-start.12 = (bf16[3,32,512]{2,1,0:T(8,128)(2,1)S(1)}, bf16[3,32,512]{2,1,0:T(8,128)(2,1)S(1)}, u32[]{:S(2)}, u32[]{:S(2)}) collective-permute-start(bf16[3,32,512]{2,1,0:T(8,128)(2,1)S(1)} %get-tuple-element.56), channel_id=1, source_target_pairs={{0,6},{2,4},{4,2},{6,0},{8,14},{10,12},{12,10},{14,8},{16,22},{18,... | collective-permute-start | bytes 294920 | tf_op jit(solution)/shard_map/ppermute | solution.py:623
  113.3 6.4 %collective-permute-start.13 = (bf16[3,32,512]{2,1,0:T(8,128)(2,1)S(1)}, bf16[3,32,512]{2,1,0:T(8,128)(2,1)S(1)}, u32[]{:S(2)}, u32[]{:S(2)}) collective-permute-start(bf16[3,32,512]{2,1,0:T(8,128)(2,1)S(1)} %get-tuple-element.57), channel_id=1, source_target_pairs={{0,8},{2,10},{4,12},{6,14},{8,0},{10,2},{12,4},{14,6},{16,24},{18,... | collective-permute-start | bytes 294920 | tf_op jit(solution)/shard_map/ppermute | solution.py:623
  114.4 11.7 %collective-permute-start.14 = (bf16[3,32,512]{2,1,0:T(8,128)(2,1)S(1)}, bf16[3,32,512]{2,1,0:T(8,128)(2,1)S(1)}, u32[]{:S(2)}, u32[]{:S(2)}) collective-permute-start(bf16[3,32,512]{2,1,0:T(8,128)(2,1)S(1)} %get-tuple-element.58), channel_id=1, source_target_pairs={{0,10},{2,8},{4,14},{6,12},{8,2},{10,0},{12,6},{14,4},{16,26},{18,... | collective-permute-start | bytes 294920 | tf_op jit(solution)/shard_map/ppermute | solution.py:623
  116.5 9.6 %collective-permute-start.15 = (bf16[3,32,512]{2,1,0:T(8,128)(2,1)S(1)}, bf16[3,32,512]{2,1,0:T(8,128)(2,1)S(1)}, u32[]{:S(2)}, u32[]{:S(2)}) collective-permute-start(bf16[3,32,512]{2,1,0:T(8,128)(2,1)S(1)} %get-tuple-element.59), channel_id=1, source_target_pairs={{0,12},{2,14},{4,8},{6,10},{8,4},{10,6},{12,0},{14,2},{16,28},{18,... | collective-permute-start | bytes 294920 | tf_op jit(solution)/shard_map/ppermute | solution.py:623
  118.2 8.0 %collective-permute-start.16 = (bf16[3,32,512]{2,1,0:T(8,128)(2,1)S(1)}, bf16[3,32,512]{2,1,0:T(8,128)(2,1)S(1)}, u32[]{:S(2)}, u32[]{:S(2)}) collective-permute-start(bf16[3,32,512]{2,1,0:T(8,128)(2,1)S(1)} %get-tuple-element.60), channel_id=1, source_target_pairs={{0,14},{2,12},{4,10},{6,8},{8,6},{10,4},{12,2},{14,0},{16,30},{18,... | collective-permute-start | bytes 294920 | tf_op jit(solution)/shard_map/ppermute | solution.py:623
  119.7 20.1 %collective-permute-start.33 = (bf16[8,6,32,512]{3,2,1,0:T(8,128)(2,1)S(1)}, bf16[8,6,32,512]{3,2,1,0:T(8,128)(2,1)S(1)}, u32[]{:S(2)}, u32[]{:S(2)}) collective-permute-start(bf16[8,6,32,512]{3,2,1,0:T(8,128)(2,1)S(1)} %pack.5.refs_4_), channel_id=1, source_target_pairs={{1,0},{0,1},{3,2},{2,3},{5,4},{4,5},{7,6},{6,7},{9,8},{8,9},{11,10... | collective-permute-start | bytes 4718600 | tf_op jit(solution)/shard_map/ppermute | solution.py:628
  126.8 13.1 %collective-permute-start.17 = (bf16[8,3,32,512]{3,2,1,0:T(8,128)(2,1)S(1)}, bf16[8,3,32,512]{3,2,1,0:T(8,128)(2,1)S(1)}, u32[]{:S(2)}, u32[]{:S(2)}) collective-permute-start(bf16[8,3,32,512]{3,2,1,0:T(8,128)(2,1)S(1)} %pack.4.refs_2_), channel_id=1, source_target_pairs={{1,0},{0,1},{3,2},{2,3},{5,4},{4,5},{7,6},{6,7},{9,8},{8,9},{11,10... | collective-permute-start | bytes 2359304 | tf_op jit(solution)/shard_map/ppermute | solution.py:628
